TPU v7x, 256 devices: a 4x2x16 block of a 4x16x16 slice. The times are simulated.
256 devices in a mesh: groups: 2 (over y), seq: 16 (over z), tensor: 4 (over x), cfg: 2 (over core).
Axes of the slice: x: 4, y: 2, z: 16, core: 2. Of those that a mesh axis runs over, the one named last changes fastest.
The devices are a block of a 4x16x16 slice.
Arguments:
- latent: bfloat16 [8192, 3072], P(('groups', 'seq')), parts along dimension 0, may hold values from -6 to 6
- positions: int32 [3, 8192], P(None, ('groups', 'seq')), parts along dimension 1, may hold values from 0 to 79, as said below
- text_kv: bfloat16 [2, 2, 512, 3072], P('cfg', None, ('groups', 'seq'), 'tensor'), parts along dimension 2, may hold values from -6 to 6
- text_len: int32 [4], P(('groups', 'cfg')), parts along dimension 0, may hold values from 1 to 256
- modulation: float32 [3, 4, 3072], P(None, 'groups'), parts along dimension 1, may hold values from -3 to 3
- w_qkv: bfloat16 [3, 3072, 3072], P(None, 'cfg', 'tensor'), may hold values from -0.109375 to 0.109375
- norm_gains: float32 [2, 128], replicated, may hold values from 0.5 to 2.5
- w_out: bfloat16 [3072, 3072], P('tensor', 'cfg'), may hold values from -0.109375 to 0.109375
- guidance: float32 [2], P('groups'), parts along dimension 0, may hold values from 3 to 8
Outputs:
- guided: bfloat16 [8192, 3072], P(('groups', 'seq', 'tensor'), 'cfg'), parts along dimension 0
There are 2 independent parts, one for each index of `groups`. A program takes and returns all parts, laid end to end along the dimension named above; an argument that names none is the same for every part. Nothing has to cross between parts.
Inputs may be any that keep to these rules, and one draw needn't show every extreme that they name: `positions`: frame indices are below 33, height indices below 45, width indices below 80. `text_len`: text rows at or beyond the count are ignored.
All inputs are finite; a program needn't handle non-finite values.
Results may differ from a plain program's by a relative error of at most 0.018.
Values may be sent and summed in bfloat16 or wider, within the bound.
No kernel may reach another device: no remote copies, remote signals or barrier semaphores. Data moves between devices by JAX's collectives and lax.ppermute only.
A program may use at most 128 MiB of HBM per device.

v0:
```python
import functools
import math

import jax
import jax.numpy as jnp
import numpy as np
from jax import lax
from jax.experimental import pallas as pl
from jax.experimental.pallas import tpu as pltpu
from jax.sharding import PartitionSpec as P


HEAD_DIM = 128
EPS = 1e-06


def shifted(value, axis, by):
    n = lax.axis_size(axis)
    return lax.ppermute(value, axis, [(i, (i + by) % n) for i in range(n)])


def dot(a, b):
    return jnp.dot(a, b, preferred_element_type=jnp.float32)


POSITIONS = (33, 45, 80)


def rotary_constants():
    blocks = (HEAD_DIM // 8, 7 * HEAD_DIM // 16, 7 * HEAD_DIM // 16)
    angle = np.zeros((256, HEAD_DIM), np.float32)
    used = np.zeros((256, HEAD_DIM), bool)
    signs = np.zeros((4, HEAD_DIM), np.float32)
    offset = base = 0
    for axis_id, width in enumerate(blocks):
        half = width // 2
        kind = 0 if axis_id == 0 else 2
        freq = np.float32(256.0) ** (-np.arange(half, dtype=np.float32) / np.float32(half))
        count = POSITIONS[axis_id]
        turn = np.arange(count, dtype=np.float32)[:, None] * np.tile(freq, 2)[None, :]
        angle[base : base + count, offset : offset + width] = turn
        used[base : base + count, offset : offset + width] = True
        signs[kind, offset : offset + half] = -1.0
        signs[kind + 1, offset + half : offset + width] = 1.0
        offset += width
        base += count
    parts = []
    for values in (np.cos(angle.astype(np.float64)), np.sin(angle.astype(np.float64))):
        values = np.where(used, values, 0.0).astype(np.float32)
        high = values.astype(jnp.bfloat16)
        parts += [high, (values - high.astype(np.float32)).astype(jnp.bfloat16)]
    return np.concatenate(parts, axis=1), signs


def table_rows(pos, turn_ref, sign_ref, out_ref):
    d = HEAD_DIM
    pos = pos.T
    lane = lax.broadcasted_iota(jnp.int32, (pos.shape[0], turn_ref.shape[0]), 1).astype(jnp.float32)
    hot = lane == pos[:, 0:1]
    hot = hot | (lane == pos[:, 1:2] + POSITIONS[0])
    hot = hot | (lane == pos[:, 2:3] + (POSITIONS[0] + POSITIONS[1]))
    y = dot(jnp.where(hot, 1.0, 0.0).astype(jnp.bfloat16), turn_ref[...])
    sine = y[:, 2 * d : 3 * d] + y[:, 3 * d :]
    out_ref[:, 0:d] = y[:, 0:d] + y[:, d : 2 * d]
    for i in range(4):
        out_ref[:, (i + 1) * d : (i + 2) * d] = sine * sign_ref[i : i + 1, :]


def padded(pos):
    return jnp.concatenate([pos, jnp.zeros((8 - pos.shape[0], pos.shape[1]), pos.dtype)], axis=0)


def tables_kernel(pos_ref, turn_ref, sign_ref, out_ref):
    table_rows(padded(pos_ref[...].astype(jnp.float32)), turn_ref, sign_ref, out_ref)


def rotary_tables(positions):
    turn, signs = rotary_constants()
    count = positions.shape[1]
    return pl.pallas_call(
        tables_kernel,
        grid=(count // 128,),
        in_specs=[
            pl.BlockSpec((3, 128), lambda i: (0, i)),
            pl.BlockSpec(turn.shape, lambda i: (0, 0)),
            pl.BlockSpec(signs.shape, lambda i: (0, 0)),
        ],
        out_specs=pl.BlockSpec((128, 5 * HEAD_DIM), lambda i: (i, 0)),
        out_shape=jax.ShapeDtypeStruct((count, 5 * HEAD_DIM), jnp.float32),
        cost_estimate=pl.CostEstimate(flops=2000000 * count, bytes_accessed=2560 * count, transcendentals=0),
        compiler_params=pltpu.CompilerParams(vmem_limit_bytes=8 << 20),
        name="tables",
    )(positions, jnp.asarray(turn), jnp.asarray(signs))


def head_norm(heads_in, gain):
    return heads_in * lax.rsqrt(jnp.mean(heads_in * heads_in, axis=-1, keepdims=True) + EPS) * gain


def rotate(x, tables):
    d = HEAD_DIM
    small, large = d // 16, 7 * d // 32
    parts = [tables[:, i * d : (i + 1) * d] for i in range(5)]
    return (
        x * parts[0]
        + pltpu.roll(x, d - small, 1) * parts[1]
        + pltpu.roll(x, small, 1) * parts[2]
        + pltpu.roll(x, d - large, 1) * parts[3]
        + pltpu.roll(x, large, 1) * parts[4]
    )


def norm_kernel(c_ref, x_ref, mod_ref, own_ref, other_ref):
    x = x_ref[...].astype(jnp.float32)
    center = x - jnp.mean(x, axis=-1, keepdims=True)
    normed = center * lax.rsqrt(jnp.mean(center * center, axis=-1, keepdims=True) + EPS)
    half = normed.shape[1] // 2
    mine = jnp.where(c_ref[0] == 0, normed[:, :half], normed[:, half:])
    for branch, out_ref in ((c_ref[0], own_ref), (1 - c_ref[0], other_ref)):
        at = pl.ds(branch, 1)
        out_ref[...] = (mine * (1.0 + mod_ref[1, at, :]) + mod_ref[0, at, :]).astype(jnp.bfloat16)


def modulate(branch, latent, mod):
    rows, width = latent.shape
    half = width // 2
    step = 64
    shape = jax.ShapeDtypeStruct((rows, half), jnp.bfloat16)
    spec = pl.BlockSpec((step, half), lambda i, c: (i, 0))
    return pl.pallas_call(
        norm_kernel,
        grid_spec=pltpu.PrefetchScalarGridSpec(
            num_scalar_prefetch=1,
            grid=(rows // step,),
            in_specs=[
                pl.BlockSpec((step, width), lambda i, c: (i, 0)),
                pl.BlockSpec((*mod.shape[:2], half), lambda i, c: (0, 0, c[0])),
            ],
            out_specs=(spec, spec),
        ),
        out_shape=(shape, shape),
        cost_estimate=pl.CostEstimate(flops=3000000000, bytes_accessed=4 * rows * width, transcendentals=0),
        compiler_params=pltpu.CompilerParams(vmem_limit_bytes=8 << 20),
        name="norm",
    )(branch, latent, mod)


def terms_kernel(own_ref, other_ref, w_ref, *refs):
    mine_ref, theirs_ref = refs[-2:]
    w = w_ref[0]
    theirs_ref[...] = dot(other_ref[...], w).astype(jnp.bfloat16)
    mine_ref[...] = dot(own_ref[...], w)


def terms(own, other, w_qkv, first, count, after=()):
    rows, half = own.shape
    width = w_qkv.shape[2]
    tile = 2 * HEAD_DIM
    tiles = width // tile
    whole = pl.BlockSpec((rows, half), lambda n: (0, 0))
    part = pl.BlockSpec((rows, tile), lambda n: (0, n))
    return pl.pallas_call(
        terms_kernel,
        grid=(count * tiles,),
        in_specs=[whole, whole, pl.BlockSpec((1, half, tile), lambda n: (first + n // tiles, 0, n % tiles))]
        + [pl.BlockSpec((16, HEAD_DIM), lambda n: (0, 0)) for _ in after],
        out_specs=(part, part),
        out_shape=(
            jax.ShapeDtypeStruct((rows, count * width), jnp.float32),
            jax.ShapeDtypeStruct((rows, count * width), jnp.bfloat16),
        ),
        cost_estimate=pl.CostEstimate(
            flops=4 * rows * half * count * width, bytes_accessed=2 * half * count * width, transcendentals=0
        ),
        compiler_params=pltpu.CompilerParams(vmem_limit_bytes=16 << 20),
        name="terms",
    )(own, other, w_qkv, *after)


def over_heads(width, body, each=1):
    @pl.loop(0, width // (each * HEAD_DIM))
    def _(i):
        for k in range(each):
            at = (each * i + k) * HEAD_DIM
            body(
                pl.ds(pl.multiple_of(at, HEAD_DIM), HEAD_DIM),
                pl.ds(pl.multiple_of(width + at, HEAD_DIM), HEAD_DIM),
            )


def keys_kernel(mine_ref, got_ref, text_ref, gain_ref, tab_ref, first_ref, second_ref):
    rows, width = mine_ref.shape[0], mine_ref.shape[1] // 2
    cut = second_ref.shape[0]
    gain = gain_ref[1:2, :]
    tables = tab_ref[...]

    def head(cols, vcols):
        y = mine_ref[:, cols] + got_ref[:, cols].astype(jnp.float32)
        key = rotate(head_norm(y, gain), tables).astype(jnp.bfloat16)
        first_ref[0 : rows - cut, cols] = key[: rows - cut]
        second_ref[:, cols] = key[rows - cut :]
        prompt = head_norm(text_ref[0, 0, :, cols].astype(jnp.float32), gain)
        first_ref[rows - cut :, cols] = prompt.astype(jnp.bfloat16)
        value = (mine_ref[:, vcols] + got_ref[:, vcols].astype(jnp.float32)).astype(jnp.bfloat16)
        first_ref[0 : rows - cut, vcols] = value[: rows - cut]
        second_ref[:, vcols] = value[rows - cut :]
        first_ref[rows - cut :, vcols] = text_ref[0, 1, :, cols]

    over_heads(width, head)


def keys_values(mine, got, text_kv, gains, tables, cut):
    rows, width = mine.shape
    text_rows = text_kv.shape[2]
    vmem = pl.BlockSpec(memory_space=pltpu.VMEM)
    return pl.pallas_call(
        keys_kernel,
        in_specs=[vmem] * 5,
        out_specs=(vmem, vmem),
        out_shape=(
            jax.ShapeDtypeStruct((rows - cut + text_rows, width), jnp.bfloat16),
            jax.ShapeDtypeStruct((cut, width), jnp.bfloat16),
        ),
        cost_estimate=pl.CostEstimate(flops=1000000000, bytes_accessed=8 * rows * width, transcendentals=0),
        compiler_params=pltpu.CompilerParams(vmem_limit_bytes=12 << 20),
        name="keys",
    )(mine, got, text_kv, gains, tables)


def query_kernel(mine_ref, got_ref, gain_ref, tab_ref, out_ref):
    gain = gain_ref[0:1, :]
    tables = tab_ref[...]

    def head(cols, _):
        y = mine_ref[:, cols] + got_ref[:, cols].astype(jnp.float32)
        out_ref[:, cols] = rotate(head_norm(y, gain), tables).astype(jnp.bfloat16)

    over_heads(mine_ref.shape[1], head)


def query_rows(mine, got, gains, tables):
    vmem = pl.BlockSpec(memory_space=pltpu.VMEM)
    return pl.pallas_call(
        query_kernel,
        in_specs=[vmem] * 4,
        out_specs=vmem,
        out_shape=jax.ShapeDtypeStruct(mine.shape, jnp.bfloat16),
        cost_estimate=pl.CostEstimate(flops=1000000000, bytes_accessed=8 * mine.size, transcendentals=0),
        compiler_params=pltpu.CompilerParams(vmem_limit_bytes=8 << 20),
        name="queries",
    )(mine, got, gains, tables)


SCALE = HEAD_DIM ** (-0.5) * math.log2(math.e)


def attend_block(query, key, value, total, accum, valid=None):
    scores = lax.dot_general(query, key, (((1,), (1,)), ((), ())), preferred_element_type=jnp.float32)
    expo = jnp.exp2(scores * SCALE)
    if valid is not None:
        expo = jnp.where(valid, expo, 0.0)
    for at in range(0, expo.shape[1], HEAD_DIM):
        total = total + expo[:, at : at + HEAD_DIM]
    accum = accum + dot(expo.astype(jnp.bfloat16), value)
    return total, accum


def step_kernel(n_blocks, first, used, *refs):
    q_ref = refs[0]
    blocks = refs[1 : 1 + n_blocks]
    rest = refs[1 + n_blocks :]
    if first:
        sum_out, acc_out, text_out = rest
    else:
        sum_in, acc_in, sum_out, acc_out, text_out = rest
    text_rows = blocks[0].shape[0] - used
    for i in range(0, n_blocks, 2):
        text_out[i // 2 * text_rows : (i // 2 + 1) * text_rows, :] = blocks[i][used:, :]
    rows = slice(0, used)

    def head(cols, vcols):
        if first:
            total = jnp.zeros((q_ref.shape[0], HEAD_DIM), jnp.float32)
            accum = total
        else:
            total, accum = sum_in[:, cols], acc_in[:, cols]
        for i in range(0, n_blocks, 2):
            key = jnp.concatenate([block[rows, cols] for block in blocks[i : i + 2]], axis=0)
            value = jnp.concatenate([block[rows, vcols] for block in blocks[i : i + 2]], axis=0)
            total, accum = attend_block(q_ref[:, cols], key, value, total, accum)
        sum_out[:, cols] = total
        acc_out[:, cols] = accum

    over_heads(q_ref.shape[1], head)


def attend_step(queries, blocks, state, used):
    rows, width = queries.shape
    first = state is None
    shape = jax.ShapeDtypeStruct((rows, width), jnp.float32)
    args = (queries, *blocks) + (() if first else tuple(state))
    n_in = 1 + len(blocks)
    text_rows = (blocks[0].shape[0] - used) * (len(blocks) // 2)
    return pl.pallas_call(
        functools.partial(step_kernel, len(blocks), first, used),
        out_shape=(shape, shape, jax.ShapeDtypeStruct((text_rows, 2 * width), jnp.bfloat16)),
        in_specs=[pl.BlockSpec(memory_space=pltpu.VMEM)] * len(args),
        out_specs=(pl.BlockSpec(memory_space=pltpu.VMEM),) * 3,
        input_output_aliases={} if first else {n_in: 0, n_in + 1: 1},
        cost_estimate=pl.CostEstimate(
            flops=len(blocks) * 16 * rows * used * width, bytes_accessed=4 * rows * width, transcendentals=0
        ),
        compiler_params=pltpu.CompilerParams(vmem_limit_bytes=12 << 20),
        name="attend",
    )(*args)


def last_kernel(offsets, z_ref, length_ref, q_ref, first_ref, second_ref, *rest):
    texts = rest[: len(offsets)]
    sum_in, acc_in, out_ref, prompt = rest[len(offsets) :]
    z, length, n_seq = z_ref[0], length_ref[0], 2 * len(offsets)
    cut = second_ref.shape[0]
    text_rows = first_ref.shape[0] - cut
    width = q_ref.shape[1]

    def place(offset, rows):
        source = lax.rem(z + offset + n_seq, n_seq)
        prompt[pl.ds(pl.multiple_of(source * text_rows, text_rows), text_rows), :] = rows

    for text, pair in zip(texts, offsets):
        for i, offset in enumerate(pair):
            place(offset, text[i * text_rows : (i + 1) * text_rows, :])
    place(len(offsets), first_ref[cut:, :])
    valid = lax.broadcasted_iota(jnp.int32, (q_ref.shape[0], prompt.shape[0]), 1) < length

    def head(cols, vcols):
        query = q_ref[:, cols]
        total, accum = sum_in[:, cols], acc_in[:, cols]
        key = jnp.concatenate([first_ref[0:cut, cols], second_ref[:, cols]], axis=0)
        value = jnp.concatenate([first_ref[0:cut, vcols], second_ref[:, vcols]], axis=0)
        total, accum = attend_block(query, key, value, total, accum)
        total, accum = attend_block(query, prompt[:, cols], prompt[:, vcols], total, accum, valid)
        out_ref[:, cols] = (accum / jnp.sum(total, axis=-1, keepdims=True)).astype(jnp.bfloat16)

    over_heads(width, head, 2)


def attend_last(z, length, queries, first, second, texts, offsets, state):
    rows, width = queries.shape
    n_seq = 2 * len(offsets)
    cut = second.shape[0]
    text_rows = first.shape[0] - cut
    whole = lambda a: pl.BlockSpec(a.shape, lambda i, z, n: (0, 0))
    return pl.pallas_call(
        functools.partial(last_kernel, offsets),
        grid_spec=pltpu.PrefetchScalarGridSpec(
            num_scalar_prefetch=2,
            grid=(1,),
            in_specs=[whole(queries), whole(first), whole(second)]
            + [whole(a) for a in texts]
            + [whole(queries)] * 2,
            out_specs=pl.BlockSpec((rows, width), lambda i, z, n: (0, 0)),
            scratch_shapes=[pltpu.VMEM((n_seq * text_rows, 2 * width), jnp.bfloat16)],
        ),
        out_shape=jax.ShapeDtypeStruct((rows, width), jnp.bfloat16),
        cost_estimate=pl.CostEstimate(flops=32 * rows * rows * width, bytes_accessed=8 * rows * width, transcendentals=0),
        compiler_params=pltpu.CompilerParams(vmem_limit_bytes=16 << 20),
        name="attend_last",
    )(z, length, queries, first, second, *texts, *state)


def out_kernel(n_parts, x_ref, c_ref, strength_ref, own_ref, other_ref, w_ref, mod_ref, *refs):
    outs, scratch = refs[:n_parts], refs[n_parts]
    tile = 2 * HEAD_DIM
    width = w_ref.shape[1]
    x, c = x_ref[0], c_ref[0]
    strength = strength_ref[0]
    mine = jnp.where(c == 0, strength, 1.0 - strength)

    @pl.loop(0, w_ref.shape[1] // tile)
    def _(i):
        cols = pl.ds(pl.multiple_of(i * tile, tile), tile)
        w = w_ref[:, cols]
        own, other = dot(own_ref[...], w), dot(other_ref[...], w)
        place = pl.ds(pl.multiple_of(c * width + i * tile, tile), tile)
        gate = mod_ref[2, pl.ds(c, 1), place]
        other_gate = mod_ref[2, pl.ds(1 - c, 1), place]
        scratch[:, cols] = mine * gate * own + (1.0 - mine) * other_gate * other

    piece = outs[0].shape[0]
    for k, out in enumerate(outs):
        part = lax.rem(x + k, n_parts)
        rows = scratch[pl.ds(pl.multiple_of(part * piece, piece), piece), :]
        out[...] = rows.astype(out.dtype)


def out_parts(x, c, strength, own, other, w_out, mod, n_parts):
    rows, width = own.shape
    cols = w_out.shape[1]
    piece = rows // n_parts
    vmem = pl.BlockSpec(memory_space=pltpu.VMEM)
    return pl.pallas_call(
        functools.partial(out_kernel, n_parts),
        in_specs=[pl.BlockSpec(memory_space=pltpu.SMEM)] * 3 + [vmem] * 4,
        out_specs=(vmem,) * n_parts,
        out_shape=tuple(
            jax.ShapeDtypeStruct((piece, cols), jnp.float32 if k == 0 else jnp.bfloat16) for k in range(n_parts)
        ),
        scratch_shapes=[pltpu.VMEM((rows, cols), jnp.float32)],
        cost_estimate=pl.CostEstimate(flops=4 * rows * width * cols, bytes_accessed=2 * width * cols, transcendentals=0),
        compiler_params=pltpu.CompilerParams(vmem_limit_bytes=16 << 20),
        name="out",
    )(x, c, strength, own, other, w_out, mod)


def block(latent, positions, text_kv, text_len, modulation, w_qkv, norm_gains, w_out, guidance):
    rows = latent.shape[0]
    n_seq, n_tensor = lax.axis_size("seq"), lax.axis_size("tensor")
    c = lax.axis_index("cfg").astype(jnp.int32)
    z = lax.axis_index("seq").astype(jnp.int32)
    x = lax.axis_index("tensor").astype(jnp.int32)
    latent, z, x, branch = lax.optimization_barrier((latent, z[None], x[None], c[None]))
    half = n_seq // 2
    cut = rows // 2
    latent, modulation, w_qkv = (
        pltpu.with_memory_space_constraint(a, pltpu.MemorySpace.HBM) for a in (latent, modulation, w_qkv)
    )
    own, other = modulate(branch, latent, modulation)
    kv_mine, kv_theirs = terms(own, other, w_qkv, 1, 2)
    kv_got = shifted(kv_theirs, "cfg", 1)
    tables = rotary_tables(positions)
    first, second = keys_values(kv_mine, kv_got, text_kv, norm_gains, tables, cut)
    q_mine, q_theirs = terms(own, other, w_qkv, 0, 1, (second,))
    queries = query_rows(q_mine, shifted(q_theirs, "cfg", 1), norm_gains, tables)
    texts, offsets, state = [], [], None
    ahead = behind = (first, second)
    for step in range(1, half + 1):
        if step > 1:
            front, back, state = lax.optimization_barrier((ahead[0], behind[0], state))
            ahead, behind = (front, ahead[1]), (back, behind[1])
        if step < half:
            new_ahead = tuple(shifted(a, "seq", 1) for a in ahead)
            new_behind = tuple(shifted(a, "seq", -1) for a in behind)
        else:
            new_ahead = (shifted(ahead[0], "seq", 1),)
            new_behind = (shifted(behind[1], "seq", -1),)
        *state, text = attend_step(queries, ahead if step == 1 else (*ahead, *behind), state, cut)
        texts.append(text)
        offsets.append((0,) if step == 1 else (1 - step, step - 1))
        ahead, behind = new_ahead, new_behind
    attended = attend_last(z, text_len, queries, ahead[0], behind[0], texts, tuple(offsets), state)
    other = shifted(attended, "cfg", 1)
    parts = out_parts(x, branch, guidance, attended, other, w_out, modulation, n_tensor)
    total = parts[0]
    for k in (2, 1, 3):
        total = total + shifted(parts[k], "tensor", k).astype(jnp.float32)
    return total.astype(jnp.bfloat16)


def solution(mesh):
    placed = (
        P(("groups", "seq"), None),
        P(None, ("groups", "seq")),
        P("cfg", None, ("groups", "seq"), "tensor"),
        P(("groups", "cfg")),
        P(None, "groups", None),
        P(None, "cfg", "tensor"),
        P(),
        P("tensor", "cfg"),
        P("groups"),
    )
    return jax.shard_map(
        block,
        mesh=mesh,
        in_specs=placed,
        out_specs=P(("groups", "seq", "tensor"), "cfg"),
        check_vma=False,
    )
```

profile of v0, /device:TPU:33, one launch (start us, length us, event | category | flops | bytes accessed | tf_op | source)
XLA Modules:
  0.0 199.1 jit_solution(9356459293371964172)
XLA Ops:
  0.0 3.2 %norm.1 = (bf16[256,1536]{1,0:T(8,128)(2,1)S(1)}, bf16[256,1536]{1,0:T(8,128)(2,1)S(1)}) custom-call(s32[1]{0:T(128)} %bitcast.2.c_ref, bf16[256,3072]{1,0:T(8,128)(2,1)} %x_ref, f32[3,2,3072]{2,1,0:T(2,128)} %mod_ref.3), custom_call_target="tpu_custom_call" | custom-call | flops 3000000000 | bytes 3145728 | tf_op jit(solution)/shard_map/norm/pallas_call | solution.py:130
  3.2 0.0 copy-start.2
  3.2 0.0 copy-start.4
  3.2 0.0 copy-start.5
  3.2 0.0 copy-start.1
  3.2 0.0 copy-start.3
  3.3 6.1 %terms.2 = (f32[256,1536]{1,0:T(8,128)S(1)}, bf16[256,1536]{1,0:T(8,128)(2,1)S(1)}) custom-call(bf16[256,1536]{1,0:T(8,128)(2,1)S(1)} %get-tuple-element.77.own_ref, bf16[256,1536]{1,0:T(8,128)(2,1)S(1)} %get-tuple-element.78.other_ref, bf16[3,1536,768]{2,1,0:T(8,128)(2,1)} %w_ref.4), custom_call_target="tpu_custom_call" | custom-call | flops 2415919104 | bytes 4718592 | tf_op jit(solution)/shard_map/terms/pallas_call | solution.py:162
  9.3 20.5 %collective-permute-start = (bf16[256,1536]{1,0:T(8,128)(2,1)S(1)}, bf16[256,1536]{1,0:T(8,128)(2,1)S(1)}, u32[]{:S(2)}, u32[]{:S(2)}) collective-permute-start(bf16[256,1536]{1,0:T(8,128)(2,1)S(1)} %get-tuple-element.80), channel_id=1, source_target_pairs={{0,1},{1,0},{2,3},{3,2},{4,5},{5,4},{6,7},{7,6},{8,9},{9,8},{10,11... | collective-permute-start | bytes 2359304 | tf_op jit(solution)/shard_map/ppermute | solution.py:19
  29.9 0.8 tables.1.tab_ref
  30.6 1.1 collective-permute-done.got_ref
  31.8 2.1 %keys.1 = (bf16[144,1536]{1,0:T(8,128)(2,1)S(1)}, bf16[128,1536]{1,0:T(8,128)(2,1)S(1)}) custom-call(f32[256,1536]{1,0:T(8,128)S(1)} %get-tuple-element.79.mine_ref, bf16[256,1536]{1,0:T(8,128)(2,1)S(1)} %collective-permute-done.got_ref, bf16[1,2,16,768]{3,2,1,0:T(8,128)(2,1)S(1)} %copy-done.1, f32[2,128]{1,0:T(2,128)S(1)} %copy-done.3, ...), custom_call_target="tpu_custom_call" | custom-call | flops 1000000000 | bytes 3145728 | tf_op jit(solution)/shard_map/keys/pallas_call | solution.py:216
  33.9 3.5 %terms.3 = (f32[256,768]{1,0:T(8,128)S(1)}, bf16[256,768]{1,0:T(8,128)(2,1)S(1)}) custom-call(bf16[256,1536]{1,0:T(8,128)(2,1)S(1)} %get-tuple-element.77.own_ref, bf16[256,1536]{1,0:T(8,128)(2,1)S(1)} %get-tuple-element.78.other_ref, bf16[3,1536,768]{2,1,0:T(8,128)(2,1)} %w_ref.4, bf16[128,1536]{1,0:T(8,128)(2,1)S(1)} %get-tuple-element.81.refs_0_.refs_2_), custom_call_target="tpu_custom_call" | custom-call | flops 1207959552 | bytes 2359296 | tf_op jit(solution)/shard_map/terms/pallas_call | solution.py:162
  37.4 0.5 collective-permute-start.1
  37.9 3.1 %collective-permute-start.3 = (bf16[144,1536]{1,0:T(8,128)(2,1)S(1)}, bf16[144,1536]{1,0:T(8,128)(2,1)S(1)}, u32[]{:S(2)}, u32[]{:S(2)}) collective-permute-start(bf16[144,1536]{1,0:T(8,128)(2,1)S(1)} %get-tuple-element.84.refs_1_), channel_id=1, source_target_pairs={{0,120},{8,0},{16,8},{24,16},{32,24},{40,32},{48,40},{56,48},{64,5... | collective-permute-start | bytes 1327112 | tf_op jit(solution)/shard_map/ppermute | solution.py:19
  41.0 2.7 %collective-permute-start.7 = (bf16[128,1536]{1,0:T(8,128)(2,1)S(1)}, bf16[128,1536]{1,0:T(8,128)(2,1)S(1)}, u32[]{:S(2)}, u32[]{:S(2)}) collective-permute-start(bf16[128,1536]{1,0:T(8,128)(2,1)S(1)} %get-tuple-element.81.refs_0_.refs_2_), channel_id=1, source_target_pairs={{0,120},{8,0},{16,8},{24,16},{32,24},{40,32},{48,40},{56,48},{64,5... | collective-permute-start | bytes 1179656 | tf_op jit(solution)/shard_map/ppermute | solution.py:19
  43.7 1.9 queries.1.refs_0_.q_ref
  45.6 2.0 %attend.8 = (f32[256,768]{1,0:T(8,128)S(1)}, f32[256,768]{1,0:T(8,128)S(1)}, bf16[16,1536]{1,0:T(8,128)(2,1)S(1)}) custom-call(bf16[256,768]{1,0:T(8,128)(2,1)S(1)} %queries.1.refs_0_.q_ref, bf16[144,1536]{1,0:T(8,128)(2,1)S(1)} %get-tuple-element.84.refs_1_, bf16[128,1536]{1,0:T(8,128)(2,1)S(1)} %get-tuple-element.81.refs_0_.refs_2_), custom_call_target="tpu_custom_call" | custom-call | flops 805306368 | bytes 786432 | tf_op jit(solution)/shard_map/attend/pallas_call | solution.py:304
  47.6 3.8 %collective-permute-done.2.refs_1_ = bf16[144,1536]{1,0:T(8,128)(2,1)S(1)} collective-permute-done((bf16[144,1536]{1,0:T(8,128)(2,1)S(1)}, bf16[144,1536]{1,0:T(8,128)(2,1)S(1)}, u32[]{:S(2)}, u32[]{:S(2)}) %collective-permute-start.2) | collective-permute-done | bytes 442400 | tf_op jit(solution)/shard_map/ppermute | solution.py:19
  51.4 2.7 %collective-permute-start.5 = (bf16[144,1536]{1,0:T(8,128)(2,1)S(1)}, bf16[144,1536]{1,0:T(8,128)(2,1)S(1)}, u32[]{:S(2)}, u32[]{:S(2)}) collective-permute-start(bf16[144,1536]{1,0:T(8,128)(2,1)S(1)} %collective-permute-done.3.refs_3_), channel_id=1, source_target_pairs={{0,120},{8,0},{16,8},{24,16},{32,24},{40,32},{48,40},{56,48},{64,5... | collective-permute-start | bytes 1327112 | tf_op jit(solution)/shard_map/ppermute | solution.py:19
  54.1 5.7 %collective-permute-done.6.refs_2_ = bf16[128,1536]{1,0:T(8,128)(2,1)S(1)} collective-permute-done((bf16[128,1536]{1,0:T(8,128)(2,1)S(1)}, bf16[128,1536]{1,0:T(8,128)(2,1)S(1)}, u32[]{:S(2)}, u32[]{:S(2)}) %collective-permute-start.6) | collective-permute-done | bytes 393248 | tf_op jit(solution)/shard_map/ppermute | solution.py:19
  59.8 2.7 %collective-permute-start.11 = (bf16[128,1536]{1,0:T(8,128)(2,1)S(1)}, bf16[128,1536]{1,0:T(8,128)(2,1)S(1)}, u32[]{:S(2)}, u32[]{:S(2)}) collective-permute-start(bf16[128,1536]{1,0:T(8,128)(2,1)S(1)} %collective-permute-done.7.refs_4_), channel_id=1, source_target_pairs={{0,120},{8,0},{16,8},{24,16},{32,24},{40,32},{48,40},{56,48},{64,5... | collective-permute-start | bytes 1179656 | tf_op jit(solution)/shard_map/ppermute | solution.py:19
  62.5 3.2 %attend.9 = (f32[256,768]{1,0:T(8,128)S(1)}, f32[256,768]{1,0:T(8,128)S(1)}, bf16[32,1536]{1,0:T(8,128)(2,1)S(1)}) custom-call(bf16[256,768]{1,0:T(8,128)(2,1)S(1)} %queries.1.refs_0_.q_ref, bf16[144,1536]{1,0:T(8,128)(2,1)S(1)} %collective-permute-done.2.refs_1_, ...), custom_call_target="tpu_custom_call", output_to_operand_aliasing={{0}: (5, {}), {1}: (6, {})} | custom-call | flops 1610612736 | bytes 786432 | tf_op jit(solution)/shard_map/attend/pallas_call | solution.py:304
  65.7 3.6 %collective-permute-done.4.refs_1_ = bf16[144,1536]{1,0:T(8,128)(2,1)S(1)} collective-permute-done((bf16[144,1536]{1,0:T(8,128)(2,1)S(1)}, bf16[144,1536]{1,0:T(8,128)(2,1)S(1)}, u32[]{:S(2)}, u32[]{:S(2)}) %collective-permute-start.4) | collective-permute-done | bytes 442400 | tf_op jit(solution)/shard_map/ppermute | solution.py:19
  69.3 2.7 %collective-permute-start.9 = (bf16[144,1536]{1,0:T(8,128)(2,1)S(1)}, bf16[144,1536]{1,0:T(8,128)(2,1)S(1)}, u32[]{:S(2)}, u32[]{:S(2)}) collective-permute-start(bf16[144,1536]{1,0:T(8,128)(2,1)S(1)} %collective-permute-done.5.refs_3_), channel_id=1, source_target_pairs={{0,120},{8,0},{16,8},{24,16},{32,24},{40,32},{48,40},{56,48},{64,5... | collective-permute-start | bytes 1327112 | tf_op jit(solution)/shard_map/ppermute | solution.py:19
  72.0 5.7 %collective-permute-done.10.refs_2_ = bf16[128,1536]{1,0:T(8,128)(2,1)S(1)} collective-permute-done((bf16[128,1536]{1,0:T(8,128)(2,1)S(1)}, bf16[128,1536]{1,0:T(8,128)(2,1)S(1)}, u32[]{:S(2)}, u32[]{:S(2)}) %collective-permute-start.10) | collective-permute-done | bytes 393248 | tf_op jit(solution)/shard_map/ppermute | solution.py:19
  77.7 0.0 collective-permute-start.14
  77.7 2.7 %collective-permute-start.15 = (bf16[128,1536]{1,0:T(8,128)(2,1)S(1)}, bf16[128,1536]{1,0:T(8,128)(2,1)S(1)}, u32[]{:S(2)}, u32[]{:S(2)}) collective-permute-start(bf16[128,1536]{1,0:T(8,128)(2,1)S(1)} %collective-permute-done.11.refs_4_), channel_id=1, source_target_pairs={{0,120},{8,0},{16,8},{24,16},{32,24},{40,32},{48,40},{56,48},{64,5... | collective-permute-start | bytes 1179656 | tf_op jit(solution)/shard_map/ppermute | solution.py:19
  80.4 3.2 %attend.10 = (f32[256,768]{1,0:T(8,128)S(1)}, f32[256,768]{1,0:T(8,128)S(1)}, bf16[32,1536]{1,0:T(8,128)(2,1)S(1)}) custom-call(bf16[256,768]{1,0:T(8,128)(2,1)S(1)} %queries.1.refs_0_.q_ref, bf16[144,1536]{1,0:T(8,128)(2,1)S(1)} %collective-permute-done.4.refs_1_, ...), custom_call_target="tpu_custom_call", output_to_operand_aliasing={{0}: (5, {}), {1}: (6, {})} | custom-call | flops 1610612736 | bytes 786432 | tf_op jit(solution)/shard_map/attend/pallas_call | solution.py:304
  83.6 3.6 %collective-permute-done.8.refs_1_ = bf16[144,1536]{1,0:T(8,128)(2,1)S(1)} collective-permute-done((bf16[144,1536]{1,0:T(8,128)(2,1)S(1)}, bf16[144,1536]{1,0:T(8,128)(2,1)S(1)}, u32[]{:S(2)}, u32[]{:S(2)}) %collective-permute-start.8) | collective-permute-done | bytes 442400 | tf_op jit(solution)/shard_map/ppermute | solution.py:19
  87.2 2.7 %collective-permute-start.13 = (bf16[144,1536]{1,0:T(8,128)(2,1)S(1)}, bf16[144,1536]{1,0:T(8,128)(2,1)S(1)}, u32[]{:S(2)}, u32[]{:S(2)}) collective-permute-start(bf16[144,1536]{1,0:T(8,128)(2,1)S(1)} %collective-permute-done.9.refs_3_), channel_id=1, source_target_pairs={{0,120},{8,0},{16,8},{24,16},{32,24},{40,32},{48,40},{56,48},{64,5... | collective-permute-start | bytes 1327112 | tf_op jit(solution)/shard_map/ppermute | solution.py:19
  89.9 4.6 %collective-permute-done.15.refs_4_ = bf16[128,1536]{1,0:T(8,128)(2,1)S(1)} collective-permute-done((bf16[128,1536]{1,0:T(8,128)(2,1)S(1)}, bf16[128,1536]{1,0:T(8,128)(2,1)S(1)}, u32[]{:S(2)}, u32[]{:S(2)}) %collective-permute-start.15) | collective-permute-done | bytes 393248 | tf_op jit(solution)/shard_map/ppermute | solution.py:19
  94.5 3.4 %collective-permute-start.19 = (bf16[128,1536]{1,0:T(8,128)(2,1)S(1)}, bf16[128,1536]{1,0:T(8,128)(2,1)S(1)}, u32[]{:S(2)}, u32[]{:S(2)}) collective-permute-start(bf16[128,1536]{1,0:T(8,128)(2,1)S(1)} %collective-permute-done.15.refs_4_), channel_id=1, source_target_pairs={{0,120},{8,0},{16,8},{24,16},{32,24},{40,32},{48,40},{56,48},{64,5... | collective-permute-start | bytes 1179656 | tf_op jit(solution)/shard_map/ppermute | solution.py:19
  97.9 3.2 %attend.11 = (f32[256,768]{1,0:T(8,128)S(1)}, f32[256,768]{1,0:T(8,128)S(1)}, bf16[32,1536]{1,0:T(8,128)(2,1)S(1)}) custom-call(bf16[256,768]{1,0:T(8,128)(2,1)S(1)} %queries.1.refs_0_.q_ref, bf16[144,1536]{1,0:T(8,128)(2,1)S(1)} %collective-permute-done.8.refs_1_, ...), custom_call_target="tpu_custom_call", output_to_operand_aliasing={{0}: (5, {}), {1}: (6, {})} | custom-call | flops 1610612736 | bytes 786432 | tf_op jit(solution)/shard_map/attend/pallas_call | solution.py:304
  101.2 4.0 %collective-permute-done.12.refs_1_ = bf16[144,1536]{1,0:T(8,128)(2,1)S(1)} collective-permute-done((bf16[144,1536]{1,0:T(8,128)(2,1)S(1)}, bf16[144,1536]{1,0:T(8,128)(2,1)S(1)}, u32[]{:S(2)}, u32[]{:S(2)}) %collective-permute-start.12) | collective-permute-done | bytes 442400 | tf_op jit(solution)/shard_map/ppermute | solution.py:19
  105.1 2.7 %collective-permute-start.17 = (bf16[144,1536]{1,0:T(8,128)(2,1)S(1)}, bf16[144,1536]{1,0:T(8,128)(2,1)S(1)}, u32[]{:S(2)}, u32[]{:S(2)}) collective-permute-start(bf16[144,1536]{1,0:T(8,128)(2,1)S(1)} %collective-permute-done.13.refs_3_), channel_id=1, source_target_pairs={{0,120},{8,0},{16,8},{24,16},{32,24},{40,32},{48,40},{56,48},{64,5... | collective-permute-start | bytes 1327112 | tf_op jit(solution)/shard_map/ppermute | solution.py:19
  107.8 4.6 %collective-permute-done.19.refs_4_ = bf16[128,1536]{1,0:T(8,128)(2,1)S(1)} collective-permute-done((bf16[128,1536]{1,0:T(8,128)(2,1)S(1)}, bf16[128,1536]{1,0:T(8,128)(2,1)S(1)}, u32[]{:S(2)}, u32[]{:S(2)}) %collective-permute-start.19) | collective-permute-done | bytes 393248 | tf_op jit(solution)/shard_map/ppermute | solution.py:19
  112.4 3.4 %collective-permute-start.23 = (bf16[128,1536]{1,0:T(8,128)(2,1)S(1)}, bf16[128,1536]{1,0:T(8,128)(2,1)S(1)}, u32[]{:S(2)}, u32[]{:S(2)}) collective-permute-start(bf16[128,1536]{1,0:T(8,128)(2,1)S(1)} %collective-permute-done.19.refs_4_), channel_id=1, source_target_pairs={{0,120},{8,0},{16,8},{24,16},{32,24},{40,32},{48,40},{56,48},{64,5... | collective-permute-start | bytes 1179656 | tf_op jit(solution)/shard_map/ppermute | solution.py:19
  115.8 3.2 %attend.12 = (f32[256,768]{1,0:T(8,128)S(1)}, f32[256,768]{1,0:T(8,128)S(1)}, bf16[32,1536]{1,0:T(8,128)(2,1)S(1)}) custom-call(bf16[256,768]{1,0:T(8,128)(2,1)S(1)} %queries.1.refs_0_.q_ref, bf16[144,1536]{1,0:T(8,128)(2,1)S(1)} %collective-permute-done.12.refs_1_, ...), custom_call_target="tpu_custom_call", output_to_operand_aliasing={{0}: (5, {}), {1}: (6, {})} | custom-call | flops 1610612736 | bytes 786432 | tf_op jit(solution)/shard_map/attend/pallas_call | solution.py:304
  119.1 4.0 %collective-permute-done.16.refs_1_ = bf16[144,1536]{1,0:T(8,128)(2,1)S(1)} collective-permute-done((bf16[144,1536]{1,0:T(8,128)(2,1)S(1)}, bf16[144,1536]{1,0:T(8,128)(2,1)S(1)}, u32[]{:S(2)}, u32[]{:S(2)}) %collective-permute-start.16) | collective-permute-done | bytes 442400 | tf_op jit(solution)/shard_map/ppermute | solution.py:19
  123.0 2.7 %collective-permute-start.21 = (bf16[144,1536]{1,0:T(8,128)(2,1)S(1)}, bf16[144,1536]{1,0:T(8,128)(2,1)S(1)}, u32[]{:S(2)}, u32[]{:S(2)}) collective-permute-start(bf16[144,1536]{1,0:T(8,128)(2,1)S(1)} %collective-permute-done.17.refs_3_), channel_id=1, source_target_pairs={{0,120},{8,0},{16,8},{24,16},{32,24},{40,32},{48,40},{56,48},{64,5... | collective-permute-start | bytes 1327112 | tf_op jit(solution)/shard_map/ppermute | solution.py:19
  125.7 4.6 %collective-permute-done.23.refs_4_ = bf16[128,1536]{1,0:T(8,128)(2,1)S(1)} collective-permute-done((bf16[128,1536]{1,0:T(8,128)(2,1)S(1)}, bf16[128,1536]{1,0:T(8,128)(2,1)S(1)}, u32[]{:S(2)}, u32[]{:S(2)}) %collective-permute-start.23) | collective-permute-done | bytes 393248 | tf_op jit(solution)/shard_map/ppermute | solution.py:19
  130.3 3.4 %collective-permute-start.27 = (bf16[128,1536]{1,0:T(8,128)(2,1)S(1)}, bf16[128,1536]{1,0:T(8,128)(2,1)S(1)}, u32[]{:S(2)}, u32[]{:S(2)}) collective-permute-start(bf16[128,1536]{1,0:T(8,128)(2,1)S(1)} %collective-permute-done.23.refs_4_), channel_id=1, source_target_pairs={{0,120},{8,0},{16,8},{24,16},{32,24},{40,32},{48,40},{56,48},{64,5... | collective-permute-start | bytes 1179656 | tf_op jit(solution)/shard_map/ppermute | solution.py:19
  133.7 3.2 %attend.13 = (f32[256,768]{1,0:T(8,128)S(1)}, f32[256,768]{1,0:T(8,128)S(1)}, bf16[32,1536]{1,0:T(8,128)(2,1)S(1)}) custom-call(bf16[256,768]{1,0:T(8,128)(2,1)S(1)} %queries.1.refs_0_.q_ref, bf16[144,1536]{1,0:T(8,128)(2,1)S(1)} %collective-permute-done.16.refs_1_, ...), custom_call_target="tpu_custom_call", output_to_operand_aliasing={{0}: (5, {}), {1}: (6, {})} | custom-call | flops 1610612736 | bytes 786432 | tf_op jit(solution)/shard_map/attend/pallas_call | solution.py:304
  137.0 4.0 %collective-permute-done.20.refs_1_ = bf16[144,1536]{1,0:T(8,128)(2,1)S(1)} collective-permute-done((bf16[144,1536]{1,0:T(8,128)(2,1)S(1)}, bf16[144,1536]{1,0:T(8,128)(2,1)S(1)}, u32[]{:S(2)}, u32[]{:S(2)}) %collective-permute-start.20) | collective-permute-done | bytes 442400 | tf_op jit(solution)/shard_map/ppermute | solution.py:19
  140.9 0.0 collective-permute-start.24
  140.9 2.7 %collective-permute-start.25 = (bf16[144,1536]{1,0:T(8,128)(2,1)S(1)}, bf16[144,1536]{1,0:T(8,128)(2,1)S(1)}, u32[]{:S(2)}, u32[]{:S(2)}) collective-permute-start(bf16[144,1536]{1,0:T(8,128)(2,1)S(1)} %collective-permute-done.21.refs_3_), channel_id=1, source_target_pairs={{0,120},{8,0},{16,8},{24,16},{32,24},{40,32},{48,40},{56,48},{64,5... | collective-permute-start | bytes 1327112 | tf_op jit(solution)/shard_map/ppermute | solution.py:19
  143.6 4.6 %collective-permute-done.27.refs_4_ = bf16[128,1536]{1,0:T(8,128)(2,1)S(1)} collective-permute-done((bf16[128,1536]{1,0:T(8,128)(2,1)S(1)}, bf16[128,1536]{1,0:T(8,128)(2,1)S(1)}, u32[]{:S(2)}, u32[]{:S(2)}) %collective-permute-start.27) | collective-permute-done | bytes 393248 | tf_op jit(solution)/shard_map/ppermute | solution.py:19
  148.2 3.4 %collective-permute-start.29 = (bf16[128,1536]{1,0:T(8,128)(2,1)S(1)}, bf16[128,1536]{1,0:T(8,128)(2,1)S(1)}, u32[]{:S(2)}, u32[]{:S(2)}) collective-permute-start(bf16[128,1536]{1,0:T(8,128)(2,1)S(1)} %collective-permute-done.27.refs_4_), channel_id=1, source_target_pairs={{0,120},{8,0},{16,8},{24,16},{32,24},{40,32},{48,40},{56,48},{64,5... | collective-permute-start | bytes 1179656 | tf_op jit(solution)/shard_map/ppermute | solution.py:19
  151.7 3.2 %attend.14 = (f32[256,768]{1,0:T(8,128)S(1)}, f32[256,768]{1,0:T(8,128)S(1)}, bf16[32,1536]{1,0:T(8,128)(2,1)S(1)}) custom-call(bf16[256,768]{1,0:T(8,128)(2,1)S(1)} %queries.1.refs_0_.q_ref, bf16[144,1536]{1,0:T(8,128)(2,1)S(1)} %collective-permute-done.20.refs_1_, ...), custom_call_target="tpu_custom_call", output_to_operand_aliasing={{0}: (5, {}), {1}: (6, {})} | custom-call | flops 1610612736 | bytes 786432 | tf_op jit(solution)/shard_map/attend/pallas_call | solution.py:304
  154.9 4.0 %collective-permute-done.24.refs_1_ = bf16[144,1536]{1,0:T(8,128)(2,1)S(1)} collective-permute-done((bf16[144,1536]{1,0:T(8,128)(2,1)S(1)}, bf16[144,1536]{1,0:T(8,128)(2,1)S(1)}, u32[]{:S(2)}, u32[]{:S(2)}) %collective-permute-start.24) | collective-permute-done | bytes 442400 | tf_op jit(solution)/shard_map/ppermute | solution.py:19
  158.9 7.3 %collective-permute-done.29.refs_4_ = bf16[128,1536]{1,0:T(8,128)(2,1)S(1)} collective-permute-done((bf16[128,1536]{1,0:T(8,128)(2,1)S(1)}, bf16[128,1536]{1,0:T(8,128)(2,1)S(1)}, u32[]{:S(2)}, u32[]{:S(2)}) %collective-permute-start.29) | collective-permute-done | bytes 393248 | tf_op jit(solution)/shard_map/ppermute | solution.py:19
  166.1 3.4 %collective-permute-start.30 = (bf16[128,1536]{1,0:T(8,128)(2,1)S(1)}, bf16[128,1536]{1,0:T(8,128)(2,1)S(1)}, u32[]{:S(2)}, u32[]{:S(2)}) collective-permute-start(bf16[128,1536]{1,0:T(8,128)(2,1)S(1)} %collective-permute-done.29.refs_4_), channel_id=1, source_target_pairs={{0,120},{8,0},{16,8},{24,16},{32,24},{40,32},{48,40},{56,48},{64,5... | collective-permute-start | bytes 1179656 | tf_op jit(solution)/shard_map/ppermute | solution.py:19
  170.2 3.2 %attend.15 = (f32[256,768]{1,0:T(8,128)S(1)}, f32[256,768]{1,0:T(8,128)S(1)}, bf16[32,1536]{1,0:T(8,128)(2,1)S(1)}) custom-call(bf16[256,768]{1,0:T(8,128)(2,1)S(1)} %queries.1.refs_0_.q_ref, bf16[144,1536]{1,0:T(8,128)(2,1)S(1)} %collective-permute-done.24.refs_1_, ...), custom_call_target="tpu_custom_call", output_to_operand_aliasing={{0}: (5, {}), {1}: (6, {})} | custom-call | flops 1610612736 | bytes 786432 | tf_op jit(solution)/shard_map/attend/pallas_call | solution.py:304
  173.5 3.4 %collective-permute-done.30.second_ref = bf16[128,1536]{1,0:T(8,128)(2,1)S(1)} collective-permute-done((bf16[128,1536]{1,0:T(8,128)(2,1)S(1)}, bf16[128,1536]{1,0:T(8,128)(2,1)S(1)}, u32[]{:S(2)}, u32[]{:S(2)}) %collective-permute-start.30) | collective-permute-done | bytes 393248 | tf_op jit(solution)/shard_map/ppermute | solution.py:19
  176.9 2.1 %attend_last.1.own_ref = bf16[256,768]{1,0:T(8,128)(2,1)S(1)} custom-call(s32[1]{0:T(128)} %bitcast.z_ref, s32[1]{0:T(128)S(6)} %copy.40.length_ref, bf16[256,768]{1,0:T(8,128)(2,1)S(1)} %queries.1.refs_0_.q_ref, bf16[144,1536]{1,0:T(8,128)(2,1)S(1)} %collective-permute-done.28.first_ref, bf16[128,1536]{1,0:T(8,128)(2,1)S(1)} %collective-permute-done.30.second_ref, ...), custom_call_target="tpu_custom_call" | custom-call | flops 1610612736 | bytes 1572864 | tf_op jit(solution)/shard_map/attend_last/pallas_call | solution.py:354
  179.0 2.1 %collective-permute-start.32 = (bf16[256,768]{1,0:T(8,128)(2,1)S(1)}, bf16[256,768]{1,0:T(8,128)(2,1)S(1)}, u32[]{:S(2)}, u32[]{:S(2)}) collective-permute-start(bf16[256,768]{1,0:T(8,128)(2,1)S(1)} %attend_last.1.own_ref), channel_id=1, source_target_pairs={{0,1},{1,0},{2,3},{3,2},{4,5},{5,4},{6,7},{7,6},{8,9},{9,8},{10,11... | collective-permute-start | bytes 1179656 | tf_op jit(solution)/shard_map/ppermute | solution.py:19
  181.8 0.7 collective-permute-done.32.other_ref
  182.5 3.2 %out.1 = (f32[64,1536]{1,0:T(8,128)S(1)}, bf16[64,1536]{1,0:T(8,128)(2,1)S(1)}, bf16[64,1536]{1,0:T(8,128)(2,1)S(1)}, bf16[64,1536]{1,0:T(8,128)(2,1)S(1)}) custom-call(s32[1]{0:T(128)} %bitcast.1.x_ref, s32[1]{0:T(128)} %bitcast.2.c_ref, f32[1]{0:T(128)S(6)} %copy.41.strength_ref, bf16[256,768]{1,0:T(8,128)(2,1)S(1)} %attend_last.1.own_ref, ...), custom_call_target="tpu_custom_call" | custom-call | flops 1207959552 | bytes 2359296 | tf_op jit(solution)/shard_map/out/pallas_call | solution.py:402
  185.7 3.1 %collective-permute-start.33 = (bf16[64,1536]{1,0:T(8,128)(2,1)S(1)}, bf16[64,1536]{1,0:T(8,128)(2,1)S(1)}, u32[]{:S(2)}, u32[]{:S(2)}) collective-permute-start(bf16[64,1536]{1,0:T(8,128)(2,1)S(1)} %get-tuple-element.138), channel_id=1, source_target_pairs={{0,4},{2,6},{4,0},{6,2},{1,5},{3,7},{5,1},{7,3},{8,12},{10,14},{12... | collective-permute-start | bytes 589832 | tf_op jit(solution)/shard_map/ppermute | solution.py:19
  188.8 0.4 collective-permute-start.34
  189.3 2.2 %collective-permute-start.35 = (bf16[64,1536]{1,0:T(8,128)(2,1)S(1)}, bf16[64,1536]{1,0:T(8,128)(2,1)S(1)}, u32[]{:S(2)}, u32[]{:S(2)}) collective-permute-start(bf16[64,1536]{1,0:T(8,128)(2,1)S(1)} %get-tuple-element.140), channel_id=1, source_target_pairs={{0,6},{2,0},{4,2},{6,4},{1,7},{3,1},{5,3},{7,5},{8,14},{10,8},{12,... | collective-permute-start | bytes 589832 | tf_op jit(solution)/shard_map/ppermute | solution.py:19
  191.5 2.0 %collective-permute-done.33 = bf16[64,1536]{1,0:T(8,128)(2,1)S(1)} collective-permute-done((bf16[64,1536]{1,0:T(8,128)(2,1)S(1)}, bf16[64,1536]{1,0:T(8,128)(2,1)S(1)}, u32[]{:S(2)}, u32[]{:S(2)}) %collective-permute-start.33) | collective-permute-done | bytes 196640 | tf_op jit(solution)/shard_map/ppermute | solution.py:19
  193.5 4.8 %collective-permute-done.34 = bf16[64,1536]{1,0:T(8,128)(2,1)S(1)} collective-permute-done((bf16[64,1536]{1,0:T(8,128)(2,1)S(1)}, bf16[64,1536]{1,0:T(8,128)(2,1)S(1)}, u32[]{:S(2)}, u32[]{:S(2)}) %collective-permute-start.34) | collective-permute-done | bytes 196640 | tf_op jit(solution)/shard_map/ppermute | solution.py:19
  198.4 0.8 add_convert_fusion
  (37 shorter events, 0.1 us)
Async XLA Ops:
  3.2 26.7 %copy-start.2 = (s32[3,256]{1,0:T(4,128)S(1)}, s32[3,256]{1,0:T(4,128)}, u32[]{:S(2)}) copy-start(s32[3,256]{1,0:T(4,128)} %pos_ref.1) | copy-start | bytes 9220
  3.2 26.7 %copy-start.4 = (bf16[256,512]{1,0:T(8,128)(2,1)S(1)}, bf16[256,512]{1,0:T(8,128)(2,1)}, u32[]{:S(2)}) copy-start(bf16[256,512]{1,0:T(8,128)(2,1)} %constant.17.clone.turn_ref) | copy-start | bytes 786436
  3.2 26.7 %copy-start.5 = (f32[4,128]{1,0:T(4,128)S(1)}, f32[4,128]{1,0:T(4,128)}, u32[]{:S(2)}) copy-start(f32[4,128]{1,0:T(4,128)} %constant.18.clone.sign_ref) | copy-start | bytes 6148
  3.2 28.6 %copy-start.1 = (bf16[1,2,16,768]{3,2,1,0:T(8,128)(2,1)S(1)}, bf16[1,2,16,768]{3,2,1,0:T(8,128)(2,1)}, u32[]{:S(2)}) copy-start(bf16[1,2,16,768]{3,2,1,0:T(8,128)(2,1)} %text_ref.1) | copy-start | bytes 147460
  3.2 28.5 %copy-start.3 = (f32[2,128]{1,0:T(2,128)S(1)}, f32[2,128]{1,0:T(2,128)}, u32[]{:S(2)}) copy-start(f32[2,128]{1,0:T(2,128)} %gain_ref.3) | copy-start | bytes 3076
  9.3 22.4 %collective-permute-start = (bf16[256,1536]{1,0:T(8,128)(2,1)S(1)}, bf16[256,1536]{1,0:T(8,128)(2,1)S(1)}, u32[]{:S(2)}, u32[]{:S(2)}) collective-permute-start(bf16[256,1536]{1,0:T(8,128)(2,1)S(1)} %get-tuple-element.80), channel_id=1, source_target_pairs={{0,1},{1,0},{2,3},{3,2},{4,5},{5,4},{6,7},{7,6},{8,9},{9,8},{10,11... | collective-permute-start | bytes 2359304 | tf_op jit(solution)/shard_map/ppermute | solution.py:19
  37.4 6.3 %collective-permute-start.1 = (bf16[256,768]{1,0:T(8,128)(2,1)S(1)}, bf16[256,768]{1,0:T(8,128)(2,1)S(1)}, u32[]{:S(2)}, u32[]{:S(2)}) collective-permute-start(bf16[256,768]{1,0:T(8,128)(2,1)S(1)} %get-tuple-element.83), channel_id=1, source_target_pairs={{0,1},{1,0},{2,3},{3,2},{4,5},{5,4},{6,7},{7,6},{8,9},{9,8},{10,11... | collective-permute-start | bytes 1179656 | tf_op jit(solution)/shard_map/ppermute | solution.py:19
  37.9 13.5 %collective-permute-start.2 = (bf16[144,1536]{1,0:T(8,128)(2,1)S(1)}, bf16[144,1536]{1,0:T(8,128)(2,1)S(1)}, u32[]{:S(2)}, u32[]{:S(2)}) collective-permute-start(bf16[144,1536]{1,0:T(8,128)(2,1)S(1)} %get-tuple-element.84.refs_1_), channel_id=1, source_target_pairs={{0,8},{8,16},{16,24},{24,32},{32,40},{40,48},{48,56},{56,64},{64,7... | collective-permute-start | bytes 1327112 | tf_op jit(solution)/shard_map/ppermute | solution.py:19
  37.9 13.5 %collective-permute-start.3 = (bf16[144,1536]{1,0:T(8,128)(2,1)S(1)}, bf16[144,1536]{1,0:T(8,128)(2,1)S(1)}, u32[]{:S(2)}, u32[]{:S(2)}) collective-permute-start(bf16[144,1536]{1,0:T(8,128)(2,1)S(1)} %get-tuple-element.84.refs_1_), channel_id=1, source_target_pairs={{0,120},{8,0},{16,8},{24,16},{32,24},{40,32},{48,40},{56,48},{64,5... | collective-permute-start | bytes 1327112 | tf_op jit(solution)/shard_map/ppermute | solution.py:19
  41.0 18.8 %collective-permute-start.6 = (bf16[128,1536]{1,0:T(8,128)(2,1)S(1)}, bf16[128,1536]{1,0:T(8,128)(2,1)S(1)}, u32[]{:S(2)}, u32[]{:S(2)}) collective-permute-start(bf16[128,1536]{1,0:T(8,128)(2,1)S(1)} %get-tuple-element.81.refs_0_.refs_2_), channel_id=1, source_target_pairs={{0,8},{8,16},{16,24},{24,32},{32,40},{40,48},{48,56},{56,64},{64,7... | collective-permute-start | bytes 1179656 | tf_op jit(solution)/shard_map/ppermute | solution.py:19
  41.0 18.8 %collective-permute-start.7 = (bf16[128,1536]{1,0:T(8,128)(2,1)S(1)}, bf16[128,1536]{1,0:T(8,128)(2,1)S(1)}, u32[]{:S(2)}, u32[]{:S(2)}) collective-permute-start(bf16[128,1536]{1,0:T(8,128)(2,1)S(1)} %get-tuple-element.81.refs_0_.refs_2_), channel_id=1, source_target_pairs={{0,120},{8,0},{16,8},{24,16},{32,24},{40,32},{48,40},{56,48},{64,5... | collective-permute-start | bytes 1179656 | tf_op jit(solution)/shard_map/ppermute | solution.py:19
  51.4 17.9 %collective-permute-start.4 = (bf16[144,1536]{1,0:T(8,128)(2,1)S(1)}, bf16[144,1536]{1,0:T(8,128)(2,1)S(1)}, u32[]{:S(2)}, u32[]{:S(2)}) collective-permute-start(bf16[144,1536]{1,0:T(8,128)(2,1)S(1)} %collective-permute-done.2.refs_1_), channel_id=1, source_target_pairs={{0,8},{8,16},{16,24},{24,32},{32,40},{40,48},{48,56},{56,64},{64,7... | collective-permute-start | bytes 1327112 | tf_op jit(solution)/shard_map/ppermute | solution.py:19
  51.4 17.9 %collective-permute-start.5 = (bf16[144,1536]{1,0:T(8,128)(2,1)S(1)}, bf16[144,1536]{1,0:T(8,128)(2,1)S(1)}, u32[]{:S(2)}, u32[]{:S(2)}) collective-permute-start(bf16[144,1536]{1,0:T(8,128)(2,1)S(1)} %collective-permute-done.3.refs_3_), channel_id=1, source_target_pairs={{0,120},{8,0},{16,8},{24,16},{32,24},{40,32},{48,40},{56,48},{64,5... | collective-permute-start | bytes 1327112 | tf_op jit(solution)/shard_map/ppermute | solution.py:19
  59.8 17.9 %collective-permute-start.10 = (bf16[128,1536]{1,0:T(8,128)(2,1)S(1)}, bf16[128,1536]{1,0:T(8,128)(2,1)S(1)}, u32[]{:S(2)}, u32[]{:S(2)}) collective-permute-start(bf16[128,1536]{1,0:T(8,128)(2,1)S(1)} %collective-permute-done.6.refs_2_), channel_id=1, source_target_pairs={{0,8},{8,16},{16,24},{24,32},{32,40},{40,48},{48,56},{56,64},{64,7... | collective-permute-start | bytes 1179656 | tf_op jit(solution)/shard_map/ppermute | solution.py:19
  59.8 17.9 %collective-permute-start.11 = (bf16[128,1536]{1,0:T(8,128)(2,1)S(1)}, bf16[128,1536]{1,0:T(8,128)(2,1)S(1)}, u32[]{:S(2)}, u32[]{:S(2)}) collective-permute-start(bf16[128,1536]{1,0:T(8,128)(2,1)S(1)} %collective-permute-done.7.refs_4_), channel_id=1, source_target_pairs={{0,120},{8,0},{16,8},{24,16},{32,24},{40,32},{48,40},{56,48},{64,5... | collective-permute-start | bytes 1179656 | tf_op jit(solution)/shard_map/ppermute | solution.py:19
  69.3 17.9 %collective-permute-start.8 = (bf16[144,1536]{1,0:T(8,128)(2,1)S(1)}, bf16[144,1536]{1,0:T(8,128)(2,1)S(1)}, u32[]{:S(2)}, u32[]{:S(2)}) collective-permute-start(bf16[144,1536]{1,0:T(8,128)(2,1)S(1)} %collective-permute-done.4.refs_1_), channel_id=1, source_target_pairs={{0,8},{8,16},{16,24},{24,32},{32,40},{40,48},{48,56},{56,64},{64,7... | collective-permute-start | bytes 1327112 | tf_op jit(solution)/shard_map/ppermute | solution.py:19
  69.3 17.9 %collective-permute-start.9 = (bf16[144,1536]{1,0:T(8,128)(2,1)S(1)}, bf16[144,1536]{1,0:T(8,128)(2,1)S(1)}, u32[]{:S(2)}, u32[]{:S(2)}) collective-permute-start(bf16[144,1536]{1,0:T(8,128)(2,1)S(1)} %collective-permute-done.5.refs_3_), channel_id=1, source_target_pairs={{0,120},{8,0},{16,8},{24,16},{32,24},{40,32},{48,40},{56,48},{64,5... | collective-permute-start | bytes 1327112 | tf_op jit(solution)/shard_map/ppermute | solution.py:19
  77.7 20.2 %collective-permute-start.14 = (bf16[128,1536]{1,0:T(8,128)(2,1)S(1)}, bf16[128,1536]{1,0:T(8,128)(2,1)S(1)}, u32[]{:S(2)}, u32[]{:S(2)}) collective-permute-start(bf16[128,1536]{1,0:T(8,128)(2,1)S(1)} %collective-permute-done.10.refs_2_), channel_id=1, source_target_pairs={{0,8},{8,16},{16,24},{24,32},{32,40},{40,48},{48,56},{56,64},{64,7... | collective-permute-start | bytes 1179656 | tf_op jit(solution)/shard_map/ppermute | solution.py:19
  77.7 16.8 %collective-permute-start.15 = (bf16[128,1536]{1,0:T(8,128)(2,1)S(1)}, bf16[128,1536]{1,0:T(8,128)(2,1)S(1)}, u32[]{:S(2)}, u32[]{:S(2)}) collective-permute-start(bf16[128,1536]{1,0:T(8,128)(2,1)S(1)} %collective-permute-done.11.refs_4_), channel_id=1, source_target_pairs={{0,120},{8,0},{16,8},{24,16},{32,24},{40,32},{48,40},{56,48},{64,5... | collective-permute-start | bytes 1179656 | tf_op jit(solution)/shard_map/ppermute | solution.py:19
  87.2 17.9 %collective-permute-start.12 = (bf16[144,1536]{1,0:T(8,128)(2,1)S(1)}, bf16[144,1536]{1,0:T(8,128)(2,1)S(1)}, u32[]{:S(2)}, u32[]{:S(2)}) collective-permute-start(bf16[144,1536]{1,0:T(8,128)(2,1)S(1)} %collective-permute-done.8.refs_1_), channel_id=1, source_target_pairs={{0,8},{8,16},{16,24},{24,32},{32,40},{40,48},{48,56},{56,64},{64,7... | collective-permute-start | bytes 1327112 | tf_op jit(solution)/shard_map/ppermute | solution.py:19
  87.2 17.9 %collective-permute-start.13 = (bf16[144,1536]{1,0:T(8,128)(2,1)S(1)}, bf16[144,1536]{1,0:T(8,128)(2,1)S(1)}, u32[]{:S(2)}, u32[]{:S(2)}) collective-permute-start(bf16[144,1536]{1,0:T(8,128)(2,1)S(1)} %collective-permute-done.9.refs_3_), channel_id=1, source_target_pairs={{0,120},{8,0},{16,8},{24,16},{32,24},{40,32},{48,40},{56,48},{64,5... | collective-permute-start | bytes 1327112 | tf_op jit(solution)/shard_map/ppermute | solution.py:19
  94.5 17.9 %collective-permute-start.19 = (bf16[128,1536]{1,0:T(8,128)(2,1)S(1)}, bf16[128,1536]{1,0:T(8,128)(2,1)S(1)}, u32[]{:S(2)}, u32[]{:S(2)}) collective-permute-start(bf16[128,1536]{1,0:T(8,128)(2,1)S(1)} %collective-permute-done.15.refs_4_), channel_id=1, source_target_pairs={{0,120},{8,0},{16,8},{24,16},{32,24},{40,32},{48,40},{56,48},{64,5... | collective-permute-start | bytes 1179656 | tf_op jit(solution)/shard_map/ppermute | solution.py:19
  97.9 17.9 %collective-permute-start.18 = (bf16[128,1536]{1,0:T(8,128)(2,1)S(1)}, bf16[128,1536]{1,0:T(8,128)(2,1)S(1)}, u32[]{:S(2)}, u32[]{:S(2)}) collective-permute-start(bf16[128,1536]{1,0:T(8,128)(2,1)S(1)} %collective-permute-done.14.refs_2_), channel_id=1, source_target_pairs={{0,8},{8,16},{16,24},{24,32},{32,40},{40,48},{48,56},{56,64},{64,7... | collective-permute-start | bytes 1179656 | tf_op jit(solution)/shard_map/ppermute | solution.py:19
  105.1 17.9 %collective-permute-start.16 = (bf16[144,1536]{1,0:T(8,128)(2,1)S(1)}, bf16[144,1536]{1,0:T(8,128)(2,1)S(1)}, u32[]{:S(2)}, u32[]{:S(2)}) collective-permute-start(bf16[144,1536]{1,0:T(8,128)(2,1)S(1)} %collective-permute-done.12.refs_1_), channel_id=1, source_target_pairs={{0,8},{8,16},{16,24},{24,32},{32,40},{40,48},{48,56},{56,64},{64,7... | collective-permute-start | bytes 1327112 | tf_op jit(solution)/shard_map/ppermute | solution.py:19
  105.1 17.9 %collective-permute-start.17 = (bf16[144,1536]{1,0:T(8,128)(2,1)S(1)}, bf16[144,1536]{1,0:T(8,128)(2,1)S(1)}, u32[]{:S(2)}, u32[]{:S(2)}) collective-permute-start(bf16[144,1536]{1,0:T(8,128)(2,1)S(1)} %collective-permute-done.13.refs_3_), channel_id=1, source_target_pairs={{0,120},{8,0},{16,8},{24,16},{32,24},{40,32},{48,40},{56,48},{64,5... | collective-permute-start | bytes 1327112 | tf_op jit(solution)/shard_map/ppermute | solution.py:19
  112.4 17.9 %collective-permute-start.23 = (bf16[128,1536]{1,0:T(8,128)(2,1)S(1)}, bf16[128,1536]{1,0:T(8,128)(2,1)S(1)}, u32[]{:S(2)}, u32[]{:S(2)}) collective-permute-start(bf16[128,1536]{1,0:T(8,128)(2,1)S(1)} %collective-permute-done.19.refs_4_), channel_id=1, source_target_pairs={{0,120},{8,0},{16,8},{24,16},{32,24},{40,32},{48,40},{56,48},{64,5... | collective-permute-start | bytes 1179656 | tf_op jit(solution)/shard_map/ppermute | solution.py:19
  115.8 17.9 %collective-permute-start.22 = (bf16[128,1536]{1,0:T(8,128)(2,1)S(1)}, bf16[128,1536]{1,0:T(8,128)(2,1)S(1)}, u32[]{:S(2)}, u32[]{:S(2)}) collective-permute-start(bf16[128,1536]{1,0:T(8,128)(2,1)S(1)} %collective-permute-done.18.refs_2_), channel_id=1, source_target_pairs={{0,8},{8,16},{16,24},{24,32},{32,40},{40,48},{48,56},{56,64},{64,7... | collective-permute-start | bytes 1179656 | tf_op jit(solution)/shard_map/ppermute | solution.py:19
  123.0 17.9 %collective-permute-start.20 = (bf16[144,1536]{1,0:T(8,128)(2,1)S(1)}, bf16[144,1536]{1,0:T(8,128)(2,1)S(1)}, u32[]{:S(2)}, u32[]{:S(2)}) collective-permute-start(bf16[144,1536]{1,0:T(8,128)(2,1)S(1)} %collective-permute-done.16.refs_1_), channel_id=1, source_target_pairs={{0,8},{8,16},{16,24},{24,32},{32,40},{40,48},{48,56},{56,64},{64,7... | collective-permute-start | bytes 1327112 | tf_op jit(solution)/shard_map/ppermute | solution.py:19
  123.0 17.9 %collective-permute-start.21 = (bf16[144,1536]{1,0:T(8,128)(2,1)S(1)}, bf16[144,1536]{1,0:T(8,128)(2,1)S(1)}, u32[]{:S(2)}, u32[]{:S(2)}) collective-permute-start(bf16[144,1536]{1,0:T(8,128)(2,1)S(1)} %collective-permute-done.17.refs_3_), channel_id=1, source_target_pairs={{0,120},{8,0},{16,8},{24,16},{32,24},{40,32},{48,40},{56,48},{64,5... | collective-permute-start | bytes 1327112 | tf_op jit(solution)/shard_map/ppermute | solution.py:19
  130.3 17.9 %collective-permute-start.27 = (bf16[128,1536]{1,0:T(8,128)(2,1)S(1)}, bf16[128,1536]{1,0:T(8,128)(2,1)S(1)}, u32[]{:S(2)}, u32[]{:S(2)}) collective-permute-start(bf16[128,1536]{1,0:T(8,128)(2,1)S(1)} %collective-permute-done.23.refs_4_), channel_id=1, source_target_pairs={{0,120},{8,0},{16,8},{24,16},{32,24},{40,32},{48,40},{56,48},{64,5... | collective-permute-start | bytes 1179656 | tf_op jit(solution)/shard_map/ppermute | solution.py:19
  133.7 17.9 %collective-permute-start.26 = (bf16[128,1536]{1,0:T(8,128)(2,1)S(1)}, bf16[128,1536]{1,0:T(8,128)(2,1)S(1)}, u32[]{:S(2)}, u32[]{:S(2)}) collective-permute-start(bf16[128,1536]{1,0:T(8,128)(2,1)S(1)} %collective-permute-done.22.refs_2_), channel_id=1, source_target_pairs={{0,8},{8,16},{16,24},{24,32},{32,40},{40,48},{48,56},{56,64},{64,7... | collective-permute-start | bytes 1179656 | tf_op jit(solution)/shard_map/ppermute | solution.py:19
  140.9 17.9 %collective-permute-start.24 = (bf16[144,1536]{1,0:T(8,128)(2,1)S(1)}, bf16[144,1536]{1,0:T(8,128)(2,1)S(1)}, u32[]{:S(2)}, u32[]{:S(2)}) collective-permute-start(bf16[144,1536]{1,0:T(8,128)(2,1)S(1)} %collective-permute-done.20.refs_1_), channel_id=1, source_target_pairs={{0,8},{8,16},{16,24},{24,32},{32,40},{40,48},{48,56},{56,64},{64,7... | collective-permute-start | bytes 1327112 | tf_op jit(solution)/shard_map/ppermute | solution.py:19
  140.9 17.9 %collective-permute-start.25 = (bf16[144,1536]{1,0:T(8,128)(2,1)S(1)}, bf16[144,1536]{1,0:T(8,128)(2,1)S(1)}, u32[]{:S(2)}, u32[]{:S(2)}) collective-permute-start(bf16[144,1536]{1,0:T(8,128)(2,1)S(1)} %collective-permute-done.21.refs_3_), channel_id=1, source_target_pairs={{0,120},{8,0},{16,8},{24,16},{32,24},{40,32},{48,40},{56,48},{64,5... | collective-permute-start | bytes 1327112 | tf_op jit(solution)/shard_map/ppermute | solution.py:19
  148.2 17.9 %collective-permute-start.29 = (bf16[128,1536]{1,0:T(8,128)(2,1)S(1)}, bf16[128,1536]{1,0:T(8,128)(2,1)S(1)}, u32[]{:S(2)}, u32[]{:S(2)}) collective-permute-start(bf16[128,1536]{1,0:T(8,128)(2,1)S(1)} %collective-permute-done.27.refs_4_), channel_id=1, source_target_pairs={{0,120},{8,0},{16,8},{24,16},{32,24},{40,32},{48,40},{56,48},{64,5... | collective-permute-start | bytes 1179656 | tf_op jit(solution)/shard_map/ppermute | solution.py:19
  151.7 18.6 %collective-permute-start.31 = (bf16[128,1536]{1,0:T(8,128)(2,1)S(1)}, bf16[128,1536]{1,0:T(8,128)(2,1)S(1)}, u32[]{:S(2)}, u32[]{:S(2)}) collective-permute-start(bf16[128,1536]{1,0:T(8,128)(2,1)S(1)} %collective-permute-done.26.refs_2_), channel_id=1, source_target_pairs={{0,8},{8,16},{16,24},{24,32},{32,40},{40,48},{48,56},{56,64},{64,7... | collective-permute-start | bytes 1179656 | tf_op jit(solution)/shard_map/ppermute | solution.py:19
  158.8 18.1 %collective-permute-start.28 = (bf16[144,1536]{1,0:T(8,128)(2,1)S(1)}, bf16[144,1536]{1,0:T(8,128)(2,1)S(1)}, u32[]{:S(2)}, u32[]{:S(2)}) collective-permute-start(bf16[144,1536]{1,0:T(8,128)(2,1)S(1)} %collective-permute-done.24.refs_1_), channel_id=1, source_target_pairs={{0,8},{8,16},{16,24},{24,32},{32,40},{40,48},{48,56},{56,64},{64,7... | collective-permute-start | bytes 1327112 | tf_op jit(solution)/shard_map/ppermute | solution.py:19
  166.1 10.8 %collective-permute-start.30 = (bf16[128,1536]{1,0:T(8,128)(2,1)S(1)}, bf16[128,1536]{1,0:T(8,128)(2,1)S(1)}, u32[]{:S(2)}, u32[]{:S(2)}) collective-permute-start(bf16[128,1536]{1,0:T(8,128)(2,1)S(1)} %collective-permute-done.29.refs_4_), channel_id=1, source_target_pairs={{0,120},{8,0},{16,8},{24,16},{32,24},{40,32},{48,40},{56,48},{64,5... | collective-permute-start | bytes 1179656 | tf_op jit(solution)/shard_map/ppermute | solution.py:19
  176.9 5.6 %copy-start = (bf16[768,1536]{1,0:T(8,128)(2,1)S(1)}, bf16[768,1536]{1,0:T(8,128)(2,1)}, u32[]{:S(2)}) copy-start(bf16[768,1536]{1,0:T(8,128)(2,1)} %w_ref.5) | copy-start | bytes 7077892
  179.0 3.5 %collective-permute-start.32 = (bf16[256,768]{1,0:T(8,128)(2,1)S(1)}, bf16[256,768]{1,0:T(8,128)(2,1)S(1)}, u32[]{:S(2)}, u32[]{:S(2)}) collective-permute-start(bf16[256,768]{1,0:T(8,128)(2,1)S(1)} %attend_last.1.own_ref), channel_id=1, source_target_pairs={{0,1},{1,0},{2,3},{3,2},{4,5},{5,4},{6,7},{7,6},{8,9},{9,8},{10,11... | collective-permute-start | bytes 1179656 | tf_op jit(solution)/shard_map/ppermute | solution.py:19
  185.7 7.8 %collective-permute-start.33 = (bf16[64,1536]{1,0:T(8,128)(2,1)S(1)}, bf16[64,1536]{1,0:T(8,128)(2,1)S(1)}, u32[]{:S(2)}, u32[]{:S(2)}) collective-permute-start(bf16[64,1536]{1,0:T(8,128)(2,1)S(1)} %get-tuple-element.138), channel_id=1, source_target_pairs={{0,4},{2,6},{4,0},{6,2},{1,5},{3,7},{5,1},{7,3},{8,12},{10,14},{12... | collective-permute-start | bytes 589832 | tf_op jit(solution)/shard_map/ppermute | solution.py:19
  188.8 9.5 %collective-permute-start.34 = (bf16[64,1536]{1,0:T(8,128)(2,1)S(1)}, bf16[64,1536]{1,0:T(8,128)(2,1)S(1)}, u32[]{:S(2)}, u32[]{:S(2)}) collective-permute-start(bf16[64,1536]{1,0:T(8,128)(2,1)S(1)} %get-tuple-element.139), channel_id=1, source_target_pairs={{0,2},{2,4},{4,6},{6,0},{1,3},{3,5},{5,7},{7,1},{8,10},{10,12},{12... | collective-permute-start | bytes 589832 | tf_op jit(solution)/shard_map/ppermute | solution.py:19
  189.3 9.1 %collective-permute-start.35 = (bf16[64,1536]{1,0:T(8,128)(2,1)S(1)}, bf16[64,1536]{1,0:T(8,128)(2,1)S(1)}, u32[]{:S(2)}, u32[]{:S(2)}) collective-permute-start(bf16[64,1536]{1,0:T(8,128)(2,1)S(1)} %get-tuple-element.140), channel_id=1, source_target_pairs={{0,6},{2,0},{4,2},{6,4},{1,7},{3,1},{5,3},{7,5},{8,14},{10,8},{12,... | collective-permute-start | bytes 589832 | tf_op jit(solution)/shard_map/ppermute | solution.py:19
where the time goes:
time: 200 us; the launch traced here: 199 us
  waiting for transfers between devices  76.2 us (38%)
  starting transfers between devices  73.2 us (37%)
  Pallas kernels  47.4 us (24%)
    ppermute x36, waiting for transfers between devices, shifted(): return lax.ppermute(value, axis, [(i, (i + by) % n) for i in range(n)])  76.2 us
    ppermute x36, starting transfers between devices, shifted(): return lax.ppermute(value, axis, [(i, (i + by) % n) for i in range(n)])  73.2 us
    pallas_call x8, Pallas kernels, attend_step(): pl.pallas_call(functools.partial(step_kernel, len(blocks), first, used),...  24.6 us
    pallas_call x2, Pallas kernels, terms(): pl.pallas_call(terms_kernel, grid=(count * tiles,), in_specs=[whole, whol...  9.61 us
  transfers between devices with their start and end apart: 36, of which 19 were waited for; matrix products, arithmetic and copies ran while one was open for 0% of the time, Pallas kernels for 14%

commit v1 on v0

--- a/solution.py
+++ b/solution.py
@@ -110,23 +110,23 @@
     )
 
 
-def norm_kernel(c_ref, x_ref, mod_ref, own_ref, other_ref):
+def norm_kernel(c_ref, x_ref, mod_ref, out_ref):
     x = x_ref[...].astype(jnp.float32)
     center = x - jnp.mean(x, axis=-1, keepdims=True)
     normed = center * lax.rsqrt(jnp.mean(center * center, axis=-1, keepdims=True) + EPS)
     half = normed.shape[1] // 2
     mine = jnp.where(c_ref[0] == 0, normed[:, :half], normed[:, half:])
-    for branch, out_ref in ((c_ref[0], own_ref), (1 - c_ref[0], other_ref)):
+    for i, branch in enumerate((c_ref[0], 1 - c_ref[0])):
         at = pl.ds(branch, 1)
-        out_ref[...] = (mine * (1.0 + mod_ref[1, at, :]) + mod_ref[0, at, :]).astype(jnp.bfloat16)
+        out_ref[i] = (mine * (1.0 + mod_ref[1, at, :]) + mod_ref[0, at, :]).astype(jnp.bfloat16)
 
 
 def modulate(branch, latent, mod):
     rows, width = latent.shape
     half = width // 2
     step = 64
-    shape = jax.ShapeDtypeStruct((rows, half), jnp.bfloat16)
-    spec = pl.BlockSpec((step, half), lambda i, c: (i, 0))
+    shape = jax.ShapeDtypeStruct((2, rows, half), jnp.bfloat16)
+    spec = pl.BlockSpec((2, step, half), lambda i, c: (0, i, 0))
     return pl.pallas_call(
         norm_kernel,
         grid_spec=pltpu.PrefetchScalarGridSpec(
@@ -136,33 +136,34 @@
                 pl.BlockSpec((step, width), lambda i, c: (i, 0)),
                 pl.BlockSpec((*mod.shape[:2], half), lambda i, c: (0, 0, c[0])),
             ],
-            out_specs=(spec, spec),
-        ),
-        out_shape=(shape, shape),
+            out_specs=spec,
+        ),
+        out_shape=shape,
         cost_estimate=pl.CostEstimate(flops=3000000000, bytes_accessed=4 * rows * width, transcendentals=0),
         compiler_params=pltpu.CompilerParams(vmem_limit_bytes=8 << 20),
         name="norm",
     )(branch, latent, mod)
 
 
-def terms_kernel(own_ref, other_ref, w_ref, *refs):
+def terms_kernel(both_ref, w_ref, *refs):
     mine_ref, theirs_ref = refs[-2:]
-    w = w_ref[0]
-    theirs_ref[...] = dot(other_ref[...], w).astype(jnp.bfloat16)
-    mine_ref[...] = dot(own_ref[...], w)
-
-
-def terms(own, other, w_qkv, first, count, after=()):
-    rows, half = own.shape
+    rows, half = both_ref.shape[1:]
+    y = dot(both_ref[...].reshape(2 * rows, half), w_ref[0])
+    mine_ref[...] = y[:rows]
+    theirs_ref[...] = y[rows:].astype(jnp.bfloat16)
+
+
+def terms(both, w_qkv, first, count, after=()):
+    rows, half = both.shape[1:]
     width = w_qkv.shape[2]
     tile = 2 * HEAD_DIM
     tiles = width // tile
-    whole = pl.BlockSpec((rows, half), lambda n: (0, 0))
+    whole = pl.BlockSpec(both.shape, lambda n: (0, 0, 0))
     part = pl.BlockSpec((rows, tile), lambda n: (0, n))
     return pl.pallas_call(
         terms_kernel,
         grid=(count * tiles,),
-        in_specs=[whole, whole, pl.BlockSpec((1, half, tile), lambda n: (first + n // tiles, 0, n % tiles))]
+        in_specs=[whole, pl.BlockSpec((1, half, tile), lambda n: (first + n // tiles, 0, n % tiles))]
         + [pl.BlockSpec((16, HEAD_DIM), lambda n: (0, 0)) for _ in after],
         out_specs=(part, part),
         out_shape=(
@@ -174,7 +175,7 @@
         ),
         compiler_params=pltpu.CompilerParams(vmem_limit_bytes=16 << 20),
         name="terms",
-    )(own, other, w_qkv, *after)
+    )(both, w_qkv, *after)
 
 
 def over_heads(width, body, each=1):
@@ -422,15 +423,12 @@
     latent, z, x, branch = lax.optimization_barrier((latent, z[None], x[None], c[None]))
     half = n_seq // 2
     cut = rows // 2
-    latent, modulation, w_qkv = (
-        pltpu.with_memory_space_constraint(a, pltpu.MemorySpace.HBM) for a in (latent, modulation, w_qkv)
-    )
-    own, other = modulate(branch, latent, modulation)
-    kv_mine, kv_theirs = terms(own, other, w_qkv, 1, 2)
+    both = modulate(branch, latent, modulation)
+    kv_mine, kv_theirs = terms(both, w_qkv, 1, 2)
     kv_got = shifted(kv_theirs, "cfg", 1)
     tables = rotary_tables(positions)
     first, second = keys_values(kv_mine, kv_got, text_kv, norm_gains, tables, cut)
-    q_mine, q_theirs = terms(own, other, w_qkv, 0, 1, (second,))
+    q_mine, q_theirs = terms(both, w_qkv, 0, 1, (second,))
     queries = query_rows(q_mine, shifted(q_theirs, "cfg", 1), norm_gains, tables)
     texts, offsets, state = [], [], None
     ahead = behind = (first, second)

time: 200 us -> 197 us (0.985)
  Pallas kernels: 47.4 us -> 41.6 us
  local copies, waits for them, and re-layouts: 0.04 us -> 3.61 us
    unnamed x12 -> x18, local copies, waits for them, and re-layouts: 0.04 us -> 3.61 us
    pallas_call x2, Pallas kernels: 9.61 us -> 6.12 us  [terms(): pl.pallas_call(terms_kernel, grid=(count * tiles,), in_specs=[whole, pl.B...]
where the time goes in v1:
time: 197 us
  waiting for transfers between devices  76.2 us (39%)
  starting transfers between devices  73.2 us (37%)
  Pallas kernels  41.6 us (21%)
  local copies, waits for them, and re-layouts  3.61 us (2%)
    ppermute x36, waiting for transfers between devices, shifted(): return lax.ppermute(value, axis, [(i, (i + by) % n) for i in range(n)])  76.2 us
    ppermute x36, starting transfers between devices, shifted(): return lax.ppermute(value, axis, [(i, (i + by) % n) for i in range(n)])  73.2 us
    pallas_call x8, Pallas kernels, attend_step(): pl.pallas_call(functools.partial(step_kernel, len(blocks), first, used),...  24.6 us
    pallas_call x2, Pallas kernels, terms(): pl.pallas_call(terms_kernel, grid=(count * tiles,), in_specs=[whole, pl.B...  6.12 us
  transfers between devices with their start and end apart: 36, of which 19 were waited for; matrix products, arithmetic and copies ran while one was open for 0% of the time, Pallas kernels for 14%

profile of v1, /device:TPU:33, one launch (start us, length us, event | category | flops | bytes accessed | tf_op | source)
XLA Modules:
  0.0 196.9 jit_solution(15593347869340118121)
XLA Ops:
  0.0 1.4 copy-done.2
  1.4 0.9 copy-done.3
  2.3 1.7 norm.1.both_ref
  4.0 1.3 copy-done
  5.3 4.0 %terms.2 = (f32[256,1536]{1,0:T(8,128)S(1)}, bf16[256,1536]{1,0:T(8,128)(2,1)S(1)}) custom-call(bf16[2,256,1536]{2,1,0:T(8,128)(2,1)S(1)} %norm.1.both_ref, bf16[3,1536,768]{2,1,0:T(8,128)(2,1)S(1)} %copy-done), custom_call_target="tpu_custom_call" | custom-call | flops 2415919104 | bytes 4718592 | tf_op jit(solution)/shard_map/terms/pallas_call | solution.py:163
  9.4 0.0 copy-start.4
  9.4 0.0 copy-start.6
  9.4 20.5 %collective-permute-start = (bf16[256,1536]{1,0:T(8,128)(2,1)S(1)}, bf16[256,1536]{1,0:T(8,128)(2,1)S(1)}, u32[]{:S(2)}, u32[]{:S(2)}) collective-permute-start(bf16[256,1536]{1,0:T(8,128)(2,1)S(1)} %get-tuple-element.76), channel_id=1, source_target_pairs={{0,1},{1,0},{2,3},{3,2},{4,5},{5,4},{6,7},{7,6},{8,9},{9,8},{10,11... | collective-permute-start | bytes 2359304 | tf_op jit(solution)/shard_map/ppermute | solution.py:19
  29.9 0.8 tables.1.tab_ref
  30.7 1.1 collective-permute-done.got_ref
  31.8 2.1 %keys.1 = (bf16[144,1536]{1,0:T(8,128)(2,1)S(1)}, bf16[128,1536]{1,0:T(8,128)(2,1)S(1)}) custom-call(f32[256,1536]{1,0:T(8,128)S(1)} %get-tuple-element.75.mine_ref, bf16[256,1536]{1,0:T(8,128)(2,1)S(1)} %collective-permute-done.got_ref, bf16[1,2,16,768]{3,2,1,0:T(8,128)(2,1)S(1)} %copy-done.4, f32[2,128]{1,0:T(2,128)S(1)} %copy-done.6, ...), custom_call_target="tpu_custom_call" | custom-call | flops 1000000000 | bytes 3145728 | tf_op jit(solution)/shard_map/keys/pallas_call | solution.py:217
  33.9 2.1 %terms.3 = (f32[256,768]{1,0:T(8,128)S(1)}, bf16[256,768]{1,0:T(8,128)(2,1)S(1)}) custom-call(bf16[2,256,1536]{2,1,0:T(8,128)(2,1)S(1)} %norm.1.both_ref, bf16[3,1536,768]{2,1,0:T(8,128)(2,1)S(1)} %copy-done, bf16[128,1536]{1,0:T(8,128)(2,1)S(1)} %get-tuple-element.77.refs_0_.refs_2_), custom_call_target="tpu_custom_call" | custom-call | flops 1207959552 | bytes 2359296 | tf_op jit(solution)/shard_map/terms/pallas_call | solution.py:163
  36.0 0.5 collective-permute-start.1
  36.5 3.1 %collective-permute-start.3 = (bf16[144,1536]{1,0:T(8,128)(2,1)S(1)}, bf16[144,1536]{1,0:T(8,128)(2,1)S(1)}, u32[]{:S(2)}, u32[]{:S(2)}) collective-permute-start(bf16[144,1536]{1,0:T(8,128)(2,1)S(1)} %get-tuple-element.80.refs_1_), channel_id=1, source_target_pairs={{0,120},{8,0},{16,8},{24,16},{32,24},{40,32},{48,40},{56,48},{64,5... | collective-permute-start | bytes 1327112 | tf_op jit(solution)/shard_map/ppermute | solution.py:19
  39.6 2.7 %collective-permute-start.7 = (bf16[128,1536]{1,0:T(8,128)(2,1)S(1)}, bf16[128,1536]{1,0:T(8,128)(2,1)S(1)}, u32[]{:S(2)}, u32[]{:S(2)}) collective-permute-start(bf16[128,1536]{1,0:T(8,128)(2,1)S(1)} %get-tuple-element.77.refs_0_.refs_2_), channel_id=1, source_target_pairs={{0,120},{8,0},{16,8},{24,16},{32,24},{40,32},{48,40},{56,48},{64,5... | collective-permute-start | bytes 1179656 | tf_op jit(solution)/shard_map/ppermute | solution.py:19
  42.3 1.9 queries.1.refs_0_.q_ref
  44.2 2.0 %attend.8 = (f32[256,768]{1,0:T(8,128)S(1)}, f32[256,768]{1,0:T(8,128)S(1)}, bf16[16,1536]{1,0:T(8,128)(2,1)S(1)}) custom-call(bf16[256,768]{1,0:T(8,128)(2,1)S(1)} %queries.1.refs_0_.q_ref, bf16[144,1536]{1,0:T(8,128)(2,1)S(1)} %get-tuple-element.80.refs_1_, bf16[128,1536]{1,0:T(8,128)(2,1)S(1)} %get-tuple-element.77.refs_0_.refs_2_), custom_call_target="tpu_custom_call" | custom-call | flops 805306368 | bytes 786432 | tf_op jit(solution)/shard_map/attend/pallas_call | solution.py:305
  46.2 3.8 %collective-permute-done.2.refs_1_ = bf16[144,1536]{1,0:T(8,128)(2,1)S(1)} collective-permute-done((bf16[144,1536]{1,0:T(8,128)(2,1)S(1)}, bf16[144,1536]{1,0:T(8,128)(2,1)S(1)}, u32[]{:S(2)}, u32[]{:S(2)}) %collective-permute-start.2) | collective-permute-done | bytes 442400 | tf_op jit(solution)/shard_map/ppermute | solution.py:19
  50.0 2.7 %collective-permute-start.5 = (bf16[144,1536]{1,0:T(8,128)(2,1)S(1)}, bf16[144,1536]{1,0:T(8,128)(2,1)S(1)}, u32[]{:S(2)}, u32[]{:S(2)}) collective-permute-start(bf16[144,1536]{1,0:T(8,128)(2,1)S(1)} %collective-permute-done.3.refs_3_), channel_id=1, source_target_pairs={{0,120},{8,0},{16,8},{24,16},{32,24},{40,32},{48,40},{56,48},{64,5... | collective-permute-start | bytes 1327112 | tf_op jit(solution)/shard_map/ppermute | solution.py:19
  52.7 5.7 %collective-permute-done.6.refs_2_ = bf16[128,1536]{1,0:T(8,128)(2,1)S(1)} collective-permute-done((bf16[128,1536]{1,0:T(8,128)(2,1)S(1)}, bf16[128,1536]{1,0:T(8,128)(2,1)S(1)}, u32[]{:S(2)}, u32[]{:S(2)}) %collective-permute-start.6) | collective-permute-done | bytes 393248 | tf_op jit(solution)/shard_map/ppermute | solution.py:19
  58.4 2.7 %collective-permute-start.11 = (bf16[128,1536]{1,0:T(8,128)(2,1)S(1)}, bf16[128,1536]{1,0:T(8,128)(2,1)S(1)}, u32[]{:S(2)}, u32[]{:S(2)}) collective-permute-start(bf16[128,1536]{1,0:T(8,128)(2,1)S(1)} %collective-permute-done.7.refs_4_), channel_id=1, source_target_pairs={{0,120},{8,0},{16,8},{24,16},{32,24},{40,32},{48,40},{56,48},{64,5... | collective-permute-start | bytes 1179656 | tf_op jit(solution)/shard_map/ppermute | solution.py:19
  61.1 3.2 %attend.9 = (f32[256,768]{1,0:T(8,128)S(1)}, f32[256,768]{1,0:T(8,128)S(1)}, bf16[32,1536]{1,0:T(8,128)(2,1)S(1)}) custom-call(bf16[256,768]{1,0:T(8,128)(2,1)S(1)} %queries.1.refs_0_.q_ref, bf16[144,1536]{1,0:T(8,128)(2,1)S(1)} %collective-permute-done.2.refs_1_, ...), custom_call_target="tpu_custom_call", output_to_operand_aliasing={{0}: (5, {}), {1}: (6, {})} | custom-call | flops 1610612736 | bytes 786432 | tf_op jit(solution)/shard_map/attend/pallas_call | solution.py:305
  64.3 3.6 %collective-permute-done.4.refs_1_ = bf16[144,1536]{1,0:T(8,128)(2,1)S(1)} collective-permute-done((bf16[144,1536]{1,0:T(8,128)(2,1)S(1)}, bf16[144,1536]{1,0:T(8,128)(2,1)S(1)}, u32[]{:S(2)}, u32[]{:S(2)}) %collective-permute-start.4) | collective-permute-done | bytes 442400 | tf_op jit(solution)/shard_map/ppermute | solution.py:19
  67.9 2.7 %collective-permute-start.9 = (bf16[144,1536]{1,0:T(8,128)(2,1)S(1)}, bf16[144,1536]{1,0:T(8,128)(2,1)S(1)}, u32[]{:S(2)}, u32[]{:S(2)}) collective-permute-start(bf16[144,1536]{1,0:T(8,128)(2,1)S(1)} %collective-permute-done.5.refs_3_), channel_id=1, source_target_pairs={{0,120},{8,0},{16,8},{24,16},{32,24},{40,32},{48,40},{56,48},{64,5... | collective-permute-start | bytes 1327112 | tf_op jit(solution)/shard_map/ppermute | solution.py:19
  70.6 5.7 %collective-permute-done.10.refs_2_ = bf16[128,1536]{1,0:T(8,128)(2,1)S(1)} collective-permute-done((bf16[128,1536]{1,0:T(8,128)(2,1)S(1)}, bf16[128,1536]{1,0:T(8,128)(2,1)S(1)}, u32[]{:S(2)}, u32[]{:S(2)}) %collective-permute-start.10) | collective-permute-done | bytes 393248 | tf_op jit(solution)/shard_map/ppermute | solution.py:19
  76.3 0.0 collective-permute-start.14
  76.3 2.7 %collective-permute-start.15 = (bf16[128,1536]{1,0:T(8,128)(2,1)S(1)}, bf16[128,1536]{1,0:T(8,128)(2,1)S(1)}, u32[]{:S(2)}, u32[]{:S(2)}) collective-permute-start(bf16[128,1536]{1,0:T(8,128)(2,1)S(1)} %collective-permute-done.11.refs_4_), channel_id=1, source_target_pairs={{0,120},{8,0},{16,8},{24,16},{32,24},{40,32},{48,40},{56,48},{64,5... | collective-permute-start | bytes 1179656 | tf_op jit(solution)/shard_map/ppermute | solution.py:19
  79.0 3.2 %attend.10 = (f32[256,768]{1,0:T(8,128)S(1)}, f32[256,768]{1,0:T(8,128)S(1)}, bf16[32,1536]{1,0:T(8,128)(2,1)S(1)}) custom-call(bf16[256,768]{1,0:T(8,128)(2,1)S(1)} %queries.1.refs_0_.q_ref, bf16[144,1536]{1,0:T(8,128)(2,1)S(1)} %collective-permute-done.4.refs_1_, ...), custom_call_target="tpu_custom_call", output_to_operand_aliasing={{0}: (5, {}), {1}: (6, {})} | custom-call | flops 1610612736 | bytes 786432 | tf_op jit(solution)/shard_map/attend/pallas_call | solution.py:305
  82.2 3.6 %collective-permute-done.8.refs_1_ = bf16[144,1536]{1,0:T(8,128)(2,1)S(1)} collective-permute-done((bf16[144,1536]{1,0:T(8,128)(2,1)S(1)}, bf16[144,1536]{1,0:T(8,128)(2,1)S(1)}, u32[]{:S(2)}, u32[]{:S(2)}) %collective-permute-start.8) | collective-permute-done | bytes 442400 | tf_op jit(solution)/shard_map/ppermute | solution.py:19
  85.8 2.7 %collective-permute-start.13 = (bf16[144,1536]{1,0:T(8,128)(2,1)S(1)}, bf16[144,1536]{1,0:T(8,128)(2,1)S(1)}, u32[]{:S(2)}, u32[]{:S(2)}) collective-permute-start(bf16[144,1536]{1,0:T(8,128)(2,1)S(1)} %collective-permute-done.9.refs_3_), channel_id=1, source_target_pairs={{0,120},{8,0},{16,8},{24,16},{32,24},{40,32},{48,40},{56,48},{64,5... | collective-permute-start | bytes 1327112 | tf_op jit(solution)/shard_map/ppermute | solution.py:19
  88.5 4.6 %collective-permute-done.15.refs_4_ = bf16[128,1536]{1,0:T(8,128)(2,1)S(1)} collective-permute-done((bf16[128,1536]{1,0:T(8,128)(2,1)S(1)}, bf16[128,1536]{1,0:T(8,128)(2,1)S(1)}, u32[]{:S(2)}, u32[]{:S(2)}) %collective-permute-start.15) | collective-permute-done | bytes 393248 | tf_op jit(solution)/shard_map/ppermute | solution.py:19
  93.1 3.4 %collective-permute-start.19 = (bf16[128,1536]{1,0:T(8,128)(2,1)S(1)}, bf16[128,1536]{1,0:T(8,128)(2,1)S(1)}, u32[]{:S(2)}, u32[]{:S(2)}) collective-permute-start(bf16[128,1536]{1,0:T(8,128)(2,1)S(1)} %collective-permute-done.15.refs_4_), channel_id=1, source_target_pairs={{0,120},{8,0},{16,8},{24,16},{32,24},{40,32},{48,40},{56,48},{64,5... | collective-permute-start | bytes 1179656 | tf_op jit(solution)/shard_map/ppermute | solution.py:19
  96.5 3.2 %attend.11 = (f32[256,768]{1,0:T(8,128)S(1)}, f32[256,768]{1,0:T(8,128)S(1)}, bf16[32,1536]{1,0:T(8,128)(2,1)S(1)}) custom-call(bf16[256,768]{1,0:T(8,128)(2,1)S(1)} %queries.1.refs_0_.q_ref, bf16[144,1536]{1,0:T(8,128)(2,1)S(1)} %collective-permute-done.8.refs_1_, ...), custom_call_target="tpu_custom_call", output_to_operand_aliasing={{0}: (5, {}), {1}: (6, {})} | custom-call | flops 1610612736 | bytes 786432 | tf_op jit(solution)/shard_map/attend/pallas_call | solution.py:305
  99.7 4.0 %collective-permute-done.12.refs_1_ = bf16[144,1536]{1,0:T(8,128)(2,1)S(1)} collective-permute-done((bf16[144,1536]{1,0:T(8,128)(2,1)S(1)}, bf16[144,1536]{1,0:T(8,128)(2,1)S(1)}, u32[]{:S(2)}, u32[]{:S(2)}) %collective-permute-start.12) | collective-permute-done | bytes 442400 | tf_op jit(solution)/shard_map/ppermute | solution.py:19
  103.7 2.7 %collective-permute-start.17 = (bf16[144,1536]{1,0:T(8,128)(2,1)S(1)}, bf16[144,1536]{1,0:T(8,128)(2,1)S(1)}, u32[]{:S(2)}, u32[]{:S(2)}) collective-permute-start(bf16[144,1536]{1,0:T(8,128)(2,1)S(1)} %collective-permute-done.13.refs_3_), channel_id=1, source_target_pairs={{0,120},{8,0},{16,8},{24,16},{32,24},{40,32},{48,40},{56,48},{64,5... | collective-permute-start | bytes 1327112 | tf_op jit(solution)/shard_map/ppermute | solution.py:19
  106.4 4.6 %collective-permute-done.19.refs_4_ = bf16[128,1536]{1,0:T(8,128)(2,1)S(1)} collective-permute-done((bf16[128,1536]{1,0:T(8,128)(2,1)S(1)}, bf16[128,1536]{1,0:T(8,128)(2,1)S(1)}, u32[]{:S(2)}, u32[]{:S(2)}) %collective-permute-start.19) | collective-permute-done | bytes 393248 | tf_op jit(solution)/shard_map/ppermute | solution.py:19
  111.0 3.4 %collective-permute-start.23 = (bf16[128,1536]{1,0:T(8,128)(2,1)S(1)}, bf16[128,1536]{1,0:T(8,128)(2,1)S(1)}, u32[]{:S(2)}, u32[]{:S(2)}) collective-permute-start(bf16[128,1536]{1,0:T(8,128)(2,1)S(1)} %collective-permute-done.19.refs_4_), channel_id=1, source_target_pairs={{0,120},{8,0},{16,8},{24,16},{32,24},{40,32},{48,40},{56,48},{64,5... | collective-permute-start | bytes 1179656 | tf_op jit(solution)/shard_map/ppermute | solution.py:19
  114.4 3.2 %attend.12 = (f32[256,768]{1,0:T(8,128)S(1)}, f32[256,768]{1,0:T(8,128)S(1)}, bf16[32,1536]{1,0:T(8,128)(2,1)S(1)}) custom-call(bf16[256,768]{1,0:T(8,128)(2,1)S(1)} %queries.1.refs_0_.q_ref, bf16[144,1536]{1,0:T(8,128)(2,1)S(1)} %collective-permute-done.12.refs_1_, ...), custom_call_target="tpu_custom_call", output_to_operand_aliasing={{0}: (5, {}), {1}: (6, {})} | custom-call | flops 1610612736 | bytes 786432 | tf_op jit(solution)/shard_map/attend/pallas_call | solution.py:305
  117.6 4.0 %collective-permute-done.16.refs_1_ = bf16[144,1536]{1,0:T(8,128)(2,1)S(1)} collective-permute-done((bf16[144,1536]{1,0:T(8,128)(2,1)S(1)}, bf16[144,1536]{1,0:T(8,128)(2,1)S(1)}, u32[]{:S(2)}, u32[]{:S(2)}) %collective-permute-start.16) | collective-permute-done | bytes 442400 | tf_op jit(solution)/shard_map/ppermute | solution.py:19
  121.6 2.7 %collective-permute-start.21 = (bf16[144,1536]{1,0:T(8,128)(2,1)S(1)}, bf16[144,1536]{1,0:T(8,128)(2,1)S(1)}, u32[]{:S(2)}, u32[]{:S(2)}) collective-permute-start(bf16[144,1536]{1,0:T(8,128)(2,1)S(1)} %collective-permute-done.17.refs_3_), channel_id=1, source_target_pairs={{0,120},{8,0},{16,8},{24,16},{32,24},{40,32},{48,40},{56,48},{64,5... | collective-permute-start | bytes 1327112 | tf_op jit(solution)/shard_map/ppermute | solution.py:19
  124.3 4.6 %collective-permute-done.23.refs_4_ = bf16[128,1536]{1,0:T(8,128)(2,1)S(1)} collective-permute-done((bf16[128,1536]{1,0:T(8,128)(2,1)S(1)}, bf16[128,1536]{1,0:T(8,128)(2,1)S(1)}, u32[]{:S(2)}, u32[]{:S(2)}) %collective-permute-start.23) | collective-permute-done | bytes 393248 | tf_op jit(solution)/shard_map/ppermute | solution.py:19
  128.9 3.4 %collective-permute-start.27 = (bf16[128,1536]{1,0:T(8,128)(2,1)S(1)}, bf16[128,1536]{1,0:T(8,128)(2,1)S(1)}, u32[]{:S(2)}, u32[]{:S(2)}) collective-permute-start(bf16[128,1536]{1,0:T(8,128)(2,1)S(1)} %collective-permute-done.23.refs_4_), channel_id=1, source_target_pairs={{0,120},{8,0},{16,8},{24,16},{32,24},{40,32},{48,40},{56,48},{64,5... | collective-permute-start | bytes 1179656 | tf_op jit(solution)/shard_map/ppermute | solution.py:19
  132.3 3.2 %attend.13 = (f32[256,768]{1,0:T(8,128)S(1)}, f32[256,768]{1,0:T(8,128)S(1)}, bf16[32,1536]{1,0:T(8,128)(2,1)S(1)}) custom-call(bf16[256,768]{1,0:T(8,128)(2,1)S(1)} %queries.1.refs_0_.q_ref, bf16[144,1536]{1,0:T(8,128)(2,1)S(1)} %collective-permute-done.16.refs_1_, ...), custom_call_target="tpu_custom_call", output_to_operand_aliasing={{0}: (5, {}), {1}: (6, {})} | custom-call | flops 1610612736 | bytes 786432 | tf_op jit(solution)/shard_map/attend/pallas_call | solution.py:305
  135.6 4.0 %collective-permute-done.20.refs_1_ = bf16[144,1536]{1,0:T(8,128)(2,1)S(1)} collective-permute-done((bf16[144,1536]{1,0:T(8,128)(2,1)S(1)}, bf16[144,1536]{1,0:T(8,128)(2,1)S(1)}, u32[]{:S(2)}, u32[]{:S(2)}) %collective-permute-start.20) | collective-permute-done | bytes 442400 | tf_op jit(solution)/shard_map/ppermute | solution.py:19
  139.5 0.0 collective-permute-start.24
  139.5 2.7 %collective-permute-start.25 = (bf16[144,1536]{1,0:T(8,128)(2,1)S(1)}, bf16[144,1536]{1,0:T(8,128)(2,1)S(1)}, u32[]{:S(2)}, u32[]{:S(2)}) collective-permute-start(bf16[144,1536]{1,0:T(8,128)(2,1)S(1)} %collective-permute-done.21.refs_3_), channel_id=1, source_target_pairs={{0,120},{8,0},{16,8},{24,16},{32,24},{40,32},{48,40},{56,48},{64,5... | collective-permute-start | bytes 1327112 | tf_op jit(solution)/shard_map/ppermute | solution.py:19
  142.2 4.6 %collective-permute-done.27.refs_4_ = bf16[128,1536]{1,0:T(8,128)(2,1)S(1)} collective-permute-done((bf16[128,1536]{1,0:T(8,128)(2,1)S(1)}, bf16[128,1536]{1,0:T(8,128)(2,1)S(1)}, u32[]{:S(2)}, u32[]{:S(2)}) %collective-permute-start.27) | collective-permute-done | bytes 393248 | tf_op jit(solution)/shard_map/ppermute | solution.py:19
  146.8 3.4 %collective-permute-start.29 = (bf16[128,1536]{1,0:T(8,128)(2,1)S(1)}, bf16[128,1536]{1,0:T(8,128)(2,1)S(1)}, u32[]{:S(2)}, u32[]{:S(2)}) collective-permute-start(bf16[128,1536]{1,0:T(8,128)(2,1)S(1)} %collective-permute-done.27.refs_4_), channel_id=1, source_target_pairs={{0,120},{8,0},{16,8},{24,16},{32,24},{40,32},{48,40},{56,48},{64,5... | collective-permute-start | bytes 1179656 | tf_op jit(solution)/shard_map/ppermute | solution.py:19
  150.2 3.2 %attend.14 = (f32[256,768]{1,0:T(8,128)S(1)}, f32[256,768]{1,0:T(8,128)S(1)}, bf16[32,1536]{1,0:T(8,128)(2,1)S(1)}) custom-call(bf16[256,768]{1,0:T(8,128)(2,1)S(1)} %queries.1.refs_0_.q_ref, bf16[144,1536]{1,0:T(8,128)(2,1)S(1)} %collective-permute-done.20.refs_1_, ...), custom_call_target="tpu_custom_call", output_to_operand_aliasing={{0}: (5, {}), {1}: (6, {})} | custom-call | flops 1610612736 | bytes 786432 | tf_op jit(solution)/shard_map/attend/pallas_call | solution.py:305
  153.5 4.0 %collective-permute-done.24.refs_1_ = bf16[144,1536]{1,0:T(8,128)(2,1)S(1)} collective-permute-done((bf16[144,1536]{1,0:T(8,128)(2,1)S(1)}, bf16[144,1536]{1,0:T(8,128)(2,1)S(1)}, u32[]{:S(2)}, u32[]{:S(2)}) %collective-permute-start.24) | collective-permute-done | bytes 442400 | tf_op jit(solution)/shard_map/ppermute | solution.py:19
  157.4 7.3 %collective-permute-done.29.refs_4_ = bf16[128,1536]{1,0:T(8,128)(2,1)S(1)} collective-permute-done((bf16[128,1536]{1,0:T(8,128)(2,1)S(1)}, bf16[128,1536]{1,0:T(8,128)(2,1)S(1)}, u32[]{:S(2)}, u32[]{:S(2)}) %collective-permute-start.29) | collective-permute-done | bytes 393248 | tf_op jit(solution)/shard_map/ppermute | solution.py:19
  164.7 3.4 %collective-permute-start.30 = (bf16[128,1536]{1,0:T(8,128)(2,1)S(1)}, bf16[128,1536]{1,0:T(8,128)(2,1)S(1)}, u32[]{:S(2)}, u32[]{:S(2)}) collective-permute-start(bf16[128,1536]{1,0:T(8,128)(2,1)S(1)} %collective-permute-done.29.refs_4_), channel_id=1, source_target_pairs={{0,120},{8,0},{16,8},{24,16},{32,24},{40,32},{48,40},{56,48},{64,5... | collective-permute-start | bytes 1179656 | tf_op jit(solution)/shard_map/ppermute | solution.py:19
  168.8 3.2 %attend.15 = (f32[256,768]{1,0:T(8,128)S(1)}, f32[256,768]{1,0:T(8,128)S(1)}, bf16[32,1536]{1,0:T(8,128)(2,1)S(1)}) custom-call(bf16[256,768]{1,0:T(8,128)(2,1)S(1)} %queries.1.refs_0_.q_ref, bf16[144,1536]{1,0:T(8,128)(2,1)S(1)} %collective-permute-done.24.refs_1_, ...), custom_call_target="tpu_custom_call", output_to_operand_aliasing={{0}: (5, {}), {1}: (6, {})} | custom-call | flops 1610612736 | bytes 786432 | tf_op jit(solution)/shard_map/attend/pallas_call | solution.py:305
  172.0 3.4 %collective-permute-done.30.second_ref = bf16[128,1536]{1,0:T(8,128)(2,1)S(1)} collective-permute-done((bf16[128,1536]{1,0:T(8,128)(2,1)S(1)}, bf16[128,1536]{1,0:T(8,128)(2,1)S(1)}, u32[]{:S(2)}, u32[]{:S(2)}) %collective-permute-start.30) | collective-permute-done | bytes 393248 | tf_op jit(solution)/shard_map/ppermute | solution.py:19
  175.5 2.1 %attend_last.1.own_ref = bf16[256,768]{1,0:T(8,128)(2,1)S(1)} custom-call(s32[1]{0:T(128)} %bitcast.z_ref, s32[1]{0:T(128)S(6)} %copy.40.length_ref, bf16[256,768]{1,0:T(8,128)(2,1)S(1)} %queries.1.refs_0_.q_ref, bf16[144,1536]{1,0:T(8,128)(2,1)S(1)} %collective-permute-done.28.first_ref, bf16[128,1536]{1,0:T(8,128)(2,1)S(1)} %collective-permute-done.30.second_ref, ...), custom_call_target="tpu_custom_call" | custom-call | flops 1610612736 | bytes 1572864 | tf_op jit(solution)/shard_map/attend_last/pallas_call | solution.py:355
  177.6 2.1 %collective-permute-start.32 = (bf16[256,768]{1,0:T(8,128)(2,1)S(1)}, bf16[256,768]{1,0:T(8,128)(2,1)S(1)}, u32[]{:S(2)}, u32[]{:S(2)}) collective-permute-start(bf16[256,768]{1,0:T(8,128)(2,1)S(1)} %attend_last.1.own_ref), channel_id=1, source_target_pairs={{0,1},{1,0},{2,3},{3,2},{4,5},{5,4},{6,7},{7,6},{8,9},{9,8},{10,11... | collective-permute-start | bytes 1179656 | tf_op jit(solution)/shard_map/ppermute | solution.py:19
  180.4 0.7 collective-permute-done.32.other_ref
  181.1 2.3 %out.1 = (f32[64,1536]{1,0:T(8,128)S(1)}, bf16[64,1536]{1,0:T(8,128)(2,1)S(1)}, bf16[64,1536]{1,0:T(8,128)(2,1)S(1)}, bf16[64,1536]{1,0:T(8,128)(2,1)S(1)}) custom-call(s32[1]{0:T(128)} %bitcast.1.x_ref, s32[1]{0:T(128)} %bitcast.2.c_ref, f32[1]{0:T(128)S(6)} %copy.41.strength_ref, bf16[256,768]{1,0:T(8,128)(2,1)S(1)} %attend_last.1.own_ref, ...), custom_call_target="tpu_custom_call" | custom-call | flops 1207959552 | bytes 2359296 | tf_op jit(solution)/shard_map/out/pallas_call | solution.py:403
  183.4 3.1 %collective-permute-start.33 = (bf16[64,1536]{1,0:T(8,128)(2,1)S(1)}, bf16[64,1536]{1,0:T(8,128)(2,1)S(1)}, u32[]{:S(2)}, u32[]{:S(2)}) collective-permute-start(bf16[64,1536]{1,0:T(8,128)(2,1)S(1)} %get-tuple-element.134), channel_id=1, source_target_pairs={{0,4},{2,6},{4,0},{6,2},{1,5},{3,7},{5,1},{7,3},{8,12},{10,14},{12... | collective-permute-start | bytes 589832 | tf_op jit(solution)/shard_map/ppermute | solution.py:19
  186.5 0.4 collective-permute-start.34
  187.0 2.2 %collective-permute-start.35 = (bf16[64,1536]{1,0:T(8,128)(2,1)S(1)}, bf16[64,1536]{1,0:T(8,128)(2,1)S(1)}, u32[]{:S(2)}, u32[]{:S(2)}) collective-permute-start(bf16[64,1536]{1,0:T(8,128)(2,1)S(1)} %get-tuple-element.136), channel_id=1, source_target_pairs={{0,6},{2,0},{4,2},{6,4},{1,7},{3,1},{5,3},{7,5},{8,14},{10,8},{12,... | collective-permute-start | bytes 589832 | tf_op jit(solution)/shard_map/ppermute | solution.py:19
  189.2 2.0 %collective-permute-done.33 = bf16[64,1536]{1,0:T(8,128)(2,1)S(1)} collective-permute-done((bf16[64,1536]{1,0:T(8,128)(2,1)S(1)}, bf16[64,1536]{1,0:T(8,128)(2,1)S(1)}, u32[]{:S(2)}, u32[]{:S(2)}) %collective-permute-start.33) | collective-permute-done | bytes 196640 | tf_op jit(solution)/shard_map/ppermute | solution.py:19
  191.3 4.8 %collective-permute-done.34 = bf16[64,1536]{1,0:T(8,128)(2,1)S(1)} collective-permute-done((bf16[64,1536]{1,0:T(8,128)(2,1)S(1)}, bf16[64,1536]{1,0:T(8,128)(2,1)S(1)}, u32[]{:S(2)}, u32[]{:S(2)}) %collective-permute-start.34) | collective-permute-done | bytes 196640 | tf_op jit(solution)/shard_map/ppermute | solution.py:19
  196.1 0.8 add_convert_fusion
  (43 shorter events, 0.1 us)
Async XLA Ops:
  0.0 1.4 copy-start.2
  1.4 0.9 copy-start.3
  2.3 3.0 %copy-start = (bf16[3,1536,768]{2,1,0:T(8,128)(2,1)S(1)}, bf16[3,1536,768]{2,1,0:T(8,128)(2,1)}, u32[]{:S(2)}) copy-start(bf16[3,1536,768]{2,1,0:T(8,128)(2,1)} %w_ref.4) | copy-start | bytes 21233668
  5.3 24.6 %copy-start.5 = (s32[3,256]{1,0:T(4,128)S(1)}, s32[3,256]{1,0:T(4,128)}, u32[]{:S(2)}) copy-start(s32[3,256]{1,0:T(4,128)} %pos_ref.1) | copy-start | bytes 9220
  5.3 24.6 %copy-start.7 = (bf16[256,512]{1,0:T(8,128)(2,1)S(1)}, bf16[256,512]{1,0:T(8,128)(2,1)}, u32[]{:S(2)}) copy-start(bf16[256,512]{1,0:T(8,128)(2,1)} %constant.17.clone.turn_ref) | copy-start | bytes 786436
  5.3 24.6 %copy-start.8 = (f32[4,128]{1,0:T(4,128)S(1)}, f32[4,128]{1,0:T(4,128)}, u32[]{:S(2)}) copy-start(f32[4,128]{1,0:T(4,128)} %constant.18.clone.sign_ref) | copy-start | bytes 6148
  9.4 22.5 %copy-start.4 = (bf16[1,2,16,768]{3,2,1,0:T(8,128)(2,1)S(1)}, bf16[1,2,16,768]{3,2,1,0:T(8,128)(2,1)}, u32[]{:S(2)}) copy-start(bf16[1,2,16,768]{3,2,1,0:T(8,128)(2,1)} %text_ref.1) | copy-start | bytes 147460
  9.4 22.5 %copy-start.6 = (f32[2,128]{1,0:T(2,128)S(1)}, f32[2,128]{1,0:T(2,128)}, u32[]{:S(2)}) copy-start(f32[2,128]{1,0:T(2,128)} %gain_ref.3) | copy-start | bytes 3076
  9.4 22.4 %collective-permute-start = (bf16[256,1536]{1,0:T(8,128)(2,1)S(1)}, bf16[256,1536]{1,0:T(8,128)(2,1)S(1)}, u32[]{:S(2)}, u32[]{:S(2)}) collective-permute-start(bf16[256,1536]{1,0:T(8,128)(2,1)S(1)} %get-tuple-element.76), channel_id=1, source_target_pairs={{0,1},{1,0},{2,3},{3,2},{4,5},{5,4},{6,7},{7,6},{8,9},{9,8},{10,11... | collective-permute-start | bytes 2359304 | tf_op jit(solution)/shard_map/ppermute | solution.py:19
  36.0 6.3 %collective-permute-start.1 = (bf16[256,768]{1,0:T(8,128)(2,1)S(1)}, bf16[256,768]{1,0:T(8,128)(2,1)S(1)}, u32[]{:S(2)}, u32[]{:S(2)}) collective-permute-start(bf16[256,768]{1,0:T(8,128)(2,1)S(1)} %get-tuple-element.79), channel_id=1, source_target_pairs={{0,1},{1,0},{2,3},{3,2},{4,5},{5,4},{6,7},{7,6},{8,9},{9,8},{10,11... | collective-permute-start | bytes 1179656 | tf_op jit(solution)/shard_map/ppermute | solution.py:19
  36.5 13.5 %collective-permute-start.2 = (bf16[144,1536]{1,0:T(8,128)(2,1)S(1)}, bf16[144,1536]{1,0:T(8,128)(2,1)S(1)}, u32[]{:S(2)}, u32[]{:S(2)}) collective-permute-start(bf16[144,1536]{1,0:T(8,128)(2,1)S(1)} %get-tuple-element.80.refs_1_), channel_id=1, source_target_pairs={{0,8},{8,16},{16,24},{24,32},{32,40},{40,48},{48,56},{56,64},{64,7... | collective-permute-start | bytes 1327112 | tf_op jit(solution)/shard_map/ppermute | solution.py:19
  36.5 13.5 %collective-permute-start.3 = (bf16[144,1536]{1,0:T(8,128)(2,1)S(1)}, bf16[144,1536]{1,0:T(8,128)(2,1)S(1)}, u32[]{:S(2)}, u32[]{:S(2)}) collective-permute-start(bf16[144,1536]{1,0:T(8,128)(2,1)S(1)} %get-tuple-element.80.refs_1_), channel_id=1, source_target_pairs={{0,120},{8,0},{16,8},{24,16},{32,24},{40,32},{48,40},{56,48},{64,5... | collective-permute-start | bytes 1327112 | tf_op jit(solution)/shard_map/ppermute | solution.py:19
  39.6 18.8 %collective-permute-start.6 = (bf16[128,1536]{1,0:T(8,128)(2,1)S(1)}, bf16[128,1536]{1,0:T(8,128)(2,1)S(1)}, u32[]{:S(2)}, u32[]{:S(2)}) collective-permute-start(bf16[128,1536]{1,0:T(8,128)(2,1)S(1)} %get-tuple-element.77.refs_0_.refs_2_), channel_id=1, source_target_pairs={{0,8},{8,16},{16,24},{24,32},{32,40},{40,48},{48,56},{56,64},{64,7... | collective-permute-start | bytes 1179656 | tf_op jit(solution)/shard_map/ppermute | solution.py:19
  39.6 18.8 %collective-permute-start.7 = (bf16[128,1536]{1,0:T(8,128)(2,1)S(1)}, bf16[128,1536]{1,0:T(8,128)(2,1)S(1)}, u32[]{:S(2)}, u32[]{:S(2)}) collective-permute-start(bf16[128,1536]{1,0:T(8,128)(2,1)S(1)} %get-tuple-element.77.refs_0_.refs_2_), channel_id=1, source_target_pairs={{0,120},{8,0},{16,8},{24,16},{32,24},{40,32},{48,40},{56,48},{64,5... | collective-permute-start | bytes 1179656 | tf_op jit(solution)/shard_map/ppermute | solution.py:19
  50.0 17.9 %collective-permute-start.4 = (bf16[144,1536]{1,0:T(8,128)(2,1)S(1)}, bf16[144,1536]{1,0:T(8,128)(2,1)S(1)}, u32[]{:S(2)}, u32[]{:S(2)}) collective-permute-start(bf16[144,1536]{1,0:T(8,128)(2,1)S(1)} %collective-permute-done.2.refs_1_), channel_id=1, source_target_pairs={{0,8},{8,16},{16,24},{24,32},{32,40},{40,48},{48,56},{56,64},{64,7... | collective-permute-start | bytes 1327112 | tf_op jit(solution)/shard_map/ppermute | solution.py:19
  50.0 17.9 %collective-permute-start.5 = (bf16[144,1536]{1,0:T(8,128)(2,1)S(1)}, bf16[144,1536]{1,0:T(8,128)(2,1)S(1)}, u32[]{:S(2)}, u32[]{:S(2)}) collective-permute-start(bf16[144,1536]{1,0:T(8,128)(2,1)S(1)} %collective-permute-done.3.refs_3_), channel_id=1, source_target_pairs={{0,120},{8,0},{16,8},{24,16},{32,24},{40,32},{48,40},{56,48},{64,5... | collective-permute-start | bytes 1327112 | tf_op jit(solution)/shard_map/ppermute | solution.py:19
  58.4 17.9 %collective-permute-start.10 = (bf16[128,1536]{1,0:T(8,128)(2,1)S(1)}, bf16[128,1536]{1,0:T(8,128)(2,1)S(1)}, u32[]{:S(2)}, u32[]{:S(2)}) collective-permute-start(bf16[128,1536]{1,0:T(8,128)(2,1)S(1)} %collective-permute-done.6.refs_2_), channel_id=1, source_target_pairs={{0,8},{8,16},{16,24},{24,32},{32,40},{40,48},{48,56},{56,64},{64,7... | collective-permute-start | bytes 1179656 | tf_op jit(solution)/shard_map/ppermute | solution.py:19
  58.4 17.9 %collective-permute-start.11 = (bf16[128,1536]{1,0:T(8,128)(2,1)S(1)}, bf16[128,1536]{1,0:T(8,128)(2,1)S(1)}, u32[]{:S(2)}, u32[]{:S(2)}) collective-permute-start(bf16[128,1536]{1,0:T(8,128)(2,1)S(1)} %collective-permute-done.7.refs_4_), channel_id=1, source_target_pairs={{0,120},{8,0},{16,8},{24,16},{32,24},{40,32},{48,40},{56,48},{64,5... | collective-permute-start | bytes 1179656 | tf_op jit(solution)/shard_map/ppermute | solution.py:19
  67.9 17.9 %collective-permute-start.8 = (bf16[144,1536]{1,0:T(8,128)(2,1)S(1)}, bf16[144,1536]{1,0:T(8,128)(2,1)S(1)}, u32[]{:S(2)}, u32[]{:S(2)}) collective-permute-start(bf16[144,1536]{1,0:T(8,128)(2,1)S(1)} %collective-permute-done.4.refs_1_), channel_id=1, source_target_pairs={{0,8},{8,16},{16,24},{24,32},{32,40},{40,48},{48,56},{56,64},{64,7... | collective-permute-start | bytes 1327112 | tf_op jit(solution)/shard_map/ppermute | solution.py:19
  67.9 17.9 %collective-permute-start.9 = (bf16[144,1536]{1,0:T(8,128)(2,1)S(1)}, bf16[144,1536]{1,0:T(8,128)(2,1)S(1)}, u32[]{:S(2)}, u32[]{:S(2)}) collective-permute-start(bf16[144,1536]{1,0:T(8,128)(2,1)S(1)} %collective-permute-done.5.refs_3_), channel_id=1, source_target_pairs={{0,120},{8,0},{16,8},{24,16},{32,24},{40,32},{48,40},{56,48},{64,5... | collective-permute-start | bytes 1327112 | tf_op jit(solution)/shard_map/ppermute | solution.py:19
  76.3 20.2 %collective-permute-start.14 = (bf16[128,1536]{1,0:T(8,128)(2,1)S(1)}, bf16[128,1536]{1,0:T(8,128)(2,1)S(1)}, u32[]{:S(2)}, u32[]{:S(2)}) collective-permute-start(bf16[128,1536]{1,0:T(8,128)(2,1)S(1)} %collective-permute-done.10.refs_2_), channel_id=1, source_target_pairs={{0,8},{8,16},{16,24},{24,32},{32,40},{40,48},{48,56},{56,64},{64,7... | collective-permute-start | bytes 1179656 | tf_op jit(solution)/shard_map/ppermute | solution.py:19
  76.3 16.8 %collective-permute-start.15 = (bf16[128,1536]{1,0:T(8,128)(2,1)S(1)}, bf16[128,1536]{1,0:T(8,128)(2,1)S(1)}, u32[]{:S(2)}, u32[]{:S(2)}) collective-permute-start(bf16[128,1536]{1,0:T(8,128)(2,1)S(1)} %collective-permute-done.11.refs_4_), channel_id=1, source_target_pairs={{0,120},{8,0},{16,8},{24,16},{32,24},{40,32},{48,40},{56,48},{64,5... | collective-permute-start | bytes 1179656 | tf_op jit(solution)/shard_map/ppermute | solution.py:19
  85.8 17.9 %collective-permute-start.12 = (bf16[144,1536]{1,0:T(8,128)(2,1)S(1)}, bf16[144,1536]{1,0:T(8,128)(2,1)S(1)}, u32[]{:S(2)}, u32[]{:S(2)}) collective-permute-start(bf16[144,1536]{1,0:T(8,128)(2,1)S(1)} %collective-permute-done.8.refs_1_), channel_id=1, source_target_pairs={{0,8},{8,16},{16,24},{24,32},{32,40},{40,48},{48,56},{56,64},{64,7... | collective-permute-start | bytes 1327112 | tf_op jit(solution)/shard_map/ppermute | solution.py:19
  85.8 17.9 %collective-permute-start.13 = (bf16[144,1536]{1,0:T(8,128)(2,1)S(1)}, bf16[144,1536]{1,0:T(8,128)(2,1)S(1)}, u32[]{:S(2)}, u32[]{:S(2)}) collective-permute-start(bf16[144,1536]{1,0:T(8,128)(2,1)S(1)} %collective-permute-done.9.refs_3_), channel_id=1, source_target_pairs={{0,120},{8,0},{16,8},{24,16},{32,24},{40,32},{48,40},{56,48},{64,5... | collective-permute-start | bytes 1327112 | tf_op jit(solution)/shard_map/ppermute | solution.py:19
  93.1 17.9 %collective-permute-start.19 = (bf16[128,1536]{1,0:T(8,128)(2,1)S(1)}, bf16[128,1536]{1,0:T(8,128)(2,1)S(1)}, u32[]{:S(2)}, u32[]{:S(2)}) collective-permute-start(bf16[128,1536]{1,0:T(8,128)(2,1)S(1)} %collective-permute-done.15.refs_4_), channel_id=1, source_target_pairs={{0,120},{8,0},{16,8},{24,16},{32,24},{40,32},{48,40},{56,48},{64,5... | collective-permute-start | bytes 1179656 | tf_op jit(solution)/shard_map/ppermute | solution.py:19
  96.5 17.9 %collective-permute-start.18 = (bf16[128,1536]{1,0:T(8,128)(2,1)S(1)}, bf16[128,1536]{1,0:T(8,128)(2,1)S(1)}, u32[]{:S(2)}, u32[]{:S(2)}) collective-permute-start(bf16[128,1536]{1,0:T(8,128)(2,1)S(1)} %collective-permute-done.14.refs_2_), channel_id=1, source_target_pairs={{0,8},{8,16},{16,24},{24,32},{32,40},{40,48},{48,56},{56,64},{64,7... | collective-permute-start | bytes 1179656 | tf_op jit(solution)/shard_map/ppermute | solution.py:19
  103.7 17.9 %collective-permute-start.16 = (bf16[144,1536]{1,0:T(8,128)(2,1)S(1)}, bf16[144,1536]{1,0:T(8,128)(2,1)S(1)}, u32[]{:S(2)}, u32[]{:S(2)}) collective-permute-start(bf16[144,1536]{1,0:T(8,128)(2,1)S(1)} %collective-permute-done.12.refs_1_), channel_id=1, source_target_pairs={{0,8},{8,16},{16,24},{24,32},{32,40},{40,48},{48,56},{56,64},{64,7... | collective-permute-start | bytes 1327112 | tf_op jit(solution)/shard_map/ppermute | solution.py:19
  103.7 17.9 %collective-permute-start.17 = (bf16[144,1536]{1,0:T(8,128)(2,1)S(1)}, bf16[144,1536]{1,0:T(8,128)(2,1)S(1)}, u32[]{:S(2)}, u32[]{:S(2)}) collective-permute-start(bf16[144,1536]{1,0:T(8,128)(2,1)S(1)} %collective-permute-done.13.refs_3_), channel_id=1, source_target_pairs={{0,120},{8,0},{16,8},{24,16},{32,24},{40,32},{48,40},{56,48},{64,5... | collective-permute-start | bytes 1327112 | tf_op jit(solution)/shard_map/ppermute | solution.py:19
  111.0 17.9 %collective-permute-start.23 = (bf16[128,1536]{1,0:T(8,128)(2,1)S(1)}, bf16[128,1536]{1,0:T(8,128)(2,1)S(1)}, u32[]{:S(2)}, u32[]{:S(2)}) collective-permute-start(bf16[128,1536]{1,0:T(8,128)(2,1)S(1)} %collective-permute-done.19.refs_4_), channel_id=1, source_target_pairs={{0,120},{8,0},{16,8},{24,16},{32,24},{40,32},{48,40},{56,48},{64,5... | collective-permute-start | bytes 1179656 | tf_op jit(solution)/shard_map/ppermute | solution.py:19
  114.4 17.9 %collective-permute-start.22 = (bf16[128,1536]{1,0:T(8,128)(2,1)S(1)}, bf16[128,1536]{1,0:T(8,128)(2,1)S(1)}, u32[]{:S(2)}, u32[]{:S(2)}) collective-permute-start(bf16[128,1536]{1,0:T(8,128)(2,1)S(1)} %collective-permute-done.18.refs_2_), channel_id=1, source_target_pairs={{0,8},{8,16},{16,24},{24,32},{32,40},{40,48},{48,56},{56,64},{64,7... | collective-permute-start | bytes 1179656 | tf_op jit(solution)/shard_map/ppermute | solution.py:19
  121.6 17.9 %collective-permute-start.20 = (bf16[144,1536]{1,0:T(8,128)(2,1)S(1)}, bf16[144,1536]{1,0:T(8,128)(2,1)S(1)}, u32[]{:S(2)}, u32[]{:S(2)}) collective-permute-start(bf16[144,1536]{1,0:T(8,128)(2,1)S(1)} %collective-permute-done.16.refs_1_), channel_id=1, source_target_pairs={{0,8},{8,16},{16,24},{24,32},{32,40},{40,48},{48,56},{56,64},{64,7... | collective-permute-start | bytes 1327112 | tf_op jit(solution)/shard_map/ppermute | solution.py:19
  121.6 17.9 %collective-permute-start.21 = (bf16[144,1536]{1,0:T(8,128)(2,1)S(1)}, bf16[144,1536]{1,0:T(8,128)(2,1)S(1)}, u32[]{:S(2)}, u32[]{:S(2)}) collective-permute-start(bf16[144,1536]{1,0:T(8,128)(2,1)S(1)} %collective-permute-done.17.refs_3_), channel_id=1, source_target_pairs={{0,120},{8,0},{16,8},{24,16},{32,24},{40,32},{48,40},{56,48},{64,5... | collective-permute-start | bytes 1327112 | tf_op jit(solution)/shard_map/ppermute | solution.py:19
  128.9 17.9 %collective-permute-start.27 = (bf16[128,1536]{1,0:T(8,128)(2,1)S(1)}, bf16[128,1536]{1,0:T(8,128)(2,1)S(1)}, u32[]{:S(2)}, u32[]{:S(2)}) collective-permute-start(bf16[128,1536]{1,0:T(8,128)(2,1)S(1)} %collective-permute-done.23.refs_4_), channel_id=1, source_target_pairs={{0,120},{8,0},{16,8},{24,16},{32,24},{40,32},{48,40},{56,48},{64,5... | collective-permute-start | bytes 1179656 | tf_op jit(solution)/shard_map/ppermute | solution.py:19
  132.3 17.9 %collective-permute-start.26 = (bf16[128,1536]{1,0:T(8,128)(2,1)S(1)}, bf16[128,1536]{1,0:T(8,128)(2,1)S(1)}, u32[]{:S(2)}, u32[]{:S(2)}) collective-permute-start(bf16[128,1536]{1,0:T(8,128)(2,1)S(1)} %collective-permute-done.22.refs_2_), channel_id=1, source_target_pairs={{0,8},{8,16},{16,24},{24,32},{32,40},{40,48},{48,56},{56,64},{64,7... | collective-permute-start | bytes 1179656 | tf_op jit(solution)/shard_map/ppermute | solution.py:19
  139.5 17.9 %collective-permute-start.24 = (bf16[144,1536]{1,0:T(8,128)(2,1)S(1)}, bf16[144,1536]{1,0:T(8,128)(2,1)S(1)}, u32[]{:S(2)}, u32[]{:S(2)}) collective-permute-start(bf16[144,1536]{1,0:T(8,128)(2,1)S(1)} %collective-permute-done.20.refs_1_), channel_id=1, source_target_pairs={{0,8},{8,16},{16,24},{24,32},{32,40},{40,48},{48,56},{56,64},{64,7... | collective-permute-start | bytes 1327112 | tf_op jit(solution)/shard_map/ppermute | solution.py:19
  139.5 17.9 %collective-permute-start.25 = (bf16[144,1536]{1,0:T(8,128)(2,1)S(1)}, bf16[144,1536]{1,0:T(8,128)(2,1)S(1)}, u32[]{:S(2)}, u32[]{:S(2)}) collective-permute-start(bf16[144,1536]{1,0:T(8,128)(2,1)S(1)} %collective-permute-done.21.refs_3_), channel_id=1, source_target_pairs={{0,120},{8,0},{16,8},{24,16},{32,24},{40,32},{48,40},{56,48},{64,5... | collective-permute-start | bytes 1327112 | tf_op jit(solution)/shard_map/ppermute | solution.py:19
  146.8 17.9 %collective-permute-start.29 = (bf16[128,1536]{1,0:T(8,128)(2,1)S(1)}, bf16[128,1536]{1,0:T(8,128)(2,1)S(1)}, u32[]{:S(2)}, u32[]{:S(2)}) collective-permute-start(bf16[128,1536]{1,0:T(8,128)(2,1)S(1)} %collective-permute-done.27.refs_4_), channel_id=1, source_target_pairs={{0,120},{8,0},{16,8},{24,16},{32,24},{40,32},{48,40},{56,48},{64,5... | collective-permute-start | bytes 1179656 | tf_op jit(solution)/shard_map/ppermute | solution.py:19
  150.2 18.6 %collective-permute-start.31 = (bf16[128,1536]{1,0:T(8,128)(2,1)S(1)}, bf16[128,1536]{1,0:T(8,128)(2,1)S(1)}, u32[]{:S(2)}, u32[]{:S(2)}) collective-permute-start(bf16[128,1536]{1,0:T(8,128)(2,1)S(1)} %collective-permute-done.26.refs_2_), channel_id=1, source_target_pairs={{0,8},{8,16},{16,24},{24,32},{32,40},{40,48},{48,56},{56,64},{64,7... | collective-permute-start | bytes 1179656 | tf_op jit(solution)/shard_map/ppermute | solution.py:19
  157.4 18.1 %collective-permute-start.28 = (bf16[144,1536]{1,0:T(8,128)(2,1)S(1)}, bf16[144,1536]{1,0:T(8,128)(2,1)S(1)}, u32[]{:S(2)}, u32[]{:S(2)}) collective-permute-start(bf16[144,1536]{1,0:T(8,128)(2,1)S(1)} %collective-permute-done.24.refs_1_), channel_id=1, source_target_pairs={{0,8},{8,16},{16,24},{24,32},{32,40},{40,48},{48,56},{56,64},{64,7... | collective-permute-start | bytes 1327112 | tf_op jit(solution)/shard_map/ppermute | solution.py:19
  164.7 10.8 %collective-permute-start.30 = (bf16[128,1536]{1,0:T(8,128)(2,1)S(1)}, bf16[128,1536]{1,0:T(8,128)(2,1)S(1)}, u32[]{:S(2)}, u32[]{:S(2)}) collective-permute-start(bf16[128,1536]{1,0:T(8,128)(2,1)S(1)} %collective-permute-done.29.refs_4_), channel_id=1, source_target_pairs={{0,120},{8,0},{16,8},{24,16},{32,24},{40,32},{48,40},{56,48},{64,5... | collective-permute-start | bytes 1179656 | tf_op jit(solution)/shard_map/ppermute | solution.py:19
  175.5 5.6 %copy-start.1 = (bf16[768,1536]{1,0:T(8,128)(2,1)S(1)}, bf16[768,1536]{1,0:T(8,128)(2,1)}, u32[]{:S(2)}) copy-start(bf16[768,1536]{1,0:T(8,128)(2,1)} %w_ref.5) | copy-start | bytes 7077892
  177.6 3.5 %collective-permute-start.32 = (bf16[256,768]{1,0:T(8,128)(2,1)S(1)}, bf16[256,768]{1,0:T(8,128)(2,1)S(1)}, u32[]{:S(2)}, u32[]{:S(2)}) collective-permute-start(bf16[256,768]{1,0:T(8,128)(2,1)S(1)} %attend_last.1.own_ref), channel_id=1, source_target_pairs={{0,1},{1,0},{2,3},{3,2},{4,5},{5,4},{6,7},{7,6},{8,9},{9,8},{10,11... | collective-permute-start | bytes 1179656 | tf_op jit(solution)/shard_map/ppermute | solution.py:19
  183.4 7.8 %collective-permute-start.33 = (bf16[64,1536]{1,0:T(8,128)(2,1)S(1)}, bf16[64,1536]{1,0:T(8,128)(2,1)S(1)}, u32[]{:S(2)}, u32[]{:S(2)}) collective-permute-start(bf16[64,1536]{1,0:T(8,128)(2,1)S(1)} %get-tuple-element.134), channel_id=1, source_target_pairs={{0,4},{2,6},{4,0},{6,2},{1,5},{3,7},{5,1},{7,3},{8,12},{10,14},{12... | collective-permute-start | bytes 589832 | tf_op jit(solution)/shard_map/ppermute | solution.py:19
  186.5 9.5 %collective-permute-start.34 = (bf16[64,1536]{1,0:T(8,128)(2,1)S(1)}, bf16[64,1536]{1,0:T(8,128)(2,1)S(1)}, u32[]{:S(2)}, u32[]{:S(2)}) collective-permute-start(bf16[64,1536]{1,0:T(8,128)(2,1)S(1)} %get-tuple-element.135), channel_id=1, source_target_pairs={{0,2},{2,4},{4,6},{6,0},{1,3},{3,5},{5,7},{7,1},{8,10},{10,12},{12... | collective-permute-start | bytes 589832 | tf_op jit(solution)/shard_map/ppermute | solution.py:19
  187.0 9.1 %collective-permute-start.35 = (bf16[64,1536]{1,0:T(8,128)(2,1)S(1)}, bf16[64,1536]{1,0:T(8,128)(2,1)S(1)}, u32[]{:S(2)}, u32[]{:S(2)}) collective-permute-start(bf16[64,1536]{1,0:T(8,128)(2,1)S(1)} %get-tuple-element.136), channel_id=1, source_target_pairs={{0,6},{2,0},{4,2},{6,4},{1,7},{3,1},{5,3},{7,5},{8,14},{10,8},{12,... | collective-permute-start | bytes 589832 | tf_op jit(solution)/shard_map/ppermute | solution.py:19

commit v2 on v1

--- a/solution.py
+++ b/solution.py
@@ -124,7 +124,7 @@
 def modulate(branch, latent, mod):
     rows, width = latent.shape
     half = width // 2
-    step = 64
+    step = 128
     shape = jax.ShapeDtypeStruct((2, rows, half), jnp.bfloat16)
     spec = pl.BlockSpec((2, step, half), lambda i, c: (0, i, 0))
     return pl.pallas_call(
@@ -423,7 +423,8 @@
     latent, z, x, branch = lax.optimization_barrier((latent, z[None], x[None], c[None]))
     half = n_seq // 2
     cut = rows // 2
-    both = modulate(branch, latent, modulation)
+    hbm = lambda a: pltpu.with_memory_space_constraint(a, pltpu.MemorySpace.HBM)
+    both = modulate(branch, hbm(latent), hbm(modulation))
     kv_mine, kv_theirs = terms(both, w_qkv, 1, 2)
     kv_got = shifted(kv_theirs, "cfg", 1)
     tables = rotary_tables(positions)

time: 197 us -> 195 us (0.990)
  local copies, waits for them, and re-layouts: 3.61 us -> 0.89 us
    unnamed x18 -> x16, local copies, waits for them, and re-layouts: 3.61 us -> 0.89 us
where the time goes in v2:
time: 195 us
  waiting for transfers between devices  76.2 us (39%)
  starting transfers between devices  73.2 us (38%)
  Pallas kernels  42.5 us (22%)
    ppermute x36, waiting for transfers between devices, shifted(): return lax.ppermute(value, axis, [(i, (i + by) % n) for i in range(n)])  76.2 us
    ppermute x36, starting transfers between devices, shifted(): return lax.ppermute(value, axis, [(i, (i + by) % n) for i in range(n)])  73.2 us
    pallas_call x8, Pallas kernels, attend_step(): pl.pallas_call(functools.partial(step_kernel, len(blocks), first, used),...  24.6 us
    pallas_call x2, Pallas kernels, terms(): pl.pallas_call(terms_kernel, grid=(count * tiles,), in_specs=[whole, pl.B...  6.12 us
  transfers between devices with their start and end apart: 36, of which 19 were waited for; matrix products, arithmetic and copies ran while one was open for 0% of the time, Pallas kernels for 14%

profile of v2, /device:TPU:33, one launch (start us, length us, event | category | flops | bytes accessed | tf_op | source)
XLA Modules:
  0.0 195.1 jit_solution(12155280636878244336)
XLA Ops:
  0.0 2.6 %norm.1.both_ref = bf16[2,256,1536]{2,1,0:T(8,128)(2,1)S(1)} custom-call(s32[1]{0:T(128)} %bitcast.2.c_ref, bf16[256,3072]{1,0:T(8,128)(2,1)} %x_ref, f32[3,2,3072]{2,1,0:T(2,128)} %mod_ref.3), custom_call_target="tpu_custom_call" | custom-call | flops 3000000000 | bytes 3145728 | tf_op jit(solution)/shard_map/norm/pallas_call | solution.py:130
  2.6 0.9 copy-done
  3.5 4.0 %terms.2 = (f32[256,1536]{1,0:T(8,128)S(1)}, bf16[256,1536]{1,0:T(8,128)(2,1)S(1)}) custom-call(bf16[2,256,1536]{2,1,0:T(8,128)(2,1)S(1)} %norm.1.both_ref, bf16[3,1536,768]{2,1,0:T(8,128)(2,1)S(1)} %copy-done), custom_call_target="tpu_custom_call" | custom-call | flops 2415919104 | bytes 4718592 | tf_op jit(solution)/shard_map/terms/pallas_call | solution.py:163
  7.6 0.0 copy-start.3
  7.6 0.0 copy-start.5
  7.6 20.5 %collective-permute-start = (bf16[256,1536]{1,0:T(8,128)(2,1)S(1)}, bf16[256,1536]{1,0:T(8,128)(2,1)S(1)}, u32[]{:S(2)}, u32[]{:S(2)}) collective-permute-start(bf16[256,1536]{1,0:T(8,128)(2,1)S(1)} %get-tuple-element.76), channel_id=1, source_target_pairs={{0,1},{1,0},{2,3},{3,2},{4,5},{5,4},{6,7},{7,6},{8,9},{9,8},{10,11... | collective-permute-start | bytes 2359304 | tf_op jit(solution)/shard_map/ppermute | solution.py:19
  28.1 0.8 tables.1.tab_ref
  28.9 1.1 collective-permute-done.got_ref
  30.0 2.1 %keys.1 = (bf16[144,1536]{1,0:T(8,128)(2,1)S(1)}, bf16[128,1536]{1,0:T(8,128)(2,1)S(1)}) custom-call(f32[256,1536]{1,0:T(8,128)S(1)} %get-tuple-element.75.mine_ref, bf16[256,1536]{1,0:T(8,128)(2,1)S(1)} %collective-permute-done.got_ref, bf16[1,2,16,768]{3,2,1,0:T(8,128)(2,1)S(1)} %copy-done.3, f32[2,128]{1,0:T(2,128)S(1)} %copy-done.5, ...), custom_call_target="tpu_custom_call" | custom-call | flops 1000000000 | bytes 3145728 | tf_op jit(solution)/shard_map/keys/pallas_call | solution.py:217
  32.1 2.1 %terms.3 = (f32[256,768]{1,0:T(8,128)S(1)}, bf16[256,768]{1,0:T(8,128)(2,1)S(1)}) custom-call(bf16[2,256,1536]{2,1,0:T(8,128)(2,1)S(1)} %norm.1.both_ref, bf16[3,1536,768]{2,1,0:T(8,128)(2,1)S(1)} %copy-done, bf16[128,1536]{1,0:T(8,128)(2,1)S(1)} %get-tuple-element.77.refs_0_.refs_2_), custom_call_target="tpu_custom_call" | custom-call | flops 1207959552 | bytes 2359296 | tf_op jit(solution)/shard_map/terms/pallas_call | solution.py:163
  34.2 0.5 collective-permute-start.1
  34.7 0.0 collective-permute-start.2
  34.7 3.1 %collective-permute-start.3 = (bf16[144,1536]{1,0:T(8,128)(2,1)S(1)}, bf16[144,1536]{1,0:T(8,128)(2,1)S(1)}, u32[]{:S(2)}, u32[]{:S(2)}) collective-permute-start(bf16[144,1536]{1,0:T(8,128)(2,1)S(1)} %get-tuple-element.80.refs_1_), channel_id=1, source_target_pairs={{0,120},{8,0},{16,8},{24,16},{32,24},{40,32},{48,40},{56,48},{64,5... | collective-permute-start | bytes 1327112 | tf_op jit(solution)/shard_map/ppermute | solution.py:19
  37.8 0.0 collective-permute-start.6
  37.8 2.7 %collective-permute-start.7 = (bf16[128,1536]{1,0:T(8,128)(2,1)S(1)}, bf16[128,1536]{1,0:T(8,128)(2,1)S(1)}, u32[]{:S(2)}, u32[]{:S(2)}) collective-permute-start(bf16[128,1536]{1,0:T(8,128)(2,1)S(1)} %get-tuple-element.77.refs_0_.refs_2_), channel_id=1, source_target_pairs={{0,120},{8,0},{16,8},{24,16},{32,24},{40,32},{48,40},{56,48},{64,5... | collective-permute-start | bytes 1179656 | tf_op jit(solution)/shard_map/ppermute | solution.py:19
  40.5 1.9 queries.1.refs_0_.q_ref
  42.4 2.0 %attend.8 = (f32[256,768]{1,0:T(8,128)S(1)}, f32[256,768]{1,0:T(8,128)S(1)}, bf16[16,1536]{1,0:T(8,128)(2,1)S(1)}) custom-call(bf16[256,768]{1,0:T(8,128)(2,1)S(1)} %queries.1.refs_0_.q_ref, bf16[144,1536]{1,0:T(8,128)(2,1)S(1)} %get-tuple-element.80.refs_1_, bf16[128,1536]{1,0:T(8,128)(2,1)S(1)} %get-tuple-element.77.refs_0_.refs_2_), custom_call_target="tpu_custom_call" | custom-call | flops 805306368 | bytes 786432 | tf_op jit(solution)/shard_map/attend/pallas_call | solution.py:305
  44.4 3.8 %collective-permute-done.2.refs_1_ = bf16[144,1536]{1,0:T(8,128)(2,1)S(1)} collective-permute-done((bf16[144,1536]{1,0:T(8,128)(2,1)S(1)}, bf16[144,1536]{1,0:T(8,128)(2,1)S(1)}, u32[]{:S(2)}, u32[]{:S(2)}) %collective-permute-start.2) | collective-permute-done | bytes 442400 | tf_op jit(solution)/shard_map/ppermute | solution.py:19
  48.2 2.7 %collective-permute-start.5 = (bf16[144,1536]{1,0:T(8,128)(2,1)S(1)}, bf16[144,1536]{1,0:T(8,128)(2,1)S(1)}, u32[]{:S(2)}, u32[]{:S(2)}) collective-permute-start(bf16[144,1536]{1,0:T(8,128)(2,1)S(1)} %collective-permute-done.3.refs_3_), channel_id=1, source_target_pairs={{0,120},{8,0},{16,8},{24,16},{32,24},{40,32},{48,40},{56,48},{64,5... | collective-permute-start | bytes 1327112 | tf_op jit(solution)/shard_map/ppermute | solution.py:19
  50.9 5.7 %collective-permute-done.6.refs_2_ = bf16[128,1536]{1,0:T(8,128)(2,1)S(1)} collective-permute-done((bf16[128,1536]{1,0:T(8,128)(2,1)S(1)}, bf16[128,1536]{1,0:T(8,128)(2,1)S(1)}, u32[]{:S(2)}, u32[]{:S(2)}) %collective-permute-start.6) | collective-permute-done | bytes 393248 | tf_op jit(solution)/shard_map/ppermute | solution.py:19
  56.6 0.0 collective-permute-done.7.refs_4_
  56.6 2.7 %collective-permute-start.11 = (bf16[128,1536]{1,0:T(8,128)(2,1)S(1)}, bf16[128,1536]{1,0:T(8,128)(2,1)S(1)}, u32[]{:S(2)}, u32[]{:S(2)}) collective-permute-start(bf16[128,1536]{1,0:T(8,128)(2,1)S(1)} %collective-permute-done.7.refs_4_), channel_id=1, source_target_pairs={{0,120},{8,0},{16,8},{24,16},{32,24},{40,32},{48,40},{56,48},{64,5... | collective-permute-start | bytes 1179656 | tf_op jit(solution)/shard_map/ppermute | solution.py:19
  59.3 3.2 %attend.9 = (f32[256,768]{1,0:T(8,128)S(1)}, f32[256,768]{1,0:T(8,128)S(1)}, bf16[32,1536]{1,0:T(8,128)(2,1)S(1)}) custom-call(bf16[256,768]{1,0:T(8,128)(2,1)S(1)} %queries.1.refs_0_.q_ref, bf16[144,1536]{1,0:T(8,128)(2,1)S(1)} %collective-permute-done.2.refs_1_, ...), custom_call_target="tpu_custom_call", output_to_operand_aliasing={{0}: (5, {}), {1}: (6, {})} | custom-call | flops 1610612736 | bytes 786432 | tf_op jit(solution)/shard_map/attend/pallas_call | solution.py:305
  62.5 3.6 %collective-permute-done.4.refs_1_ = bf16[144,1536]{1,0:T(8,128)(2,1)S(1)} collective-permute-done((bf16[144,1536]{1,0:T(8,128)(2,1)S(1)}, bf16[144,1536]{1,0:T(8,128)(2,1)S(1)}, u32[]{:S(2)}, u32[]{:S(2)}) %collective-permute-start.4) | collective-permute-done | bytes 442400 | tf_op jit(solution)/shard_map/ppermute | solution.py:19
  66.1 2.7 %collective-permute-start.9 = (bf16[144,1536]{1,0:T(8,128)(2,1)S(1)}, bf16[144,1536]{1,0:T(8,128)(2,1)S(1)}, u32[]{:S(2)}, u32[]{:S(2)}) collective-permute-start(bf16[144,1536]{1,0:T(8,128)(2,1)S(1)} %collective-permute-done.5.refs_3_), channel_id=1, source_target_pairs={{0,120},{8,0},{16,8},{24,16},{32,24},{40,32},{48,40},{56,48},{64,5... | collective-permute-start | bytes 1327112 | tf_op jit(solution)/shard_map/ppermute | solution.py:19
  68.8 5.7 %collective-permute-done.10.refs_2_ = bf16[128,1536]{1,0:T(8,128)(2,1)S(1)} collective-permute-done((bf16[128,1536]{1,0:T(8,128)(2,1)S(1)}, bf16[128,1536]{1,0:T(8,128)(2,1)S(1)}, u32[]{:S(2)}, u32[]{:S(2)}) %collective-permute-start.10) | collective-permute-done | bytes 393248 | tf_op jit(solution)/shard_map/ppermute | solution.py:19
  74.5 2.7 %collective-permute-start.15 = (bf16[128,1536]{1,0:T(8,128)(2,1)S(1)}, bf16[128,1536]{1,0:T(8,128)(2,1)S(1)}, u32[]{:S(2)}, u32[]{:S(2)}) collective-permute-start(bf16[128,1536]{1,0:T(8,128)(2,1)S(1)} %collective-permute-done.11.refs_4_), channel_id=1, source_target_pairs={{0,120},{8,0},{16,8},{24,16},{32,24},{40,32},{48,40},{56,48},{64,5... | collective-permute-start | bytes 1179656 | tf_op jit(solution)/shard_map/ppermute | solution.py:19
  77.2 3.2 %attend.10 = (f32[256,768]{1,0:T(8,128)S(1)}, f32[256,768]{1,0:T(8,128)S(1)}, bf16[32,1536]{1,0:T(8,128)(2,1)S(1)}) custom-call(bf16[256,768]{1,0:T(8,128)(2,1)S(1)} %queries.1.refs_0_.q_ref, bf16[144,1536]{1,0:T(8,128)(2,1)S(1)} %collective-permute-done.4.refs_1_, ...), custom_call_target="tpu_custom_call", output_to_operand_aliasing={{0}: (5, {}), {1}: (6, {})} | custom-call | flops 1610612736 | bytes 786432 | tf_op jit(solution)/shard_map/attend/pallas_call | solution.py:305
  80.4 3.6 %collective-permute-done.8.refs_1_ = bf16[144,1536]{1,0:T(8,128)(2,1)S(1)} collective-permute-done((bf16[144,1536]{1,0:T(8,128)(2,1)S(1)}, bf16[144,1536]{1,0:T(8,128)(2,1)S(1)}, u32[]{:S(2)}, u32[]{:S(2)}) %collective-permute-start.8) | collective-permute-done | bytes 442400 | tf_op jit(solution)/shard_map/ppermute | solution.py:19
  84.0 2.7 %collective-permute-start.13 = (bf16[144,1536]{1,0:T(8,128)(2,1)S(1)}, bf16[144,1536]{1,0:T(8,128)(2,1)S(1)}, u32[]{:S(2)}, u32[]{:S(2)}) collective-permute-start(bf16[144,1536]{1,0:T(8,128)(2,1)S(1)} %collective-permute-done.9.refs_3_), channel_id=1, source_target_pairs={{0,120},{8,0},{16,8},{24,16},{32,24},{40,32},{48,40},{56,48},{64,5... | collective-permute-start | bytes 1327112 | tf_op jit(solution)/shard_map/ppermute | solution.py:19
  86.7 4.6 %collective-permute-done.15.refs_4_ = bf16[128,1536]{1,0:T(8,128)(2,1)S(1)} collective-permute-done((bf16[128,1536]{1,0:T(8,128)(2,1)S(1)}, bf16[128,1536]{1,0:T(8,128)(2,1)S(1)}, u32[]{:S(2)}, u32[]{:S(2)}) %collective-permute-start.15) | collective-permute-done | bytes 393248 | tf_op jit(solution)/shard_map/ppermute | solution.py:19
  91.3 3.4 %collective-permute-start.19 = (bf16[128,1536]{1,0:T(8,128)(2,1)S(1)}, bf16[128,1536]{1,0:T(8,128)(2,1)S(1)}, u32[]{:S(2)}, u32[]{:S(2)}) collective-permute-start(bf16[128,1536]{1,0:T(8,128)(2,1)S(1)} %collective-permute-done.15.refs_4_), channel_id=1, source_target_pairs={{0,120},{8,0},{16,8},{24,16},{32,24},{40,32},{48,40},{56,48},{64,5... | collective-permute-start | bytes 1179656 | tf_op jit(solution)/shard_map/ppermute | solution.py:19
  94.7 3.2 %attend.11 = (f32[256,768]{1,0:T(8,128)S(1)}, f32[256,768]{1,0:T(8,128)S(1)}, bf16[32,1536]{1,0:T(8,128)(2,1)S(1)}) custom-call(bf16[256,768]{1,0:T(8,128)(2,1)S(1)} %queries.1.refs_0_.q_ref, bf16[144,1536]{1,0:T(8,128)(2,1)S(1)} %collective-permute-done.8.refs_1_, ...), custom_call_target="tpu_custom_call", output_to_operand_aliasing={{0}: (5, {}), {1}: (6, {})} | custom-call | flops 1610612736 | bytes 786432 | tf_op jit(solution)/shard_map/attend/pallas_call | solution.py:305
  97.9 4.0 %collective-permute-done.12.refs_1_ = bf16[144,1536]{1,0:T(8,128)(2,1)S(1)} collective-permute-done((bf16[144,1536]{1,0:T(8,128)(2,1)S(1)}, bf16[144,1536]{1,0:T(8,128)(2,1)S(1)}, u32[]{:S(2)}, u32[]{:S(2)}) %collective-permute-start.12) | collective-permute-done | bytes 442400 | tf_op jit(solution)/shard_map/ppermute | solution.py:19
  101.9 2.7 %collective-permute-start.17 = (bf16[144,1536]{1,0:T(8,128)(2,1)S(1)}, bf16[144,1536]{1,0:T(8,128)(2,1)S(1)}, u32[]{:S(2)}, u32[]{:S(2)}) collective-permute-start(bf16[144,1536]{1,0:T(8,128)(2,1)S(1)} %collective-permute-done.13.refs_3_), channel_id=1, source_target_pairs={{0,120},{8,0},{16,8},{24,16},{32,24},{40,32},{48,40},{56,48},{64,5... | collective-permute-start | bytes 1327112 | tf_op jit(solution)/shard_map/ppermute | solution.py:19
  104.6 4.6 %collective-permute-done.19.refs_4_ = bf16[128,1536]{1,0:T(8,128)(2,1)S(1)} collective-permute-done((bf16[128,1536]{1,0:T(8,128)(2,1)S(1)}, bf16[128,1536]{1,0:T(8,128)(2,1)S(1)}, u32[]{:S(2)}, u32[]{:S(2)}) %collective-permute-start.19) | collective-permute-done | bytes 393248 | tf_op jit(solution)/shard_map/ppermute | solution.py:19
  109.2 3.4 %collective-permute-start.23 = (bf16[128,1536]{1,0:T(8,128)(2,1)S(1)}, bf16[128,1536]{1,0:T(8,128)(2,1)S(1)}, u32[]{:S(2)}, u32[]{:S(2)}) collective-permute-start(bf16[128,1536]{1,0:T(8,128)(2,1)S(1)} %collective-permute-done.19.refs_4_), channel_id=1, source_target_pairs={{0,120},{8,0},{16,8},{24,16},{32,24},{40,32},{48,40},{56,48},{64,5... | collective-permute-start | bytes 1179656 | tf_op jit(solution)/shard_map/ppermute | solution.py:19
  112.6 3.2 %attend.12 = (f32[256,768]{1,0:T(8,128)S(1)}, f32[256,768]{1,0:T(8,128)S(1)}, bf16[32,1536]{1,0:T(8,128)(2,1)S(1)}) custom-call(bf16[256,768]{1,0:T(8,128)(2,1)S(1)} %queries.1.refs_0_.q_ref, bf16[144,1536]{1,0:T(8,128)(2,1)S(1)} %collective-permute-done.12.refs_1_, ...), custom_call_target="tpu_custom_call", output_to_operand_aliasing={{0}: (5, {}), {1}: (6, {})} | custom-call | flops 1610612736 | bytes 786432 | tf_op jit(solution)/shard_map/attend/pallas_call | solution.py:305
  115.8 4.0 %collective-permute-done.16.refs_1_ = bf16[144,1536]{1,0:T(8,128)(2,1)S(1)} collective-permute-done((bf16[144,1536]{1,0:T(8,128)(2,1)S(1)}, bf16[144,1536]{1,0:T(8,128)(2,1)S(1)}, u32[]{:S(2)}, u32[]{:S(2)}) %collective-permute-start.16) | collective-permute-done | bytes 442400 | tf_op jit(solution)/shard_map/ppermute | solution.py:19
  119.8 2.7 %collective-permute-start.21 = (bf16[144,1536]{1,0:T(8,128)(2,1)S(1)}, bf16[144,1536]{1,0:T(8,128)(2,1)S(1)}, u32[]{:S(2)}, u32[]{:S(2)}) collective-permute-start(bf16[144,1536]{1,0:T(8,128)(2,1)S(1)} %collective-permute-done.17.refs_3_), channel_id=1, source_target_pairs={{0,120},{8,0},{16,8},{24,16},{32,24},{40,32},{48,40},{56,48},{64,5... | collective-permute-start | bytes 1327112 | tf_op jit(solution)/shard_map/ppermute | solution.py:19
  122.5 4.6 %collective-permute-done.23.refs_4_ = bf16[128,1536]{1,0:T(8,128)(2,1)S(1)} collective-permute-done((bf16[128,1536]{1,0:T(8,128)(2,1)S(1)}, bf16[128,1536]{1,0:T(8,128)(2,1)S(1)}, u32[]{:S(2)}, u32[]{:S(2)}) %collective-permute-start.23) | collective-permute-done | bytes 393248 | tf_op jit(solution)/shard_map/ppermute | solution.py:19
  127.1 3.4 %collective-permute-start.27 = (bf16[128,1536]{1,0:T(8,128)(2,1)S(1)}, bf16[128,1536]{1,0:T(8,128)(2,1)S(1)}, u32[]{:S(2)}, u32[]{:S(2)}) collective-permute-start(bf16[128,1536]{1,0:T(8,128)(2,1)S(1)} %collective-permute-done.23.refs_4_), channel_id=1, source_target_pairs={{0,120},{8,0},{16,8},{24,16},{32,24},{40,32},{48,40},{56,48},{64,5... | collective-permute-start | bytes 1179656 | tf_op jit(solution)/shard_map/ppermute | solution.py:19
  130.5 0.0 collective-permute-start.26
  130.5 3.2 %attend.13 = (f32[256,768]{1,0:T(8,128)S(1)}, f32[256,768]{1,0:T(8,128)S(1)}, bf16[32,1536]{1,0:T(8,128)(2,1)S(1)}) custom-call(bf16[256,768]{1,0:T(8,128)(2,1)S(1)} %queries.1.refs_0_.q_ref, bf16[144,1536]{1,0:T(8,128)(2,1)S(1)} %collective-permute-done.16.refs_1_, ...), custom_call_target="tpu_custom_call", output_to_operand_aliasing={{0}: (5, {}), {1}: (6, {})} | custom-call | flops 1610612736 | bytes 786432 | tf_op jit(solution)/shard_map/attend/pallas_call | solution.py:305
  133.8 4.0 %collective-permute-done.20.refs_1_ = bf16[144,1536]{1,0:T(8,128)(2,1)S(1)} collective-permute-done((bf16[144,1536]{1,0:T(8,128)(2,1)S(1)}, bf16[144,1536]{1,0:T(8,128)(2,1)S(1)}, u32[]{:S(2)}, u32[]{:S(2)}) %collective-permute-start.20) | collective-permute-done | bytes 442400 | tf_op jit(solution)/shard_map/ppermute | solution.py:19
  137.7 2.7 %collective-permute-start.25 = (bf16[144,1536]{1,0:T(8,128)(2,1)S(1)}, bf16[144,1536]{1,0:T(8,128)(2,1)S(1)}, u32[]{:S(2)}, u32[]{:S(2)}) collective-permute-start(bf16[144,1536]{1,0:T(8,128)(2,1)S(1)} %collective-permute-done.21.refs_3_), channel_id=1, source_target_pairs={{0,120},{8,0},{16,8},{24,16},{32,24},{40,32},{48,40},{56,48},{64,5... | collective-permute-start | bytes 1327112 | tf_op jit(solution)/shard_map/ppermute | solution.py:19
  140.4 4.6 %collective-permute-done.27.refs_4_ = bf16[128,1536]{1,0:T(8,128)(2,1)S(1)} collective-permute-done((bf16[128,1536]{1,0:T(8,128)(2,1)S(1)}, bf16[128,1536]{1,0:T(8,128)(2,1)S(1)}, u32[]{:S(2)}, u32[]{:S(2)}) %collective-permute-start.27) | collective-permute-done | bytes 393248 | tf_op jit(solution)/shard_map/ppermute | solution.py:19
  145.0 3.4 %collective-permute-start.29 = (bf16[128,1536]{1,0:T(8,128)(2,1)S(1)}, bf16[128,1536]{1,0:T(8,128)(2,1)S(1)}, u32[]{:S(2)}, u32[]{:S(2)}) collective-permute-start(bf16[128,1536]{1,0:T(8,128)(2,1)S(1)} %collective-permute-done.27.refs_4_), channel_id=1, source_target_pairs={{0,120},{8,0},{16,8},{24,16},{32,24},{40,32},{48,40},{56,48},{64,5... | collective-permute-start | bytes 1179656 | tf_op jit(solution)/shard_map/ppermute | solution.py:19
  148.4 3.2 %attend.14 = (f32[256,768]{1,0:T(8,128)S(1)}, f32[256,768]{1,0:T(8,128)S(1)}, bf16[32,1536]{1,0:T(8,128)(2,1)S(1)}) custom-call(bf16[256,768]{1,0:T(8,128)(2,1)S(1)} %queries.1.refs_0_.q_ref, bf16[144,1536]{1,0:T(8,128)(2,1)S(1)} %collective-permute-done.20.refs_1_, ...), custom_call_target="tpu_custom_call", output_to_operand_aliasing={{0}: (5, {}), {1}: (6, {})} | custom-call | flops 1610612736 | bytes 786432 | tf_op jit(solution)/shard_map/attend/pallas_call | solution.py:305
  151.7 4.0 %collective-permute-done.24.refs_1_ = bf16[144,1536]{1,0:T(8,128)(2,1)S(1)} collective-permute-done((bf16[144,1536]{1,0:T(8,128)(2,1)S(1)}, bf16[144,1536]{1,0:T(8,128)(2,1)S(1)}, u32[]{:S(2)}, u32[]{:S(2)}) %collective-permute-start.24) | collective-permute-done | bytes 442400 | tf_op jit(solution)/shard_map/ppermute | solution.py:19
  155.6 7.3 %collective-permute-done.29.refs_4_ = bf16[128,1536]{1,0:T(8,128)(2,1)S(1)} collective-permute-done((bf16[128,1536]{1,0:T(8,128)(2,1)S(1)}, bf16[128,1536]{1,0:T(8,128)(2,1)S(1)}, u32[]{:S(2)}, u32[]{:S(2)}) %collective-permute-start.29) | collective-permute-done | bytes 393248 | tf_op jit(solution)/shard_map/ppermute | solution.py:19
  162.9 3.4 %collective-permute-start.30 = (bf16[128,1536]{1,0:T(8,128)(2,1)S(1)}, bf16[128,1536]{1,0:T(8,128)(2,1)S(1)}, u32[]{:S(2)}, u32[]{:S(2)}) collective-permute-start(bf16[128,1536]{1,0:T(8,128)(2,1)S(1)} %collective-permute-done.29.refs_4_), channel_id=1, source_target_pairs={{0,120},{8,0},{16,8},{24,16},{32,24},{40,32},{48,40},{56,48},{64,5... | collective-permute-start | bytes 1179656 | tf_op jit(solution)/shard_map/ppermute | solution.py:19
  167.0 3.2 %attend.15 = (f32[256,768]{1,0:T(8,128)S(1)}, f32[256,768]{1,0:T(8,128)S(1)}, bf16[32,1536]{1,0:T(8,128)(2,1)S(1)}) custom-call(bf16[256,768]{1,0:T(8,128)(2,1)S(1)} %queries.1.refs_0_.q_ref, bf16[144,1536]{1,0:T(8,128)(2,1)S(1)} %collective-permute-done.24.refs_1_, ...), custom_call_target="tpu_custom_call", output_to_operand_aliasing={{0}: (5, {}), {1}: (6, {})} | custom-call | flops 1610612736 | bytes 786432 | tf_op jit(solution)/shard_map/attend/pallas_call | solution.py:305
  170.2 3.4 %collective-permute-done.30.second_ref = bf16[128,1536]{1,0:T(8,128)(2,1)S(1)} collective-permute-done((bf16[128,1536]{1,0:T(8,128)(2,1)S(1)}, bf16[128,1536]{1,0:T(8,128)(2,1)S(1)}, u32[]{:S(2)}, u32[]{:S(2)}) %collective-permute-start.30) | collective-permute-done | bytes 393248 | tf_op jit(solution)/shard_map/ppermute | solution.py:19
  173.7 2.1 %attend_last.1.own_ref = bf16[256,768]{1,0:T(8,128)(2,1)S(1)} custom-call(s32[1]{0:T(128)} %bitcast.z_ref, s32[1]{0:T(128)S(6)} %copy.40.length_ref, bf16[256,768]{1,0:T(8,128)(2,1)S(1)} %queries.1.refs_0_.q_ref, bf16[144,1536]{1,0:T(8,128)(2,1)S(1)} %collective-permute-done.28.first_ref, bf16[128,1536]{1,0:T(8,128)(2,1)S(1)} %collective-permute-done.30.second_ref, ...), custom_call_target="tpu_custom_call" | custom-call | flops 1610612736 | bytes 1572864 | tf_op jit(solution)/shard_map/attend_last/pallas_call | solution.py:355
  175.8 2.1 %collective-permute-start.32 = (bf16[256,768]{1,0:T(8,128)(2,1)S(1)}, bf16[256,768]{1,0:T(8,128)(2,1)S(1)}, u32[]{:S(2)}, u32[]{:S(2)}) collective-permute-start(bf16[256,768]{1,0:T(8,128)(2,1)S(1)} %attend_last.1.own_ref), channel_id=1, source_target_pairs={{0,1},{1,0},{2,3},{3,2},{4,5},{5,4},{6,7},{7,6},{8,9},{9,8},{10,11... | collective-permute-start | bytes 1179656 | tf_op jit(solution)/shard_map/ppermute | solution.py:19
  178.6 0.7 collective-permute-done.32.other_ref
  179.3 2.3 %out.1 = (f32[64,1536]{1,0:T(8,128)S(1)}, bf16[64,1536]{1,0:T(8,128)(2,1)S(1)}, bf16[64,1536]{1,0:T(8,128)(2,1)S(1)}, bf16[64,1536]{1,0:T(8,128)(2,1)S(1)}) custom-call(s32[1]{0:T(128)} %bitcast.1.x_ref, s32[1]{0:T(128)} %bitcast.2.c_ref, f32[1]{0:T(128)S(6)} %copy.41.strength_ref, bf16[256,768]{1,0:T(8,128)(2,1)S(1)} %attend_last.1.own_ref, ...), custom_call_target="tpu_custom_call" | custom-call | flops 1207959552 | bytes 2359296 | tf_op jit(solution)/shard_map/out/pallas_call | solution.py:403
  181.6 3.1 %collective-permute-start.33 = (bf16[64,1536]{1,0:T(8,128)(2,1)S(1)}, bf16[64,1536]{1,0:T(8,128)(2,1)S(1)}, u32[]{:S(2)}, u32[]{:S(2)}) collective-permute-start(bf16[64,1536]{1,0:T(8,128)(2,1)S(1)} %get-tuple-element.134), channel_id=1, source_target_pairs={{0,4},{2,6},{4,0},{6,2},{1,5},{3,7},{5,1},{7,3},{8,12},{10,14},{12... | collective-permute-start | bytes 589832 | tf_op jit(solution)/shard_map/ppermute | solution.py:19
  184.8 0.4 collective-permute-start.34
  185.2 2.2 %collective-permute-start.35 = (bf16[64,1536]{1,0:T(8,128)(2,1)S(1)}, bf16[64,1536]{1,0:T(8,128)(2,1)S(1)}, u32[]{:S(2)}, u32[]{:S(2)}) collective-permute-start(bf16[64,1536]{1,0:T(8,128)(2,1)S(1)} %get-tuple-element.136), channel_id=1, source_target_pairs={{0,6},{2,0},{4,2},{6,4},{1,7},{3,1},{5,3},{7,5},{8,14},{10,8},{12,... | collective-permute-start | bytes 589832 | tf_op jit(solution)/shard_map/ppermute | solution.py:19
  187.4 2.0 %collective-permute-done.33 = bf16[64,1536]{1,0:T(8,128)(2,1)S(1)} collective-permute-done((bf16[64,1536]{1,0:T(8,128)(2,1)S(1)}, bf16[64,1536]{1,0:T(8,128)(2,1)S(1)}, u32[]{:S(2)}, u32[]{:S(2)}) %collective-permute-start.33) | collective-permute-done | bytes 196640 | tf_op jit(solution)/shard_map/ppermute | solution.py:19
  189.5 4.8 %collective-permute-done.34 = bf16[64,1536]{1,0:T(8,128)(2,1)S(1)} collective-permute-done((bf16[64,1536]{1,0:T(8,128)(2,1)S(1)}, bf16[64,1536]{1,0:T(8,128)(2,1)S(1)}, u32[]{:S(2)}, u32[]{:S(2)}) %collective-permute-start.34) | collective-permute-done | bytes 196640 | tf_op jit(solution)/shard_map/ppermute | solution.py:19
  194.3 0.8 add_convert_fusion
  (41 shorter events, 0.1 us)
Async XLA Ops:
  0.0 3.5 %copy-start = (bf16[3,1536,768]{2,1,0:T(8,128)(2,1)S(1)}, bf16[3,1536,768]{2,1,0:T(8,128)(2,1)}, u32[]{:S(2)}) copy-start(bf16[3,1536,768]{2,1,0:T(8,128)(2,1)} %w_ref.4) | copy-start | bytes 21233668
  3.5 24.6 %copy-start.4 = (s32[3,256]{1,0:T(4,128)S(1)}, s32[3,256]{1,0:T(4,128)}, u32[]{:S(2)}) copy-start(s32[3,256]{1,0:T(4,128)} %pos_ref.1) | copy-start | bytes 9220
  3.5 24.6 %copy-start.6 = (bf16[256,512]{1,0:T(8,128)(2,1)S(1)}, bf16[256,512]{1,0:T(8,128)(2,1)}, u32[]{:S(2)}) copy-start(bf16[256,512]{1,0:T(8,128)(2,1)} %constant.17.clone.turn_ref) | copy-start | bytes 786436
  3.5 24.6 %copy-start.7 = (f32[4,128]{1,0:T(4,128)S(1)}, f32[4,128]{1,0:T(4,128)}, u32[]{:S(2)}) copy-start(f32[4,128]{1,0:T(4,128)} %constant.18.clone.sign_ref) | copy-start | bytes 6148
  7.6 22.5 %copy-start.3 = (bf16[1,2,16,768]{3,2,1,0:T(8,128)(2,1)S(1)}, bf16[1,2,16,768]{3,2,1,0:T(8,128)(2,1)}, u32[]{:S(2)}) copy-start(bf16[1,2,16,768]{3,2,1,0:T(8,128)(2,1)} %text_ref.1) | copy-start | bytes 147460
  7.6 22.5 %copy-start.5 = (f32[2,128]{1,0:T(2,128)S(1)}, f32[2,128]{1,0:T(2,128)}, u32[]{:S(2)}) copy-start(f32[2,128]{1,0:T(2,128)} %gain_ref.3) | copy-start | bytes 3076
  7.6 22.4 %collective-permute-start = (bf16[256,1536]{1,0:T(8,128)(2,1)S(1)}, bf16[256,1536]{1,0:T(8,128)(2,1)S(1)}, u32[]{:S(2)}, u32[]{:S(2)}) collective-permute-start(bf16[256,1536]{1,0:T(8,128)(2,1)S(1)} %get-tuple-element.76), channel_id=1, source_target_pairs={{0,1},{1,0},{2,3},{3,2},{4,5},{5,4},{6,7},{7,6},{8,9},{9,8},{10,11... | collective-permute-start | bytes 2359304 | tf_op jit(solution)/shard_map/ppermute | solution.py:19
  34.2 6.3 %collective-permute-start.1 = (bf16[256,768]{1,0:T(8,128)(2,1)S(1)}, bf16[256,768]{1,0:T(8,128)(2,1)S(1)}, u32[]{:S(2)}, u32[]{:S(2)}) collective-permute-start(bf16[256,768]{1,0:T(8,128)(2,1)S(1)} %get-tuple-element.79), channel_id=1, source_target_pairs={{0,1},{1,0},{2,3},{3,2},{4,5},{5,4},{6,7},{7,6},{8,9},{9,8},{10,11... | collective-permute-start | bytes 1179656 | tf_op jit(solution)/shard_map/ppermute | solution.py:19
  34.7 13.5 %collective-permute-start.2 = (bf16[144,1536]{1,0:T(8,128)(2,1)S(1)}, bf16[144,1536]{1,0:T(8,128)(2,1)S(1)}, u32[]{:S(2)}, u32[]{:S(2)}) collective-permute-start(bf16[144,1536]{1,0:T(8,128)(2,1)S(1)} %get-tuple-element.80.refs_1_), channel_id=1, source_target_pairs={{0,8},{8,16},{16,24},{24,32},{32,40},{40,48},{48,56},{56,64},{64,7... | collective-permute-start | bytes 1327112 | tf_op jit(solution)/shard_map/ppermute | solution.py:19
  34.7 13.5 %collective-permute-start.3 = (bf16[144,1536]{1,0:T(8,128)(2,1)S(1)}, bf16[144,1536]{1,0:T(8,128)(2,1)S(1)}, u32[]{:S(2)}, u32[]{:S(2)}) collective-permute-start(bf16[144,1536]{1,0:T(8,128)(2,1)S(1)} %get-tuple-element.80.refs_1_), channel_id=1, source_target_pairs={{0,120},{8,0},{16,8},{24,16},{32,24},{40,32},{48,40},{56,48},{64,5... | collective-permute-start | bytes 1327112 | tf_op jit(solution)/shard_map/ppermute | solution.py:19
  37.8 18.8 %collective-permute-start.6 = (bf16[128,1536]{1,0:T(8,128)(2,1)S(1)}, bf16[128,1536]{1,0:T(8,128)(2,1)S(1)}, u32[]{:S(2)}, u32[]{:S(2)}) collective-permute-start(bf16[128,1536]{1,0:T(8,128)(2,1)S(1)} %get-tuple-element.77.refs_0_.refs_2_), channel_id=1, source_target_pairs={{0,8},{8,16},{16,24},{24,32},{32,40},{40,48},{48,56},{56,64},{64,7... | collective-permute-start | bytes 1179656 | tf_op jit(solution)/shard_map/ppermute | solution.py:19
  37.8 18.8 %collective-permute-start.7 = (bf16[128,1536]{1,0:T(8,128)(2,1)S(1)}, bf16[128,1536]{1,0:T(8,128)(2,1)S(1)}, u32[]{:S(2)}, u32[]{:S(2)}) collective-permute-start(bf16[128,1536]{1,0:T(8,128)(2,1)S(1)} %get-tuple-element.77.refs_0_.refs_2_), channel_id=1, source_target_pairs={{0,120},{8,0},{16,8},{24,16},{32,24},{40,32},{48,40},{56,48},{64,5... | collective-permute-start | bytes 1179656 | tf_op jit(solution)/shard_map/ppermute | solution.py:19
  48.2 17.9 %collective-permute-start.4 = (bf16[144,1536]{1,0:T(8,128)(2,1)S(1)}, bf16[144,1536]{1,0:T(8,128)(2,1)S(1)}, u32[]{:S(2)}, u32[]{:S(2)}) collective-permute-start(bf16[144,1536]{1,0:T(8,128)(2,1)S(1)} %collective-permute-done.2.refs_1_), channel_id=1, source_target_pairs={{0,8},{8,16},{16,24},{24,32},{32,40},{40,48},{48,56},{56,64},{64,7... | collective-permute-start | bytes 1327112 | tf_op jit(solution)/shard_map/ppermute | solution.py:19
  48.2 17.9 %collective-permute-start.5 = (bf16[144,1536]{1,0:T(8,128)(2,1)S(1)}, bf16[144,1536]{1,0:T(8,128)(2,1)S(1)}, u32[]{:S(2)}, u32[]{:S(2)}) collective-permute-start(bf16[144,1536]{1,0:T(8,128)(2,1)S(1)} %collective-permute-done.3.refs_3_), channel_id=1, source_target_pairs={{0,120},{8,0},{16,8},{24,16},{32,24},{40,32},{48,40},{56,48},{64,5... | collective-permute-start | bytes 1327112 | tf_op jit(solution)/shard_map/ppermute | solution.py:19
  56.6 17.9 %collective-permute-start.10 = (bf16[128,1536]{1,0:T(8,128)(2,1)S(1)}, bf16[128,1536]{1,0:T(8,128)(2,1)S(1)}, u32[]{:S(2)}, u32[]{:S(2)}) collective-permute-start(bf16[128,1536]{1,0:T(8,128)(2,1)S(1)} %collective-permute-done.6.refs_2_), channel_id=1, source_target_pairs={{0,8},{8,16},{16,24},{24,32},{32,40},{40,48},{48,56},{56,64},{64,7... | collective-permute-start | bytes 1179656 | tf_op jit(solution)/shard_map/ppermute | solution.py:19
  56.6 17.9 %collective-permute-start.11 = (bf16[128,1536]{1,0:T(8,128)(2,1)S(1)}, bf16[128,1536]{1,0:T(8,128)(2,1)S(1)}, u32[]{:S(2)}, u32[]{:S(2)}) collective-permute-start(bf16[128,1536]{1,0:T(8,128)(2,1)S(1)} %collective-permute-done.7.refs_4_), channel_id=1, source_target_pairs={{0,120},{8,0},{16,8},{24,16},{32,24},{40,32},{48,40},{56,48},{64,5... | collective-permute-start | bytes 1179656 | tf_op jit(solution)/shard_map/ppermute | solution.py:19
  66.1 17.9 %collective-permute-start.8 = (bf16[144,1536]{1,0:T(8,128)(2,1)S(1)}, bf16[144,1536]{1,0:T(8,128)(2,1)S(1)}, u32[]{:S(2)}, u32[]{:S(2)}) collective-permute-start(bf16[144,1536]{1,0:T(8,128)(2,1)S(1)} %collective-permute-done.4.refs_1_), channel_id=1, source_target_pairs={{0,8},{8,16},{16,24},{24,32},{32,40},{40,48},{48,56},{56,64},{64,7... | collective-permute-start | bytes 1327112 | tf_op jit(solution)/shard_map/ppermute | solution.py:19
  66.1 17.9 %collective-permute-start.9 = (bf16[144,1536]{1,0:T(8,128)(2,1)S(1)}, bf16[144,1536]{1,0:T(8,128)(2,1)S(1)}, u32[]{:S(2)}, u32[]{:S(2)}) collective-permute-start(bf16[144,1536]{1,0:T(8,128)(2,1)S(1)} %collective-permute-done.5.refs_3_), channel_id=1, source_target_pairs={{0,120},{8,0},{16,8},{24,16},{32,24},{40,32},{48,40},{56,48},{64,5... | collective-permute-start | bytes 1327112 | tf_op jit(solution)/shard_map/ppermute | solution.py:19
  74.5 20.2 %collective-permute-start.14 = (bf16[128,1536]{1,0:T(8,128)(2,1)S(1)}, bf16[128,1536]{1,0:T(8,128)(2,1)S(1)}, u32[]{:S(2)}, u32[]{:S(2)}) collective-permute-start(bf16[128,1536]{1,0:T(8,128)(2,1)S(1)} %collective-permute-done.10.refs_2_), channel_id=1, source_target_pairs={{0,8},{8,16},{16,24},{24,32},{32,40},{40,48},{48,56},{56,64},{64,7... | collective-permute-start | bytes 1179656 | tf_op jit(solution)/shard_map/ppermute | solution.py:19
  74.5 16.8 %collective-permute-start.15 = (bf16[128,1536]{1,0:T(8,128)(2,1)S(1)}, bf16[128,1536]{1,0:T(8,128)(2,1)S(1)}, u32[]{:S(2)}, u32[]{:S(2)}) collective-permute-start(bf16[128,1536]{1,0:T(8,128)(2,1)S(1)} %collective-permute-done.11.refs_4_), channel_id=1, source_target_pairs={{0,120},{8,0},{16,8},{24,16},{32,24},{40,32},{48,40},{56,48},{64,5... | collective-permute-start | bytes 1179656 | tf_op jit(solution)/shard_map/ppermute | solution.py:19
  84.0 17.9 %collective-permute-start.12 = (bf16[144,1536]{1,0:T(8,128)(2,1)S(1)}, bf16[144,1536]{1,0:T(8,128)(2,1)S(1)}, u32[]{:S(2)}, u32[]{:S(2)}) collective-permute-start(bf16[144,1536]{1,0:T(8,128)(2,1)S(1)} %collective-permute-done.8.refs_1_), channel_id=1, source_target_pairs={{0,8},{8,16},{16,24},{24,32},{32,40},{40,48},{48,56},{56,64},{64,7... | collective-permute-start | bytes 1327112 | tf_op jit(solution)/shard_map/ppermute | solution.py:19
  84.0 17.9 %collective-permute-start.13 = (bf16[144,1536]{1,0:T(8,128)(2,1)S(1)}, bf16[144,1536]{1,0:T(8,128)(2,1)S(1)}, u32[]{:S(2)}, u32[]{:S(2)}) collective-permute-start(bf16[144,1536]{1,0:T(8,128)(2,1)S(1)} %collective-permute-done.9.refs_3_), channel_id=1, source_target_pairs={{0,120},{8,0},{16,8},{24,16},{32,24},{40,32},{48,40},{56,48},{64,5... | collective-permute-start | bytes 1327112 | tf_op jit(solution)/shard_map/ppermute | solution.py:19
  91.3 17.9 %collective-permute-start.19 = (bf16[128,1536]{1,0:T(8,128)(2,1)S(1)}, bf16[128,1536]{1,0:T(8,128)(2,1)S(1)}, u32[]{:S(2)}, u32[]{:S(2)}) collective-permute-start(bf16[128,1536]{1,0:T(8,128)(2,1)S(1)} %collective-permute-done.15.refs_4_), channel_id=1, source_target_pairs={{0,120},{8,0},{16,8},{24,16},{32,24},{40,32},{48,40},{56,48},{64,5... | collective-permute-start | bytes 1179656 | tf_op jit(solution)/shard_map/ppermute | solution.py:19
  94.7 17.9 %collective-permute-start.18 = (bf16[128,1536]{1,0:T(8,128)(2,1)S(1)}, bf16[128,1536]{1,0:T(8,128)(2,1)S(1)}, u32[]{:S(2)}, u32[]{:S(2)}) collective-permute-start(bf16[128,1536]{1,0:T(8,128)(2,1)S(1)} %collective-permute-done.14.refs_2_), channel_id=1, source_target_pairs={{0,8},{8,16},{16,24},{24,32},{32,40},{40,48},{48,56},{56,64},{64,7... | collective-permute-start | bytes 1179656 | tf_op jit(solution)/shard_map/ppermute | solution.py:19
  101.9 17.9 %collective-permute-start.16 = (bf16[144,1536]{1,0:T(8,128)(2,1)S(1)}, bf16[144,1536]{1,0:T(8,128)(2,1)S(1)}, u32[]{:S(2)}, u32[]{:S(2)}) collective-permute-start(bf16[144,1536]{1,0:T(8,128)(2,1)S(1)} %collective-permute-done.12.refs_1_), channel_id=1, source_target_pairs={{0,8},{8,16},{16,24},{24,32},{32,40},{40,48},{48,56},{56,64},{64,7... | collective-permute-start | bytes 1327112 | tf_op jit(solution)/shard_map/ppermute | solution.py:19
  101.9 17.9 %collective-permute-start.17 = (bf16[144,1536]{1,0:T(8,128)(2,1)S(1)}, bf16[144,1536]{1,0:T(8,128)(2,1)S(1)}, u32[]{:S(2)}, u32[]{:S(2)}) collective-permute-start(bf16[144,1536]{1,0:T(8,128)(2,1)S(1)} %collective-permute-done.13.refs_3_), channel_id=1, source_target_pairs={{0,120},{8,0},{16,8},{24,16},{32,24},{40,32},{48,40},{56,48},{64,5... | collective-permute-start | bytes 1327112 | tf_op jit(solution)/shard_map/ppermute | solution.py:19
  109.2 17.9 %collective-permute-start.23 = (bf16[128,1536]{1,0:T(8,128)(2,1)S(1)}, bf16[128,1536]{1,0:T(8,128)(2,1)S(1)}, u32[]{:S(2)}, u32[]{:S(2)}) collective-permute-start(bf16[128,1536]{1,0:T(8,128)(2,1)S(1)} %collective-permute-done.19.refs_4_), channel_id=1, source_target_pairs={{0,120},{8,0},{16,8},{24,16},{32,24},{40,32},{48,40},{56,48},{64,5... | collective-permute-start | bytes 1179656 | tf_op jit(solution)/shard_map/ppermute | solution.py:19
  112.6 17.9 %collective-permute-start.22 = (bf16[128,1536]{1,0:T(8,128)(2,1)S(1)}, bf16[128,1536]{1,0:T(8,128)(2,1)S(1)}, u32[]{:S(2)}, u32[]{:S(2)}) collective-permute-start(bf16[128,1536]{1,0:T(8,128)(2,1)S(1)} %collective-permute-done.18.refs_2_), channel_id=1, source_target_pairs={{0,8},{8,16},{16,24},{24,32},{32,40},{40,48},{48,56},{56,64},{64,7... | collective-permute-start | bytes 1179656 | tf_op jit(solution)/shard_map/ppermute | solution.py:19
  119.8 17.9 %collective-permute-start.20 = (bf16[144,1536]{1,0:T(8,128)(2,1)S(1)}, bf16[144,1536]{1,0:T(8,128)(2,1)S(1)}, u32[]{:S(2)}, u32[]{:S(2)}) collective-permute-start(bf16[144,1536]{1,0:T(8,128)(2,1)S(1)} %collective-permute-done.16.refs_1_), channel_id=1, source_target_pairs={{0,8},{8,16},{16,24},{24,32},{32,40},{40,48},{48,56},{56,64},{64,7... | collective-permute-start | bytes 1327112 | tf_op jit(solution)/shard_map/ppermute | solution.py:19
  119.8 17.9 %collective-permute-start.21 = (bf16[144,1536]{1,0:T(8,128)(2,1)S(1)}, bf16[144,1536]{1,0:T(8,128)(2,1)S(1)}, u32[]{:S(2)}, u32[]{:S(2)}) collective-permute-start(bf16[144,1536]{1,0:T(8,128)(2,1)S(1)} %collective-permute-done.17.refs_3_), channel_id=1, source_target_pairs={{0,120},{8,0},{16,8},{24,16},{32,24},{40,32},{48,40},{56,48},{64,5... | collective-permute-start | bytes 1327112 | tf_op jit(solution)/shard_map/ppermute | solution.py:19
  127.1 17.9 %collective-permute-start.27 = (bf16[128,1536]{1,0:T(8,128)(2,1)S(1)}, bf16[128,1536]{1,0:T(8,128)(2,1)S(1)}, u32[]{:S(2)}, u32[]{:S(2)}) collective-permute-start(bf16[128,1536]{1,0:T(8,128)(2,1)S(1)} %collective-permute-done.23.refs_4_), channel_id=1, source_target_pairs={{0,120},{8,0},{16,8},{24,16},{32,24},{40,32},{48,40},{56,48},{64,5... | collective-permute-start | bytes 1179656 | tf_op jit(solution)/shard_map/ppermute | solution.py:19
  130.5 17.9 %collective-permute-start.26 = (bf16[128,1536]{1,0:T(8,128)(2,1)S(1)}, bf16[128,1536]{1,0:T(8,128)(2,1)S(1)}, u32[]{:S(2)}, u32[]{:S(2)}) collective-permute-start(bf16[128,1536]{1,0:T(8,128)(2,1)S(1)} %collective-permute-done.22.refs_2_), channel_id=1, source_target_pairs={{0,8},{8,16},{16,24},{24,32},{32,40},{40,48},{48,56},{56,64},{64,7... | collective-permute-start | bytes 1179656 | tf_op jit(solution)/shard_map/ppermute | solution.py:19
  137.7 17.9 %collective-permute-start.24 = (bf16[144,1536]{1,0:T(8,128)(2,1)S(1)}, bf16[144,1536]{1,0:T(8,128)(2,1)S(1)}, u32[]{:S(2)}, u32[]{:S(2)}) collective-permute-start(bf16[144,1536]{1,0:T(8,128)(2,1)S(1)} %collective-permute-done.20.refs_1_), channel_id=1, source_target_pairs={{0,8},{8,16},{16,24},{24,32},{32,40},{40,48},{48,56},{56,64},{64,7... | collective-permute-start | bytes 1327112 | tf_op jit(solution)/shard_map/ppermute | solution.py:19
  137.7 17.9 %collective-permute-start.25 = (bf16[144,1536]{1,0:T(8,128)(2,1)S(1)}, bf16[144,1536]{1,0:T(8,128)(2,1)S(1)}, u32[]{:S(2)}, u32[]{:S(2)}) collective-permute-start(bf16[144,1536]{1,0:T(8,128)(2,1)S(1)} %collective-permute-done.21.refs_3_), channel_id=1, source_target_pairs={{0,120},{8,0},{16,8},{24,16},{32,24},{40,32},{48,40},{56,48},{64,5... | collective-permute-start | bytes 1327112 | tf_op jit(solution)/shard_map/ppermute | solution.py:19
  145.0 17.9 %collective-permute-start.29 = (bf16[128,1536]{1,0:T(8,128)(2,1)S(1)}, bf16[128,1536]{1,0:T(8,128)(2,1)S(1)}, u32[]{:S(2)}, u32[]{:S(2)}) collective-permute-start(bf16[128,1536]{1,0:T(8,128)(2,1)S(1)} %collective-permute-done.27.refs_4_), channel_id=1, source_target_pairs={{0,120},{8,0},{16,8},{24,16},{32,24},{40,32},{48,40},{56,48},{64,5... | collective-permute-start | bytes 1179656 | tf_op jit(solution)/shard_map/ppermute | solution.py:19
  148.4 18.6 %collective-permute-start.31 = (bf16[128,1536]{1,0:T(8,128)(2,1)S(1)}, bf16[128,1536]{1,0:T(8,128)(2,1)S(1)}, u32[]{:S(2)}, u32[]{:S(2)}) collective-permute-start(bf16[128,1536]{1,0:T(8,128)(2,1)S(1)} %collective-permute-done.26.refs_2_), channel_id=1, source_target_pairs={{0,8},{8,16},{16,24},{24,32},{32,40},{40,48},{48,56},{56,64},{64,7... | collective-permute-start | bytes 1179656 | tf_op jit(solution)/shard_map/ppermute | solution.py:19
  155.6 18.1 %collective-permute-start.28 = (bf16[144,1536]{1,0:T(8,128)(2,1)S(1)}, bf16[144,1536]{1,0:T(8,128)(2,1)S(1)}, u32[]{:S(2)}, u32[]{:S(2)}) collective-permute-start(bf16[144,1536]{1,0:T(8,128)(2,1)S(1)} %collective-permute-done.24.refs_1_), channel_id=1, source_target_pairs={{0,8},{8,16},{16,24},{24,32},{32,40},{40,48},{48,56},{56,64},{64,7... | collective-permute-start | bytes 1327112 | tf_op jit(solution)/shard_map/ppermute | solution.py:19
  162.9 10.8 %collective-permute-start.30 = (bf16[128,1536]{1,0:T(8,128)(2,1)S(1)}, bf16[128,1536]{1,0:T(8,128)(2,1)S(1)}, u32[]{:S(2)}, u32[]{:S(2)}) collective-permute-start(bf16[128,1536]{1,0:T(8,128)(2,1)S(1)} %collective-permute-done.29.refs_4_), channel_id=1, source_target_pairs={{0,120},{8,0},{16,8},{24,16},{32,24},{40,32},{48,40},{56,48},{64,5... | collective-permute-start | bytes 1179656 | tf_op jit(solution)/shard_map/ppermute | solution.py:19
  173.7 5.6 %copy-start.1 = (bf16[768,1536]{1,0:T(8,128)(2,1)S(1)}, bf16[768,1536]{1,0:T(8,128)(2,1)}, u32[]{:S(2)}) copy-start(bf16[768,1536]{1,0:T(8,128)(2,1)} %w_ref.5) | copy-start | bytes 7077892
  173.7 5.6 %copy-start.2 = (f32[3,2,3072]{2,1,0:T(2,128)S(1)}, f32[3,2,3072]{2,1,0:T(2,128)}, u32[]{:S(2)}) copy-start(f32[3,2,3072]{2,1,0:T(2,128)} %mod_ref.3) | copy-start | bytes 221188
  175.8 3.5 %collective-permute-start.32 = (bf16[256,768]{1,0:T(8,128)(2,1)S(1)}, bf16[256,768]{1,0:T(8,128)(2,1)S(1)}, u32[]{:S(2)}, u32[]{:S(2)}) collective-permute-start(bf16[256,768]{1,0:T(8,128)(2,1)S(1)} %attend_last.1.own_ref), channel_id=1, source_target_pairs={{0,1},{1,0},{2,3},{3,2},{4,5},{5,4},{6,7},{7,6},{8,9},{9,8},{10,11... | collective-permute-start | bytes 1179656 | tf_op jit(solution)/shard_map/ppermute | solution.py:19
  181.6 7.8 %collective-permute-start.33 = (bf16[64,1536]{1,0:T(8,128)(2,1)S(1)}, bf16[64,1536]{1,0:T(8,128)(2,1)S(1)}, u32[]{:S(2)}, u32[]{:S(2)}) collective-permute-start(bf16[64,1536]{1,0:T(8,128)(2,1)S(1)} %get-tuple-element.134), channel_id=1, source_target_pairs={{0,4},{2,6},{4,0},{6,2},{1,5},{3,7},{5,1},{7,3},{8,12},{10,14},{12... | collective-permute-start | bytes 589832 | tf_op jit(solution)/shard_map/ppermute | solution.py:19
  184.8 9.5 %collective-permute-start.34 = (bf16[64,1536]{1,0:T(8,128)(2,1)S(1)}, bf16[64,1536]{1,0:T(8,128)(2,1)S(1)}, u32[]{:S(2)}, u32[]{:S(2)}) collective-permute-start(bf16[64,1536]{1,0:T(8,128)(2,1)S(1)} %get-tuple-element.135), channel_id=1, source_target_pairs={{0,2},{2,4},{4,6},{6,0},{1,3},{3,5},{5,7},{7,1},{8,10},{10,12},{12... | collective-permute-start | bytes 589832 | tf_op jit(solution)/shard_map/ppermute | solution.py:19
  185.2 9.1 %collective-permute-start.35 = (bf16[64,1536]{1,0:T(8,128)(2,1)S(1)}, bf16[64,1536]{1,0:T(8,128)(2,1)S(1)}, u32[]{:S(2)}, u32[]{:S(2)}) collective-permute-start(bf16[64,1536]{1,0:T(8,128)(2,1)S(1)} %get-tuple-element.136), channel_id=1, source_target_pairs={{0,6},{2,0},{4,2},{6,4},{1,7},{3,1},{5,3},{7,5},{8,14},{10,8},{12,... | collective-permute-start | bytes 589832 | tf_op jit(solution)/shard_map/ppermute | solution.py:19
